TPU v7x, 128 devices: a whole 4x4x4 slice. The times are simulated.
128 devices in a mesh: seq: 16 (over y, z_lo, core), tensor: 8 (over z_hi, x).
Axes of the slice: x: 4, y: 4, z: 4 (z_hi: 2, z_lo: 2; z = z_hi * 2 + z_lo), core: 2. Of those that a mesh axis runs over, the one named last changes fastest.
Arguments:
- tokens: bfloat16 [8192, 8192], P('seq', 'tensor'), may hold values from -6 to 6
- positions: int32 [8192], P('seq'), may hold values from 0 to 8191, each once
- norm_gain: float32 [8192], replicated, may hold values from 0.1 to 1.9
- w_query: bfloat16 [8192, 4096], P('seq', 'tensor'), may hold values from -0.0625 to 0.0625
- w_key: bfloat16 [8192, 1024], P('seq', 'tensor'), may hold values from -0.0625 to 0.0625
- w_value: bfloat16 [8192, 1024], P('seq', 'tensor'), may hold values from -0.0625 to 0.0625
- b_query: float32 [4096], P('tensor'), may hold values from -40 to 40
- b_key: float32 [1024], P('tensor'), may hold values from -40 to 40
- b_value: float32 [1024], P('tensor'), may hold values from -6 to 6
- w_out: bfloat16 [4096, 8192], P('tensor', 'seq'), may hold values from -0.09375 to 0.09375
Outputs:
- mixed: bfloat16 [8192, 8192], P('seq', 'tensor')
- context: bfloat16 [8192, 4096], P('seq', 'tensor')
Inputs may be any that keep to these rules, and one draw needn't show every extreme that they name: positions holds every position 0 to 8191 once.
All inputs are finite; a program needn't handle non-finite values.
Results may differ from a plain program's by a relative error of at most 0.025.
Values may be sent and summed in bfloat16 or wider, within the bound.
No kernel may reach another device: no remote copies, remote signals or barrier semaphores. Data moves between devices by JAX's collectives and lax.ppermute only.
A program may use at most 128 MiB of HBM per device.

v0:
```python
import math

import jax
import jax.numpy as jnp
from jax import lax
from jax.experimental import pallas as pl
from jax.experimental.pallas import tpu as pltpu
from jax.sharding import Mesh, PartitionSpec as P


HD = 128
NORM_EPS = 1e-06
ROPE_BASE = 1000000.0
NEG_FILL = -1e30
SEQ = ("y", "zl", "core")
TENSOR = ("zh", "x")
ROWS = 512
FEAT = 1024
MODEL = 8192
SOURCES = 16
GROUPS = 8
HEADS = 4
POS_ROWS = 16
KSTEP = 64
NSTEPS = ROWS // KSTEP
KEYS = SOURCES * KSTEP
BLOCK = 128
BLOCKS = ROWS // BLOCK
CALLS = ((0, 2), (2, 2))
PER_STEP = 2
QSCALE = HD**-0.5 * math.log2(math.e)


NEXT = [(i, (i + 1) % 4) for i in range(4)]
PREV = [(i, (i - 1) % 4) for i in range(4)]
ACROSS = [(i, (i + 2) % 4) for i in range(4)]
SWAP = [(0, 1), (1, 0)]


def fetch_all(pieces, slots, buffer, sems, step):
    def fetch(i):
        slot, start, size = slots[i]
        return pltpu.make_async_copy(pieces[i], buffer.at[slot, pl.ds(start, size)], sems.at[i])

    @pl.when(step == 0)
    def _():
        for i in range(len(slots)):
            fetch(i).start()

    for k in range(GROUPS // PER_STEP):

        @pl.when(step == k)
        def _(k=k):
            for i, (slot, _, _) in enumerate(slots):
                if slot // PER_STEP == k:
                    fetch(i).wait()


def whole(*shape):
    return pl.BlockSpec(shape, lambda k, ids: (0,) * len(shape))


def project_body(slots, queries, ids, *refs):
    pieces = refs[: len(slots)]
    refs = refs[len(slots) :]
    w_refs = refs[:PER_STEP]
    inverse_ref, bias_ref, cos_ref, sin_ref, out_ref, tbuf, acc, sems = refs[PER_STEP:]
    step = pl.program_id(0)
    fetch_all(pieces, slots, tbuf, sems, step)
    half = FEAT // 2
    total = None
    for i in range(PER_STEP):
        rows = tbuf[step * PER_STEP + i]
        for j in range(2):
            part = jnp.dot(
                rows[:, j * half : (j + 1) * half], w_refs[i][j], preferred_element_type=jnp.float32
            )
            total = part if total is None else total + part

    @pl.when(step == 0)
    def _():
        acc[...] = total

    @pl.when(step > 0)
    def _():
        acc[...] += total

    @pl.when(step == GROUPS // PER_STEP - 1)
    def _():
        inverse = inverse_ref[...]
        cosine = cos_ref[...]
        sines = sin_ref[...]

        def head(i):
            return acc[:, i * HD : (i + 1) * HD] * inverse + bias_ref[:, i * HD : (i + 1) * HD]

        def turned(u):
            return u * cosine + pltpu.roll(u, HD // 2, 1) * sines

        if queries:
            for i in range(HEADS):
                q = (turned(head(i)) * QSCALE).astype(jnp.bfloat16)
                for b in range(BLOCKS):
                    out_ref[b, i * BLOCK : (i + 1) * BLOCK] = q[b * BLOCK : (b + 1) * BLOCK]
        else:
            out_ref[:, :HD] = turned(head(0)).astype(jnp.bfloat16)
            out_ref[:, HD:] = head(1).astype(jnp.bfloat16)


def w_spec(i, width, column):
    return pl.BlockSpec((2, ROWS, width), lambda k, ids: (ids[k * PER_STEP + i], 0, column))


def project(pieces, slots, ids, weights, inverse, bias, cosine, sines, queries):
    width = HEADS * HD if queries else 2 * HD
    column = 0 if queries else HEADS // 2
    out_shape = (BLOCKS, HEADS * BLOCK, HD) if queries else (ROWS, 2 * HD)

    def body(*refs):
        project_body(slots, queries, *refs)

    return pl.pallas_call(
        body,
        grid_spec=pltpu.PrefetchScalarGridSpec(
            num_scalar_prefetch=1,
            grid=(GROUPS // PER_STEP,),
            in_specs=[pl.BlockSpec(memory_space=pl.ANY)] * len(pieces)
            + [w_spec(i, width, column) for i in range(PER_STEP)]
            + [whole(ROWS, 1), whole(1, width), whole(ROWS, HD), whole(ROWS, HD)],
            out_specs=whole(*out_shape),
            scratch_shapes=[
                pltpu.VMEM((GROUPS, ROWS, FEAT), jnp.bfloat16),
                pltpu.VMEM((ROWS, width), jnp.float32),
                pltpu.SemaphoreType.DMA((len(pieces),)),
            ],
        ),
        out_shape=jax.ShapeDtypeStruct(out_shape, jnp.bfloat16),
        compiler_params=pltpu.CompilerParams(dimension_semantics=("arbitrary",)),
        cost_estimate=pl.CostEstimate(
            flops=2 * ROWS * MODEL * width, transcendentals=0, bytes_accessed=16 << 20
        ),
        name="project_queries" if queries else "project_keys",
    )(ids, *pieces, *([weights] * PER_STEP), inverse, bias, cosine, sines)


def attend_body(bounds, q_ref, qpos_ref, own_ref, other_ref, kpos_ref, out_ref, kv_ref, top, acc, sems):
    block_at = pl.program_id(0)
    full = bounds[0, block_at]
    need = bounds[1, block_at]

    def fetch(i):
        source = (own_ref, other_ref)[i]
        half = SOURCES // 2
        return pltpu.make_async_copy(source, kv_ref.at[pl.ds(i * half, half)], sems.at[i])

    @pl.when(block_at == 0)
    def _():
        fetch(0).start()
        fetch(1).start()

    top[...] = jnp.full_like(top, NEG_FILL)
    acc[...] = jnp.zeros_like(acc)

    @pl.when(block_at == 0)
    def _():
        fetch(0).wait()
        fetch(1).wait()

    ones = jnp.ones((KEYS, HD), jnp.bfloat16)
    parts = top.shape[0]
    rows = top.shape[1]

    def one_step(j, masked):
        at = pl.multiple_of(j * KSTEP, KSTEP)
        block = kv_ref[:, pl.ds(at, KSTEP), :].reshape(KEYS, 2 * HD)
        keys = block[:, :HD]
        values = jnp.concatenate([block[:, HD:], ones], axis=1)

        def scores_of(h):
            return lax.dot_general(
                q_ref[0, h * rows : (h + 1) * rows],
                keys,
                (((1,), (1,)), ((), ())),
                preferred_element_type=jnp.float32,
            )

        following = scores_of(0)
        for h in range(parts):
            scores = following
            following = scores_of(h + 1) if h + 1 < parts else None
            if masked:
                allowed = kpos_ref[j] <= qpos_ref[0, h * rows : (h + 1) * rows]
                scores = jnp.where(allowed, scores, NEG_FILL)
            old = top[h]
            new = jnp.maximum(old, jnp.max(scores, axis=1, keepdims=True))
            weights = jnp.exp2(scores - jnp.concatenate([new] * (KEYS // HD), axis=1))
            rescale = jnp.exp2(old - new)
            top[h] = new
            acc[h] = acc[h] * jnp.concatenate([rescale, rescale], axis=1) + jnp.dot(
                weights.astype(jnp.bfloat16), values, preferred_element_type=jnp.float32
            )

    def unmasked(j, carry):
        one_step(j, False)
        return carry

    def masked(j, carry):
        one_step(j, True)
        return carry

    lax.fori_loop(0, full, unmasked, 0)
    lax.fori_loop(full, need, masked, 0)
    for h in range(HEADS):
        part, at = (h * BLOCK // rows, h * BLOCK % rows)
        done = acc[part, at : at + BLOCK, :HD] / acc[part, at : at + BLOCK, HD:]
        out_ref[:, h * HD : (h + 1) * HD] = done.astype(jnp.bfloat16)


def attend(bounds, queries, qpos, own, other, kpos, first, count):
    part = 2 * BLOCK
    return pl.pallas_call(
        attend_body,
        grid_spec=pltpu.PrefetchScalarGridSpec(
            num_scalar_prefetch=1,
            grid=(count,),
            in_specs=[
                pl.BlockSpec((1, HEADS * BLOCK, HD), lambda c, b: (c + first, 0, 0)),
                pl.BlockSpec((1, HEADS * BLOCK, 1), lambda c, b: (c + first, 0, 0)),
                pl.BlockSpec(memory_space=pl.ANY),
                pl.BlockSpec(memory_space=pl.ANY),
                whole(NSTEPS, 1, KEYS),
            ],
            out_specs=pl.BlockSpec((BLOCK, HEADS * HD), lambda c, b: (c, 0)),
            scratch_shapes=[
                pltpu.VMEM((SOURCES, ROWS, 2 * HD), jnp.bfloat16),
                pltpu.VMEM((HEADS * BLOCK // part, part, HD), jnp.float32),
                pltpu.VMEM((HEADS * BLOCK // part, part, 2 * HD), jnp.float32),
                pltpu.SemaphoreType.DMA((2,)),
            ],
        ),
        out_shape=jax.ShapeDtypeStruct((BLOCK * count, HEADS * HD), jnp.bfloat16),
        compiler_params=pltpu.CompilerParams(dimension_semantics=("arbitrary",)),
        cost_estimate=pl.CostEstimate(
            flops=4 * HEADS * BLOCK * count * SOURCES * ROWS * HD,
            transcendentals=HEADS * BLOCK * count * SOURCES * ROWS,
            bytes_accessed=6 << 20,
        ),
    )(bounds, queries, qpos, own, other, kpos)


def mix_body(slots, ids, *refs):
    pieces = refs[: len(slots)]
    refs = refs[len(slots) :]
    w_refs = refs[:PER_STEP]
    back_ref, base_ref, out_ref, cbuf, acc, sems = refs[PER_STEP:]
    step = pl.program_id(0)
    fetch_all(pieces, slots, cbuf, sems, step)
    parts = []
    for half in range(2):
        total = None
        for i in range(PER_STEP):
            part = jnp.dot(
                cbuf[step * PER_STEP + i], w_refs[i][half], preferred_element_type=jnp.float32
            )
            total = part if total is None else total + part
        parts.append(total)

    @pl.when(step == 0)
    def _():
        for half in range(2):
            acc[:, half * 512 : (half + 1) * 512] = parts[half]

    @pl.when(step > 0)
    def _():
        for half in range(2):
            acc[:, half * 512 : (half + 1) * 512] += parts[half]

    @pl.when(step == GROUPS // PER_STEP - 1)
    def _():
        back = back_ref[...]
        high = acc[...].astype(jnp.bfloat16)
        low = (acc[...] - high.astype(jnp.float32)).astype(jnp.bfloat16)
        mixed = jnp.dot(back, high, preferred_element_type=jnp.float32) + jnp.dot(
            back, low, preferred_element_type=jnp.float32
        )
        out_ref[...] = (base_ref[...].astype(jnp.float32) + mixed).astype(out_ref.dtype)


def mix(pieces, ids, w_out, back, base, last):
    rows = pieces[0].shape[0]
    slots = [(i, 0, rows) for i in range(GROUPS)]

    def body(*refs):
        mix_body(slots, *refs)

    return pl.pallas_call(
        body,
        grid_spec=pltpu.PrefetchScalarGridSpec(
            num_scalar_prefetch=1,
            grid=(GROUPS // PER_STEP,),
            in_specs=[pl.BlockSpec(memory_space=pl.ANY)] * len(pieces)
            + [w_spec(i, 512, 0) for i in range(PER_STEP)]
            + [whole(ROWS, rows), whole(ROWS, FEAT)],
            out_specs=whole(ROWS, FEAT),
            scratch_shapes=[
                pltpu.VMEM((GROUPS, rows, HEADS * HD), jnp.bfloat16),
                pltpu.VMEM((rows, FEAT), jnp.float32),
                pltpu.SemaphoreType.DMA((len(pieces),)),
            ],
        ),
        out_shape=jax.ShapeDtypeStruct((ROWS, FEAT), jnp.bfloat16 if last else jnp.float32),
        compiler_params=pltpu.CompilerParams(dimension_semantics=("arbitrary",)),
        cost_estimate=pl.CostEstimate(
            flops=2 * rows * HEADS * HD * GROUPS * FEAT, transcendentals=0, bytes_accessed=12 << 20
        ),
        name="mix_last" if last else "mix_first",
    )(ids, *pieces, *([w_out] * PER_STEP), back, base)


def block(tokens, positions, norm_gain, w_query, w_key, w_value, b_query, b_key, b_value, w_out):
    bf16, f32 = (jnp.bfloat16, jnp.float32)
    seq_at = lax.axis_index(SEQ)
    zh, x = (lax.axis_index("zh"), lax.axis_index("x"))

    rank = jnp.sum((positions[None, :] < positions[:, None]).astype(jnp.int32), 1)
    chosen = rank[None, :] == jnp.arange(ROWS, dtype=jnp.int32)[:, None]
    order = chosen.astype(bf16)
    back = (rank[:, None] == jnp.arange(ROWS, dtype=jnp.int32)[None, :]).astype(bf16)
    sorted_pos = jnp.sum(jnp.where(chosen, positions[None, :], 0), 1)
    sorted_tokens = jnp.dot(order, tokens, preferred_element_type=f32).astype(bf16)

    w_cat = jnp.concatenate((w_query, w_key, w_value), 1)
    gain = lax.dynamic_slice(norm_gain, (seq_at * ROWS,), (ROWS,))
    w_cat = (w_cat.astype(f32) * gain[:, None]).astype(bf16)
    width = w_cat.shape[1]
    pos_rows = jnp.stack([sorted_pos >> 7, sorted_pos & 127]).astype(bf16)
    pos_rows = jnp.pad(pos_rows, ((0, POS_ROWS - 2), (0, width - ROWS)))
    weights = lax.all_gather(jnp.concatenate([w_cat, pos_rows], 0), SEQ, axis=0, tiled=True)
    weights = weights.reshape(SOURCES, ROWS + POS_ROWS, width)

    def ring(own):
        half = own.shape[0] // 2
        left = lax.ppermute(own, "x", NEXT)
        right = lax.ppermute(own, "x", PREV)
        low, high = (left[:half], right[half:])
        low = lax.ppermute(low, "x", NEXT)
        high = lax.ppermute(high, "x", PREV)
        return left, right, low, high

    other = lax.ppermute(sorted_tokens, "zh", SWAP)
    left, right, low, high = ring(sorted_tokens)
    oleft, oright, olow, ohigh = ring(other)

    def square(piece):
        wide = piece.astype(f32)
        return jnp.sum(wide * wide, 1, keepdims=True)

    total = sum(square(p) for p in (sorted_tokens, left, right, other, oleft, oright))
    total += jnp.concatenate([square(low), square(high)], 0)
    total += jnp.concatenate([square(olow), square(ohigh)], 0)
    inverse = lax.rsqrt(total * (1.0 / MODEL) + NORM_EPS)
    ids = jnp.stack(
        [z * 4 + (x + d) % 4 for z in (zh, 1 - zh) for d in (0, 3, 1, 2)]
    ).astype(jnp.int32)
    ids = ids[jnp.array([0, 1, 2, 4, 3, 5, 6, 7])]
    half = ROWS // 2
    pieces = [sorted_tokens, left, right, other, low, high, oleft, oright, olow, ohigh]
    slots = [
        (0, 0, ROWS),
        (1, 0, ROWS),
        (2, 0, ROWS),
        (3, 0, ROWS),
        (4, 0, half),
        (4, half, half),
        (5, 0, ROWS),
        (6, 0, ROWS),
        (7, 0, half),
        (7, half, half),
    ]

    half_dim = HD // 2
    inv_freq = ROPE_BASE ** (-jnp.arange(half_dim, dtype=f32) * 2.0 / HD)
    angles = sorted_pos.astype(f32)[:, None] * inv_freq[None, :]
    cosine = jnp.cos(angles)
    sines = jnp.sin(angles)
    cosine = jnp.concatenate([cosine, cosine], 1)
    sines = jnp.concatenate([-sines, sines], 1)

    kv_bias = jnp.concatenate((b_key, b_value))[None, :]
    kv = project(pieces, slots, ids, weights, inverse, kv_bias, cosine, sines, False)

    def flipped(steps):
        turn = dict(steps)
        return [(a * 2 + b, turn[a] * 2 + 1 - b) for a in range(4) for b in range(2)]

    found = [kv, lax.ppermute(kv, "zl", SWAP)]
    found += [lax.ppermute(kv, "y", steps) for steps in (NEXT, PREV, ACROSS)]
    found += [lax.ppermute(kv, ("y", "zl"), flipped(steps)) for steps in (NEXT, PREV, ACROSS)]
    own_kv = jnp.stack(found)
    other_kv = lax.ppermute(own_kv, "core", SWAP)
    y, zl, core = (lax.axis_index("y"), lax.axis_index("zl"), lax.axis_index("core"))
    chips = [y * 2 + zl, y * 2 + 1 - zl]
    chips += [(y + d) % 4 * 2 + z for z in (zl, 1 - zl) for d in (3, 1, 2)]
    sources = jnp.stack([chip * 2 + c for c in (core, 1 - core) for chip in chips])

    queries = project(
        pieces, slots, ids, weights, inverse, b_query[None, :], cosine, sines, True
    )

    pos_all = weights[:, ROWS : ROWS + 2, :ROWS].astype(jnp.int32)
    pos_all = pos_all[:, 0] * 128 + pos_all[:, 1]
    picked = sources[:, None] == jnp.arange(SOURCES)[None, :]
    pos_all = jnp.sum(jnp.where(picked[:, :, None], pos_all[None], 0), 1)
    kpos = pos_all.reshape(SOURCES, NSTEPS, KSTEP).transpose(1, 0, 2)
    first_pos = jnp.min(kpos, (1, 2))
    last_pos = jnp.max(kpos, (1, 2))
    kpos = kpos.reshape(NSTEPS, 1, KEYS)
    by_block = sorted_pos.reshape(BLOCKS, BLOCK)
    full = jnp.sum((last_pos[None, :] <= by_block[:, :1]).astype(jnp.int32), 1)
    need = jnp.sum((first_pos[None, :] <= by_block[:, -1:]).astype(jnp.int32), 1)
    bounds = jnp.stack([full, need])
    qpos = jnp.tile(by_block[:, None, :], (1, HEADS, 1)).reshape(BLOCKS, HEADS * BLOCK, 1)

    swap = [
        ((a * 2 + c) * 8 + b, (b * 2 + c) * 8 + a)
        for a in range(8)
        for c in range(2)
        for b in range(8)
    ]
    moved = lax.ppermute(w_out, SEQ + TENSOR, swap)
    moved, other_kv = lax.optimization_barrier((moved, other_kv))
    w_out_all = lax.all_gather(moved, SEQ, axis=0, tiled=True).reshape(SOURCES, 512, 512)

    mix_ids = jnp.stack([z * 4 + (x + d) % 4 for z in (zh, 1 - zh) for d in (0, 3, 1, 2)])
    base = tokens
    contexts = []
    for first, count in CALLS:
        at = slice(first, first + count)
        own = attend(bounds[:, at], queries, qpos, own_kv, other_kv, kpos, first, count)
        contexts.append(own)
        across = lax.ppermute(own, "zh", SWAP)
        near = [own] + [lax.ppermute(own, "x", s) for s in (NEXT, PREV, ACROSS)]
        far = [across] + [lax.ppermute(across, "x", s) for s in (NEXT, PREV)]
        found = near + far + [lax.ppermute(near[3], "zh", SWAP)]
        last = first + count == BLOCKS
        rows = slice(first * BLOCK, (first + count) * BLOCK)
        base = mix(found, mix_ids.astype(jnp.int32), w_out_all, back[:, rows], base, last)
    context = jnp.dot(back, jnp.concatenate(contexts, 0), preferred_element_type=f32).astype(bf16)
    return (base, context)


def solution(mesh):
    fine = Mesh(mesh.devices.reshape(4, 2, 2, 2, 4), SEQ + TENSOR)
    in_specs = (
        P(SEQ, TENSOR),
        P(SEQ),
        P(),
        P(SEQ, TENSOR),
        P(SEQ, TENSOR),
        P(SEQ, TENSOR),
        P(TENSOR),
        P(TENSOR),
        P(TENSOR),
        P(TENSOR, SEQ),
    )
    out_specs = (P(SEQ, TENSOR), P(SEQ, TENSOR))
    return jax.shard_map(block, mesh=fine, in_specs=in_specs, out_specs=out_specs, check_vma=False)
```

profile of v0, /device:TPU:0, one launch (start us, length us, event | category | flops | bytes accessed | tf_op | source)
XLA Modules:
  0.0 287.1 jit_solution(7763175900579702542)
XLA Ops:
  14.1 4.0 %collective-permute-start.2 = (bf16[512,1024]{1,0:T(8,128)(2,1)}, bf16[512,1024]{1,0:T(8,128)(2,1)}, u32[]{:S(2)}, u32[]{:S(2)}) collective-permute-start(bf16[512,1024]{1,0:T(8,128)(2,1)} %get-tuple-element.21.refs_1_), channel_id=1, source_target_pairs={{0,4},{4,0},{1,5},{5,1},{2,6},{6,2},{3,7},{7,3},{8,12},{12,8},{9,1... | collective-permute-start | bytes 3145736 | tf_op jit(solution)/shard_map/ppermute | solution.py:350
  19.6 1.7 collective-permute-start.1
  23.7 35.1 %collective-permute-done.2.refs_4_ = bf16[512,1024]{1,0:T(8,128)(2,1)} collective-permute-done((bf16[512,1024]{1,0:T(8,128)(2,1)}, bf16[512,1024]{1,0:T(8,128)(2,1)}, u32[]{:S(2)}, u32[]{:S(2)}) %collective-permute-start.2) | collective-permute-done | bytes 1048608 | tf_op jit(solution)/shard_map/ppermute | solution.py:350
  60.1 1.9 collective-permute-start.6
  63.9 3.2 %collective-permute-start.4 = (bf16[256,1024]{1,0:T(8,128)(2,1)S(1)}, bf16[256,1024]{1,0:T(8,128)(2,1)S(1)}, u32[]{:S(2)}, u32[]{:S(2)}) collective-permute-start(bf16[256,1024]{1,0:T(8,128)(2,1)S(1)} %slice.58), channel_id=1, source_target_pairs={{0,3},{1,0},{2,1},{3,2},{4,7},{5,4},{6,5},{7,6},{8,11},{9,8},{10,9... | collective-permute-start | bytes 1572872 | tf_op jit(solution)/shard_map/ppermute | solution.py:347
  69.1 23.9 %collective-permute-done.4.refs_6_ = bf16[256,1024]{1,0:T(8,128)(2,1)S(1)} collective-permute-done((bf16[256,1024]{1,0:T(8,128)(2,1)S(1)}, bf16[256,1024]{1,0:T(8,128)(2,1)S(1)}, u32[]{:S(2)}, u32[]{:S(2)}) %collective-permute-start.4) | collective-permute-done | bytes 524320 | tf_op jit(solution)/shard_map/ppermute | solution.py:347
  97.7 6.8 %collective-permute-done.8.refs_10_ = bf16[256,1024]{1,0:T(8,128)(2,1)S(1)} collective-permute-done((bf16[256,1024]{1,0:T(8,128)(2,1)S(1)}, bf16[256,1024]{1,0:T(8,128)(2,1)S(1)}, u32[]{:S(2)}, u32[]{:S(2)}) %collective-permute-start.8) | collective-permute-done | bytes 524320 | tf_op jit(solution)/shard_map/ppermute | solution.py:347
  105.8 8.6 %project_keys.1 = bf16[512,256]{1,0:T(8,128)(2,1)} custom-call(s32[8]{0:T(128)} %gather_fusion, bf16[512,1024]{1,0:T(8,128)(2,1)} %get-tuple-element.21.refs_1_, bf16[512,1024]{1,0:T(8,128)(2,1)} %copy-done.1, bf16[512,1024]{1,0:T(8,128)(2,1)} %copy-done.2, bf16[512,1024]{1,0:T(8,128)(2,1)} %collective-permute-done.2.refs_4_, bf16[256,1024]{1,0:T(8,128)(2,1)} %copy-done.5, ...), custom_call_target="tpu_custom_call" | custom-call | flops 2147483648 | bytes 16777216 | tf_op jit(solution)/shard_map/project_keys/pallas_call | solution.py:122
  116.8 3.3 %collective-permute-start.11 = (bf16[512,256]{1,0:T(8,128)(2,1)}, bf16[512,256]{1,0:T(8,128)(2,1)S(1)}, u32[]{:S(2)}, u32[]{:S(2)}) collective-permute-start(bf16[512,256]{1,0:T(8,128)(2,1)} %project_keys.1), channel_id=1, source_target_pairs={{0,96},{32,0},{64,32},{96,64},{1,97},{33,1},{65,33},{97,65},{2,98}... | collective-permute-start | bytes 786440 | tf_op jit(solution)/shard_map/ppermute | solution.py:397
  121.5 2.4 collective-permute-start.13
  123.9 1.7 collective-permute-start.14
  126.4 1.9 collective-permute-start.15
  129.0 3.7 %collective-permute-done.11 = bf16[512,256]{1,0:T(8,128)(2,1)S(1)} collective-permute-done((bf16[512,256]{1,0:T(8,128)(2,1)}, bf16[512,256]{1,0:T(8,128)(2,1)S(1)}, u32[]{:S(2)}, u32[]{:S(2)}) %collective-permute-start.11) | collective-permute-done | bytes 262176 | tf_op jit(solution)/shard_map/ppermute | solution.py:397
  134.1 10.6 %collective-permute-done.13 = bf16[512,256]{1,0:T(8,128)(2,1)S(1)} collective-permute-done((bf16[512,256]{1,0:T(8,128)(2,1)}, bf16[512,256]{1,0:T(8,128)(2,1)S(1)}, u32[]{:S(2)}, u32[]{:S(2)}) %collective-permute-start.13) | collective-permute-done | bytes 262176 | tf_op jit(solution)/shard_map/ppermute | solution.py:398
  147.7 3.8 %collective-permute-done.17.other_ref = bf16[8,512,256]{2,1,0:T(8,128)(2,1)} collective-permute-done((bf16[8,512,256]{2,1,0:T(8,128)(2,1)}, bf16[8,512,256]{2,1,0:T(8,128)(2,1)}, u32[]{:S(2)}, u32[]{:S(2)}) %collective-permute-start.17) | collective-permute-done | bytes 2097184 | tf_op jit(solution)/shard_map/ppermute | solution.py:400
  156.6 11.2 %project_queries.1.q_ref = bf16[4,512,128]{2,1,0:T(8,128)(2,1)} custom-call(s32[8]{0:T(128)} %gather_fusion, bf16[512,1024]{1,0:T(8,128)(2,1)} %get-tuple-element.21.refs_1_, bf16[512,1024]{1,0:T(8,128)(2,1)} %copy-done.1, bf16[512,1024]{1,0:T(8,128)(2,1)} %copy-done.2, bf16[512,1024]{1,0:T(8,128)(2,1)} %collective-permute-done.2.refs_4_, ...), custom_call_target="tpu_custom_call" | custom-call | flops 4294967296 | bytes 16777216 | tf_op jit(solution)/shard_map/project_queries/pallas_call | solution.py:122
  167.9 18.4 %shard_map.122.refs_1_ = bf16[256,512]{1,0:T(8,128)(2,1)} custom-call(s32[2,2]{1,0:T(2,128)} %get-tuple-element.19.bounds, bf16[4,512,128]{2,1,0:T(8,128)(2,1)} %project_queries.1.q_ref, s32[4,512,1]{2,1,0:T(8,128)} %copy.45.qpos_ref, bf16[8,512,256]{2,1,0:T(8,128)(2,1)} %bitcast_dynamic-update-slice_fusion.own_ref, ...), custom_call_target="tpu_custom_call" | custom-call | flops 4294967296 | bytes 6291456 | tf_op jit(solution)/shard_map/pallas_call | solution.py:221
  186.3 18.2 %collective-permute-start.20 = (bf16[256,512]{1,0:T(8,128)(2,1)}, bf16[256,512]{1,0:T(8,128)(2,1)S(1)}, u32[]{:S(2)}, u32[]{:S(2)}) collective-permute-start(bf16[256,512]{1,0:T(8,128)(2,1)} %shard_map.122.refs_1_), channel_id=1, source_target_pairs={{0,2},{1,3},{2,0},{3,1},{4,6},{5,7},{6,4},{7,5},{8,10},{9,11},{10,... | collective-permute-start | bytes 786440 | tf_op jit(solution)/shard_map/ppermute | solution.py:442
  204.5 12.5 %shard_map.123.refs_1_ = bf16[256,512]{1,0:T(8,128)(2,1)} custom-call(s32[2,2]{1,0:T(2,128)} %get-tuple-element.18.bounds, bf16[4,512,128]{2,1,0:T(8,128)(2,1)} %project_queries.1.q_ref, s32[4,512,1]{2,1,0:T(8,128)} %copy.45.qpos_ref, bf16[8,512,256]{2,1,0:T(8,128)(2,1)} %bitcast_dynamic-update-slice_fusion.own_ref, ...), custom_call_target="tpu_custom_call" | custom-call | flops 4294967296 | bytes 6291456 | tf_op jit(solution)/shard_map/pallas_call | solution.py:221
  216.9 10.3 %collective-permute-start.28 = (bf16[256,512]{1,0:T(8,128)(2,1)}, bf16[256,512]{1,0:T(8,128)(2,1)S(1)}, u32[]{:S(2)}, u32[]{:S(2)}) collective-permute-start(bf16[256,512]{1,0:T(8,128)(2,1)} %shard_map.123.refs_1_), channel_id=1, source_target_pairs={{0,4},{4,0},{1,5},{5,1},{2,6},{6,2},{3,7},{7,3},{8,12},{12,8},{9,1... | collective-permute-start | bytes 786440 | tf_op jit(solution)/shard_map/ppermute | solution.py:441
  227.4 3.5 %collective-permute-start.27 = (bf16[256,512]{1,0:T(8,128)(2,1)}, bf16[256,512]{1,0:T(8,128)(2,1)S(1)}, u32[]{:S(2)}, u32[]{:S(2)}) collective-permute-start(bf16[256,512]{1,0:T(8,128)(2,1)} %shard_map.123.refs_1_), channel_id=1, source_target_pairs={{0,2},{1,3},{2,0},{3,1},{4,6},{5,7},{6,4},{7,5},{8,10},{9,11},{10,... | collective-permute-start | bytes 786440 | tf_op jit(solution)/shard_map/ppermute | solution.py:442
  230.9 2.1 collective-permute-start.25
  233.0 2.7 collective-permute-start.26
  235.7 2.1 collective-permute-done.28.refs_5_
  237.7 2.6 collective-permute-start.29
  240.3 2.9 %collective-permute-done.21.refs_5_ = bf16[256,512]{1,0:T(8,128)(2,1)S(1)} collective-permute-done((bf16[256,512]{1,0:T(8,128)(2,1)S(1)}, bf16[256,512]{1,0:T(8,128)(2,1)S(1)}, u32[]{:S(2)}, u32[]{:S(2)}) %collective-permute-start.21) | collective-permute-done | bytes 262176 | tf_op jit(solution)/shard_map/ppermute | solution.py:441
  243.2 2.7 collective-permute-start.30
  247.7 2.8 collective-permute-start.19
  252.6 3.7 %collective-permute-start.23 = (bf16[256,512]{1,0:T(8,128)(2,1)S(1)}, bf16[256,512]{1,0:T(8,128)(2,1)}, u32[]{:S(2)}, u32[]{:S(2)}) collective-permute-start(bf16[256,512]{1,0:T(8,128)(2,1)S(1)} %collective-permute-done.21.refs_5_), channel_id=1, source_target_pairs={{0,3},{1,0},{2,1},{3,2},{4,7},{5,4},{6,5},{7,6},{8,11},{9,8},{10,9... | collective-permute-start | bytes 786440 | tf_op jit(solution)/shard_map/ppermute | solution.py:443
  256.9 2.2 convolution_convert_fusion.1
  259.2 10.1 %mix_first.1.refs_12_ = f32[512,1024]{1,0:T(8,128)} custom-call(s32[8]{0:T(128)} %copy-done, bf16[256,512]{1,0:T(8,128)(2,1)} %shard_map.123.refs_1_, bf16[256,512]{1,0:T(8,128)(2,1)} %copy-done.16, bf16[256,512]{1,0:T(8,128)(2,1)} %copy-done.17, bf16[256,512]{1,0:T(8,128)(2,1)} %copy-done.15, bf16[256,512]{1,0:T(8,128)(2,1)} %copy-done.14, ...), custom_call_target="tpu_custom_call" | custom-call | flops 2147483648 | bytes 12582912 | tf_op jit(solution)/shard_map/mix_first/pallas_call | solution.py:296
  270.2 10.1 %mix_last.1 = bf16[512,1024]{1,0:T(8,128)(2,1)} custom-call(s32[8]{0:T(128)} %copy-done, bf16[256,512]{1,0:T(8,128)(2,1)} %shard_map.122.refs_1_, bf16[256,512]{1,0:T(8,128)(2,1)} %copy-done.18, bf16[256,512]{1,0:T(8,128)(2,1)} %copy-done.20, bf16[256,512]{1,0:T(8,128)(2,1)} %copy-done.12, bf16[256,512]{1,0:T(8,128)(2,1)} %copy-done.13, ...), custom_call_target="tpu_custom_call" | custom-call | flops 2147483648 | bytes 12582912 | tf_op jit(solution)/shard_map/mix_last/pallas_call | solution.py:296
  (167 shorter events, 41.9 us)
Async XLA Ops:
  7.2 98.6 %all-gather.3.cloned.1.call-start = ((), (), s32[]{:S(2)}) async-start(), calls=%async_computation | async-start | bytes 13787136 | tf_op jit(solution)/shard_map/all_gather | solution.py:338
  12.4 246.7 %all-gather.5.cloned.1.call-start = ((), (), s32[]{:S(2)}) async-start(), calls=%async_computation.1 | async-start | bytes 8912896 | tf_op jit(solution)/shard_map/all_gather | solution.py:432
  14.1 44.6 %collective-permute-start.2 = (bf16[512,1024]{1,0:T(8,128)(2,1)}, bf16[512,1024]{1,0:T(8,128)(2,1)}, u32[]{:S(2)}, u32[]{:S(2)}) collective-permute-start(bf16[512,1024]{1,0:T(8,128)(2,1)} %get-tuple-element.21.refs_1_), channel_id=1, source_target_pairs={{0,4},{4,0},{1,5},{5,1},{2,6},{6,2},{3,7},{7,3},{8,12},{12,8},{9,1... | collective-permute-start | bytes 3145736 | tf_op jit(solution)/shard_map/ppermute | solution.py:350
  18.1 45.5 %collective-permute-start = (bf16[512,1024]{1,0:T(8,128)(2,1)}, bf16[512,1024]{1,0:T(8,128)(2,1)S(1)}, u32[]{:S(2)}, u32[]{:S(2)}) collective-permute-start(bf16[512,1024]{1,0:T(8,128)(2,1)} %get-tuple-element.21.refs_1_), channel_id=1, source_target_pairs={{0,1},{1,2},{2,3},{3,0},{4,5},{5,6},{6,7},{7,4},{8,9},{9,10},{10,1... | collective-permute-start | bytes 3145736 | tf_op jit(solution)/shard_map/ppermute | solution.py:343
  19.6 44.2 %collective-permute-start.1 = (bf16[512,1024]{1,0:T(8,128)(2,1)}, bf16[512,1024]{1,0:T(8,128)(2,1)S(1)}, u32[]{:S(2)}, u32[]{:S(2)}) collective-permute-start(bf16[512,1024]{1,0:T(8,128)(2,1)} %get-tuple-element.21.refs_1_), channel_id=1, source_target_pairs={{0,3},{1,0},{2,1},{3,2},{4,7},{5,4},{6,5},{7,6},{8,11},{9,8},{10,9... | collective-permute-start | bytes 3145736 | tf_op jit(solution)/shard_map/ppermute | solution.py:344
  58.7 34.7 %collective-permute-start.5 = (bf16[512,1024]{1,0:T(8,128)(2,1)}, bf16[512,1024]{1,0:T(8,128)(2,1)S(1)}, u32[]{:S(2)}, u32[]{:S(2)}) collective-permute-start(bf16[512,1024]{1,0:T(8,128)(2,1)} %collective-permute-done.2.refs_4_), channel_id=1, source_target_pairs={{0,1},{1,2},{2,3},{3,0},{4,5},{5,6},{6,7},{7,4},{8,9},{9,10},{10,1... | collective-permute-start | bytes 3145736 | tf_op jit(solution)/shard_map/ppermute | solution.py:343
  60.1 35.1 %collective-permute-start.6 = (bf16[512,1024]{1,0:T(8,128)(2,1)}, bf16[512,1024]{1,0:T(8,128)(2,1)S(1)}, u32[]{:S(2)}, u32[]{:S(2)}) collective-permute-start(bf16[512,1024]{1,0:T(8,128)(2,1)} %collective-permute-done.2.refs_4_), channel_id=1, source_target_pairs={{0,3},{1,0},{2,1},{3,2},{4,7},{5,4},{6,5},{7,6},{8,11},{9,8},{10,9... | collective-permute-start | bytes 3145736 | tf_op jit(solution)/shard_map/ppermute | solution.py:344
  63.6 29.6 %collective-permute-start.3 = (bf16[256,1024]{1,0:T(8,128)(2,1)S(1)}, bf16[256,1024]{1,0:T(8,128)(2,1)S(1)}, u32[]{:S(2)}, u32[]{:S(2)}) collective-permute-start(bf16[256,1024]{1,0:T(8,128)(2,1)S(1)} %slice.57), channel_id=1, source_target_pairs={{0,1},{1,2},{2,3},{3,0},{4,5},{5,6},{6,7},{7,4},{8,9},{9,10},{10,1... | collective-permute-start | bytes 1572872 | tf_op jit(solution)/shard_map/ppermute | solution.py:346
  63.9 29.2 %collective-permute-start.4 = (bf16[256,1024]{1,0:T(8,128)(2,1)S(1)}, bf16[256,1024]{1,0:T(8,128)(2,1)S(1)}, u32[]{:S(2)}, u32[]{:S(2)}) collective-permute-start(bf16[256,1024]{1,0:T(8,128)(2,1)S(1)} %slice.58), channel_id=1, source_target_pairs={{0,3},{1,0},{2,1},{3,2},{4,7},{5,4},{6,5},{7,6},{8,11},{9,8},{10,9... | collective-permute-start | bytes 1572872 | tf_op jit(solution)/shard_map/ppermute | solution.py:347
  93.5 11.2 %collective-permute-start.7 = (bf16[256,1024]{1,0:T(8,128)(2,1)S(1)}, bf16[256,1024]{1,0:T(8,128)(2,1)S(1)}, u32[]{:S(2)}, u32[]{:S(2)}) collective-permute-start(bf16[256,1024]{1,0:T(8,128)(2,1)S(1)} %slice.59), channel_id=1, source_target_pairs={{0,1},{1,2},{2,3},{3,0},{4,5},{5,6},{6,7},{7,4},{8,9},{9,10},{10,1... | collective-permute-start | bytes 1572872 | tf_op jit(solution)/shard_map/ppermute | solution.py:346
  95.3 9.2 %collective-permute-start.8 = (bf16[256,1024]{1,0:T(8,128)(2,1)S(1)}, bf16[256,1024]{1,0:T(8,128)(2,1)S(1)}, u32[]{:S(2)}, u32[]{:S(2)}) collective-permute-start(bf16[256,1024]{1,0:T(8,128)(2,1)S(1)} %slice.60), channel_id=1, source_target_pairs={{0,3},{1,0},{2,1},{3,2},{4,7},{5,4},{6,5},{7,6},{8,11},{9,8},{10,9... | collective-permute-start | bytes 1572872 | tf_op jit(solution)/shard_map/ppermute | solution.py:347
  114.5 9.5 %collective-permute-start.9 = (bf16[512,256]{1,0:T(8,128)(2,1)}, bf16[512,256]{1,0:T(8,128)(2,1)S(1)}, u32[]{:S(2)}, u32[]{:S(2)}) collective-permute-start(bf16[512,256]{1,0:T(8,128)(2,1)} %project_keys.1), channel_id=1, source_target_pairs={{0,16},{16,0},{1,17},{17,1},{2,18},{18,2},{3,19},{19,3},{4,20},{20... | collective-permute-start | bytes 786440 | tf_op jit(solution)/shard_map/ppermute | solution.py:396
  115.1 11.4 %collective-permute-start.10 = (bf16[512,256]{1,0:T(8,128)(2,1)}, bf16[512,256]{1,0:T(8,128)(2,1)S(1)}, u32[]{:S(2)}, u32[]{:S(2)}) collective-permute-start(bf16[512,256]{1,0:T(8,128)(2,1)} %project_keys.1), channel_id=1, source_target_pairs={{0,32},{32,64},{64,96},{96,0},{1,33},{33,65},{65,97},{97,1},{2,34}... | collective-permute-start | bytes 786440 | tf_op jit(solution)/shard_map/ppermute | solution.py:397
  116.8 15.9 %collective-permute-start.11 = (bf16[512,256]{1,0:T(8,128)(2,1)}, bf16[512,256]{1,0:T(8,128)(2,1)S(1)}, u32[]{:S(2)}, u32[]{:S(2)}) collective-permute-start(bf16[512,256]{1,0:T(8,128)(2,1)} %project_keys.1), channel_id=1, source_target_pairs={{0,96},{32,0},{64,32},{96,64},{1,97},{33,1},{65,33},{97,65},{2,98}... | collective-permute-start | bytes 786440 | tf_op jit(solution)/shard_map/ppermute | solution.py:397
  120.1 13.3 %collective-permute-start.12 = (bf16[512,256]{1,0:T(8,128)(2,1)}, bf16[512,256]{1,0:T(8,128)(2,1)S(1)}, u32[]{:S(2)}, u32[]{:S(2)}) collective-permute-start(bf16[512,256]{1,0:T(8,128)(2,1)} %project_keys.1), channel_id=1, source_target_pairs={{0,64},{32,96},{64,0},{96,32},{1,65},{33,97},{65,1},{97,33},{2,66}... | collective-permute-start | bytes 786440 | tf_op jit(solution)/shard_map/ppermute | solution.py:397
  121.5 23.3 %collective-permute-start.13 = (bf16[512,256]{1,0:T(8,128)(2,1)}, bf16[512,256]{1,0:T(8,128)(2,1)S(1)}, u32[]{:S(2)}, u32[]{:S(2)}) collective-permute-start(bf16[512,256]{1,0:T(8,128)(2,1)} %project_keys.1), channel_id=1, source_target_pairs={{0,48},{16,32},{32,80},{48,64},{64,112},{80,96},{96,16},{112,0},{1... | collective-permute-start | bytes 786440 | tf_op jit(solution)/shard_map/ppermute | solution.py:398
  123.9 21.6 %collective-permute-start.14 = (bf16[512,256]{1,0:T(8,128)(2,1)}, bf16[512,256]{1,0:T(8,128)(2,1)S(1)}, u32[]{:S(2)}, u32[]{:S(2)}) collective-permute-start(bf16[512,256]{1,0:T(8,128)(2,1)} %project_keys.1), channel_id=1, source_target_pairs={{0,112},{16,96},{32,16},{48,0},{64,48},{80,32},{96,80},{112,64},{1... | collective-permute-start | bytes 786440 | tf_op jit(solution)/shard_map/ppermute | solution.py:398
  126.4 19.9 %collective-permute-start.15 = (bf16[512,256]{1,0:T(8,128)(2,1)}, bf16[512,256]{1,0:T(8,128)(2,1)S(1)}, u32[]{:S(2)}, u32[]{:S(2)}) collective-permute-start(bf16[512,256]{1,0:T(8,128)(2,1)} %project_keys.1), channel_id=1, source_target_pairs={{0,80},{16,64},{32,112},{48,96},{64,16},{80,0},{96,48},{112,32},{1... | collective-permute-start | bytes 786440 | tf_op jit(solution)/shard_map/ppermute | solution.py:398
  186.3 46.7 %collective-permute-start.20 = (bf16[256,512]{1,0:T(8,128)(2,1)}, bf16[256,512]{1,0:T(8,128)(2,1)S(1)}, u32[]{:S(2)}, u32[]{:S(2)}) collective-permute-start(bf16[256,512]{1,0:T(8,128)(2,1)} %shard_map.122.refs_1_), channel_id=1, source_target_pairs={{0,2},{1,3},{2,0},{3,1},{4,6},{5,7},{6,4},{7,5},{8,10},{9,11},{10,... | collective-permute-start | bytes 786440 | tf_op jit(solution)/shard_map/ppermute | solution.py:442
  216.9 20.8 %collective-permute-start.28 = (bf16[256,512]{1,0:T(8,128)(2,1)}, bf16[256,512]{1,0:T(8,128)(2,1)S(1)}, u32[]{:S(2)}, u32[]{:S(2)}) collective-permute-start(bf16[256,512]{1,0:T(8,128)(2,1)} %shard_map.123.refs_1_), channel_id=1, source_target_pairs={{0,4},{4,0},{1,5},{5,1},{2,6},{6,2},{3,7},{7,3},{8,12},{12,8},{9,1... | collective-permute-start | bytes 786440 | tf_op jit(solution)/shard_map/ppermute | solution.py:441
  227.3 15.9 %collective-permute-start.21 = (bf16[256,512]{1,0:T(8,128)(2,1)S(1)}, bf16[256,512]{1,0:T(8,128)(2,1)S(1)}, u32[]{:S(2)}, u32[]{:S(2)}) collective-permute-start(bf16[256,512]{1,0:T(8,128)(2,1)S(1)} %copy-done.11), channel_id=1, source_target_pairs={{0,4},{4,0},{1,5},{5,1},{2,6},{6,2},{3,7},{7,3},{8,12},{12,8},{9,1... | collective-permute-start | bytes 786440 | tf_op jit(solution)/shard_map/ppermute | solution.py:441
  227.4 18.5 %collective-permute-start.27 = (bf16[256,512]{1,0:T(8,128)(2,1)}, bf16[256,512]{1,0:T(8,128)(2,1)S(1)}, u32[]{:S(2)}, u32[]{:S(2)}) collective-permute-start(bf16[256,512]{1,0:T(8,128)(2,1)} %shard_map.123.refs_1_), channel_id=1, source_target_pairs={{0,2},{1,3},{2,0},{3,1},{4,6},{5,7},{6,4},{7,5},{8,10},{9,11},{10,... | collective-permute-start | bytes 786440 | tf_op jit(solution)/shard_map/ppermute | solution.py:442
  230.9 16.4 %collective-permute-start.25 = (bf16[256,512]{1,0:T(8,128)(2,1)}, bf16[256,512]{1,0:T(8,128)(2,1)S(1)}, u32[]{:S(2)}, u32[]{:S(2)}) collective-permute-start(bf16[256,512]{1,0:T(8,128)(2,1)} %shard_map.123.refs_1_), channel_id=1, source_target_pairs={{0,1},{1,2},{2,3},{3,0},{4,5},{5,6},{6,7},{7,4},{8,9},{9,10},{10,1... | collective-permute-start | bytes 786440 | tf_op jit(solution)/shard_map/ppermute | solution.py:442
  233.0 14.7 %collective-permute-start.26 = (bf16[256,512]{1,0:T(8,128)(2,1)}, bf16[256,512]{1,0:T(8,128)(2,1)S(1)}, u32[]{:S(2)}, u32[]{:S(2)}) collective-permute-start(bf16[256,512]{1,0:T(8,128)(2,1)} %shard_map.123.refs_1_), channel_id=1, source_target_pairs={{0,3},{1,0},{2,1},{3,2},{4,7},{5,4},{6,5},{7,6},{8,11},{9,8},{10,9... | collective-permute-start | bytes 786440 | tf_op jit(solution)/shard_map/ppermute | solution.py:442
  237.7 12.8 %collective-permute-start.29 = (bf16[256,512]{1,0:T(8,128)(2,1)S(1)}, bf16[256,512]{1,0:T(8,128)(2,1)S(1)}, u32[]{:S(2)}, u32[]{:S(2)}) collective-permute-start(bf16[256,512]{1,0:T(8,128)(2,1)S(1)} %collective-permute-done.28.refs_5_), channel_id=1, source_target_pairs={{0,1},{1,2},{2,3},{3,0},{4,5},{5,6},{6,7},{7,4},{8,9},{9,10},{10,1... | collective-permute-start | bytes 786440 | tf_op jit(solution)/shard_map/ppermute | solution.py:443
  243.2 9.4 %collective-permute-start.30 = (bf16[256,512]{1,0:T(8,128)(2,1)S(1)}, bf16[256,512]{1,0:T(8,128)(2,1)S(1)}, u32[]{:S(2)}, u32[]{:S(2)}) collective-permute-start(bf16[256,512]{1,0:T(8,128)(2,1)S(1)} %collective-permute-done.28.refs_5_), channel_id=1, source_target_pairs={{0,3},{1,0},{2,1},{3,2},{4,7},{5,4},{6,5},{7,6},{8,11},{9,8},{10,9... | collective-permute-start | bytes 786440 | tf_op jit(solution)/shard_map/ppermute | solution.py:443
  245.9 10.4 %collective-permute-start.31 = (bf16[256,512]{1,0:T(8,128)(2,1)S(1)}, bf16[256,512]{1,0:T(8,128)(2,1)S(1)}, u32[]{:S(2)}, u32[]{:S(2)}) collective-permute-start(bf16[256,512]{1,0:T(8,128)(2,1)S(1)} %collective-permute-done.27.refs_4_), channel_id=1, source_target_pairs={{0,4},{4,0},{1,5},{5,1},{2,6},{6,2},{3,7},{7,3},{8,12},{12,8},{9,1... | collective-permute-start | bytes 786440 | tf_op jit(solution)/shard_map/ppermute | solution.py:444
  247.2 22.0 %collective-permute-start.18 = (bf16[256,512]{1,0:T(8,128)(2,1)S(1)}, bf16[256,512]{1,0:T(8,128)(2,1)S(1)}, u32[]{:S(2)}, u32[]{:S(2)}) collective-permute-start(bf16[256,512]{1,0:T(8,128)(2,1)S(1)} %copy-done.11), channel_id=1, source_target_pairs={{0,1},{1,2},{2,3},{3,0},{4,5},{5,6},{6,7},{7,4},{8,9},{9,10},{10,1... | collective-permute-start | bytes 786440 | tf_op jit(solution)/shard_map/ppermute | solution.py:442
  247.7 21.6 %collective-permute-start.19 = (bf16[256,512]{1,0:T(8,128)(2,1)S(1)}, bf16[256,512]{1,0:T(8,128)(2,1)S(1)}, u32[]{:S(2)}, u32[]{:S(2)}) collective-permute-start(bf16[256,512]{1,0:T(8,128)(2,1)S(1)} %copy-done.11), channel_id=1, source_target_pairs={{0,3},{1,0},{2,1},{3,2},{4,7},{5,4},{6,5},{7,6},{8,11},{9,8},{10,9... | collective-permute-start | bytes 786440 | tf_op jit(solution)/shard_map/ppermute | solution.py:442
  250.5 18.8 %collective-permute-start.22 = (bf16[256,512]{1,0:T(8,128)(2,1)S(1)}, bf16[256,512]{1,0:T(8,128)(2,1)S(1)}, u32[]{:S(2)}, u32[]{:S(2)}) collective-permute-start(bf16[256,512]{1,0:T(8,128)(2,1)S(1)} %collective-permute-done.21.refs_5_), channel_id=1, source_target_pairs={{0,1},{1,2},{2,3},{3,0},{4,5},{5,6},{6,7},{7,4},{8,9},{9,10},{10,1... | collective-permute-start | bytes 786440 | tf_op jit(solution)/shard_map/ppermute | solution.py:443
  252.6 16.8 %collective-permute-start.23 = (bf16[256,512]{1,0:T(8,128)(2,1)S(1)}, bf16[256,512]{1,0:T(8,128)(2,1)}, u32[]{:S(2)}, u32[]{:S(2)}) collective-permute-start(bf16[256,512]{1,0:T(8,128)(2,1)S(1)} %collective-permute-done.21.refs_5_), channel_id=1, source_target_pairs={{0,3},{1,0},{2,1},{3,2},{4,7},{5,4},{6,5},{7,6},{8,11},{9,8},{10,9... | collective-permute-start | bytes 786440 | tf_op jit(solution)/shard_map/ppermute | solution.py:443
  256.3 13.1 %collective-permute-start.24 = (bf16[256,512]{1,0:T(8,128)(2,1)S(1)}, bf16[256,512]{1,0:T(8,128)(2,1)}, u32[]{:S(2)}, u32[]{:S(2)}) collective-permute-start(bf16[256,512]{1,0:T(8,128)(2,1)S(1)} %collective-permute-done.20.refs_4_), channel_id=1, source_target_pairs={{0,4},{4,0},{1,5},{5,1},{2,6},{6,2},{3,7},{7,3},{8,12},{12,8},{9,1... | collective-permute-start | bytes 786440 | tf_op jit(solution)/shard_map/ppermute | solution.py:444
  (30 other events, 389.0 us)
Sparse Core Ops, SparseCore 0:
  12.5 92.2 all-gather.2
  151.7 80.3 all-gather.4
where the time goes:
time: 290 us; the launch traced here: 287 us
  waiting for transfers between devices  90.6 us (31%)
  starting transfers between devices  79.9 us (28%)
  Pallas kernels  70.9 us (24%)
  between operations  14.6 us (5%)
  local copies, waits for them, and re-layouts  14.3 us (5%)
  other arithmetic  12.9 us (4%)
  matrix products  3.91 us (1%)
    ppermute x1, waiting for transfers between devices, block(): other = lax.ppermute(sorted_tokens, 'zh', SWAP)  35.1 us
    pallas_call x2, Pallas kernels, attend(): pl.pallas_call(attend_body, grid_spec=pltpu.PrefetchScalarGridSpec(num_sc...  30.9 us
    ppermute x2, waiting for transfers between devices, ring(): high = lax.ppermute(high, 'x', PREV)  30.7 us
    ppermute x6, starting transfers between devices, block(): near = [own] + [lax.ppermute(own, 'x', s) for s in (NEXT, PREV, ACROSS)]  29.7 us
    pallas_call x2, Pallas kernels, mix(): pl.pallas_call(body, grid_spec=pltpu.PrefetchScalarGridSpec(num_scalar_pr...  20.2 us
    pallas_call x2, Pallas kernels, project(): pl.pallas_call(body, grid_spec=pltpu.PrefetchScalarGridSpec(num_scalar_pr...  19.9 us
    ppermute x3, waiting for transfers between devices, block(): lax.ppermute(kv, ('y', 'zl'), flipped(steps))  10.6 us
    ppermute x2, starting transfers between devices, block(): across = lax.ppermute(own, 'zh', SWAP)  10.4 us
  transfers between devices with their start and end apart: 34, of which 9 were waited for; matrix products, arithmetic and copies ran while one was open for 9% of the time, Pallas kernels for 18%

commit v1 on v0

--- a/solution.py
+++ b/solution.py
@@ -47,7 +47,7 @@
         for i in range(len(slots)):
             fetch(i).start()
 
-    for k in range(GROUPS // PER_STEP):
+    for k in range(buffer.shape[0] // PER_STEP):
 
         @pl.when(step == k)
         def _(k=k):
@@ -60,12 +60,18 @@
     return pl.BlockSpec(shape, lambda k, ids: (0,) * len(shape))
 
 
-def project_body(slots, queries, ids, *refs):
+def project_body(slots, steps, queries, partial, ids, *refs):
     pieces = refs[: len(slots)]
     refs = refs[len(slots) :]
     w_refs = refs[:PER_STEP]
-    inverse_ref, bias_ref, cos_ref, sin_ref, out_ref, tbuf, acc, sems = refs[PER_STEP:]
+    refs = refs[PER_STEP:]
     step = pl.program_id(0)
+    if partial == "first":
+        acc, tbuf, sems = refs
+    elif partial == "last":
+        before_ref, inverse_ref, bias_ref, cos_ref, sin_ref, out_ref, tbuf, acc, sems = refs
+    else:
+        inverse_ref, bias_ref, cos_ref, sin_ref, out_ref, tbuf, acc, sems = refs
     fetch_all(pieces, slots, tbuf, sems, step)
     half = FEAT // 2
     total = None
@@ -79,13 +85,16 @@
 
     @pl.when(step == 0)
     def _():
-        acc[...] = total
+        acc[...] = total if partial != "last" else total + before_ref[...]
 
     @pl.when(step > 0)
     def _():
         acc[...] += total
 
-    @pl.when(step == GROUPS // PER_STEP - 1)
+    if partial == "first":
+        return
+
+    @pl.when(step == steps - 1)
     def _():
         inverse = inverse_ref[...]
         cosine = cos_ref[...]
@@ -107,40 +116,53 @@
             out_ref[:, HD:] = head(1).astype(jnp.bfloat16)
 
 
-def w_spec(i, width, column):
-    return pl.BlockSpec((2, ROWS, width), lambda k, ids: (ids[k * PER_STEP + i], 0, column))
-
-
-def project(pieces, slots, ids, weights, inverse, bias, cosine, sines, queries):
+def w_spec(i, width, first=0):
+    def at(k, ids):
+        group = (k + first) * PER_STEP + i
+        return (ids[0, group], 0, ids[1, group], 0, 0)
+
+    return pl.BlockSpec((None, 2, None, ROWS, width), at)
+
+
+def project(pieces, slots, ids, weights, finish, queries, partial=None, before=None):
     width = HEADS * HD if queries else 2 * HD
-    column = 0 if queries else HEADS // 2
-    out_shape = (BLOCKS, HEADS * BLOCK, HD) if queries else (ROWS, 2 * HD)
+    groups = GROUPS if partial is None else GROUPS // 2
+    first = groups // PER_STEP if partial == "last" else 0
+    steps = groups // PER_STEP
+    dtype = jnp.bfloat16
+    if partial == "first":
+        out_shape, dtype = ((ROWS, width), jnp.float32)
+        extra, extra_specs = ((), [])
+    else:
+        out_shape = (BLOCKS, HEADS * BLOCK, HD) if queries else (ROWS, 2 * HD)
+        extra = finish if before is None else (before,) + finish
+        extra_specs = [] if before is None else [whole(ROWS, width)]
+        extra_specs += [whole(ROWS, 1), whole(1, width), whole(ROWS, HD), whole(ROWS, HD)]
+    scratch = [pltpu.VMEM((groups, ROWS, FEAT), jnp.bfloat16)]
+    if partial != "first":
+        scratch += [pltpu.VMEM((ROWS, width), jnp.float32)]
+    scratch += [pltpu.SemaphoreType.DMA((len(pieces),))]
 
     def body(*refs):
-        project_body(slots, queries, *refs)
+        project_body(slots, steps, queries, partial, *refs)
 
     return pl.pallas_call(
         body,
         grid_spec=pltpu.PrefetchScalarGridSpec(
             num_scalar_prefetch=1,
-            grid=(GROUPS // PER_STEP,),
+            grid=(steps,),
             in_specs=[pl.BlockSpec(memory_space=pl.ANY)] * len(pieces)
-            + [w_spec(i, width, column) for i in range(PER_STEP)]
-            + [whole(ROWS, 1), whole(1, width), whole(ROWS, HD), whole(ROWS, HD)],
+            + [w_spec(i, width, first) for i in range(PER_STEP)]
+            + extra_specs,
             out_specs=whole(*out_shape),
-            scratch_shapes=[
-                pltpu.VMEM((GROUPS, ROWS, FEAT), jnp.bfloat16),
-                pltpu.VMEM((ROWS, width), jnp.float32),
-                pltpu.SemaphoreType.DMA((len(pieces),)),
-            ],
-        ),
-        out_shape=jax.ShapeDtypeStruct(out_shape, jnp.bfloat16),
+            scratch_shapes=scratch,
+        ),
+        out_shape=jax.ShapeDtypeStruct(out_shape, dtype),
         compiler_params=pltpu.CompilerParams(dimension_semantics=("arbitrary",)),
         cost_estimate=pl.CostEstimate(
-            flops=2 * ROWS * MODEL * width, transcendentals=0, bytes_accessed=16 << 20
-        ),
-        name="project_queries" if queries else "project_keys",
-    )(ids, *pieces, *([weights] * PER_STEP), inverse, bias, cosine, sines)
+            flops=2 * ROWS * groups * FEAT * width, transcendentals=0, bytes_accessed=16 << 20
+        ),
+    )(ids, *pieces, *([weights] * PER_STEP), *extra)
 
 
 def attend_body(bounds, q_ref, qpos_ref, own_ref, other_ref, kpos_ref, out_ref, kv_ref, top, acc, sems):
@@ -299,7 +321,7 @@
             num_scalar_prefetch=1,
             grid=(GROUPS // PER_STEP,),
             in_specs=[pl.BlockSpec(memory_space=pl.ANY)] * len(pieces)
-            + [w_spec(i, 512, 0) for i in range(PER_STEP)]
+            + [w_spec(i, 512) for i in range(PER_STEP)]
             + [whole(ROWS, rows), whole(ROWS, FEAT)],
             out_specs=whole(ROWS, FEAT),
             scratch_shapes=[
@@ -329,14 +351,22 @@
     sorted_pos = jnp.sum(jnp.where(chosen, positions[None, :], 0), 1)
     sorted_tokens = jnp.dot(order, tokens, preferred_element_type=f32).astype(bf16)
 
-    w_cat = jnp.concatenate((w_query, w_key, w_value), 1)
-    gain = lax.dynamic_slice(norm_gain, (seq_at * ROWS,), (ROWS,))
-    w_cat = (w_cat.astype(f32) * gain[:, None]).astype(bf16)
-    width = w_cat.shape[1]
+    gain = lax.dynamic_slice(norm_gain, (seq_at * ROWS,), (ROWS,))[:, None]
+    w_kv = (jnp.concatenate((w_key, w_value), 1).astype(f32) * gain).astype(bf16)
+    w_q = (w_query.astype(f32) * gain).astype(bf16)
     pos_rows = jnp.stack([sorted_pos >> 7, sorted_pos & 127]).astype(bf16)
-    pos_rows = jnp.pad(pos_rows, ((0, POS_ROWS - 2), (0, width - ROWS)))
-    weights = lax.all_gather(jnp.concatenate([w_cat, pos_rows], 0), SEQ, axis=0, tiled=True)
-    weights = weights.reshape(SOURCES, ROWS + POS_ROWS, width)
+    pos_rows = jnp.pad(pos_rows.reshape(4, 2 * HD), ((0, POS_ROWS - 4), (0, 0)))
+    w_kv = jnp.concatenate([w_kv, pos_rows], 0)
+
+    def over_seq(own, flip):
+        both = jnp.concatenate([own, flip], 0)
+        whole_seq = lax.all_gather(both, ("y", "core"), axis=0, tiled=True)
+        return whole_seq.reshape((4, 2, 2) + own.shape)
+
+    kv_flip = lax.ppermute(w_kv, "zl", SWAP)
+    q_flip = lax.ppermute(w_q, "zl", SWAP)
+    w_kv_all = over_seq(w_kv, kv_flip)
+    w_q_all = over_seq(w_q, q_flip)
 
     def ring(own):
         half = own.shape[0] // 2
@@ -349,7 +379,10 @@
 
     other = lax.ppermute(sorted_tokens, "zh", SWAP)
     left, right, low, high = ring(sorted_tokens)
-    oleft, oright, olow, ohigh = ring(other)
+    oleft = lax.ppermute(other, "x", NEXT)
+    oright = lax.ppermute(other, "x", PREV)
+    olow = lax.ppermute(low, "zh", SWAP)
+    ohigh = lax.ppermute(high, "zh", SWAP)
 
     def square(piece):
         wide = piece.astype(f32)
@@ -359,24 +392,12 @@
     total += jnp.concatenate([square(low), square(high)], 0)
     total += jnp.concatenate([square(olow), square(ohigh)], 0)
     inverse = lax.rsqrt(total * (1.0 / MODEL) + NORM_EPS)
-    ids = jnp.stack(
-        [z * 4 + (x + d) % 4 for z in (zh, 1 - zh) for d in (0, 3, 1, 2)]
-    ).astype(jnp.int32)
-    ids = ids[jnp.array([0, 1, 2, 4, 3, 5, 6, 7])]
+    y, zl, core = (lax.axis_index("y"), lax.axis_index("zl"), lax.axis_index("core"))
+    groups = jnp.stack([z * 4 + (x + d) % 4 for z in (zh, 1 - zh) for d in (0, 3, 1, 2)])
+    ids = jnp.stack([groups // 2, (groups % 2) ^ zl]).astype(jnp.int32)
     half = ROWS // 2
-    pieces = [sorted_tokens, left, right, other, low, high, oleft, oright, olow, ohigh]
-    slots = [
-        (0, 0, ROWS),
-        (1, 0, ROWS),
-        (2, 0, ROWS),
-        (3, 0, ROWS),
-        (4, 0, half),
-        (4, half, half),
-        (5, 0, ROWS),
-        (6, 0, ROWS),
-        (7, 0, half),
-        (7, half, half),
-    ]
+    pieces = [sorted_tokens, left, right, low, high, other, oleft, oright, olow, ohigh]
+    slots = [(0, 0, ROWS), (1, 0, ROWS), (2, 0, ROWS), (3, 0, half), (3, half, half)]
 
     half_dim = HD // 2
     inv_freq = ROPE_BASE ** (-jnp.arange(half_dim, dtype=f32) * 2.0 / HD)
@@ -386,28 +407,9 @@
     cosine = jnp.concatenate([cosine, cosine], 1)
     sines = jnp.concatenate([-sines, sines], 1)
 
-    kv_bias = jnp.concatenate((b_key, b_value))[None, :]
-    kv = project(pieces, slots, ids, weights, inverse, kv_bias, cosine, sines, False)
-
-    def flipped(steps):
-        turn = dict(steps)
-        return [(a * 2 + b, turn[a] * 2 + 1 - b) for a in range(4) for b in range(2)]
-
-    found = [kv, lax.ppermute(kv, "zl", SWAP)]
-    found += [lax.ppermute(kv, "y", steps) for steps in (NEXT, PREV, ACROSS)]
-    found += [lax.ppermute(kv, ("y", "zl"), flipped(steps)) for steps in (NEXT, PREV, ACROSS)]
-    own_kv = jnp.stack(found)
-    other_kv = lax.ppermute(own_kv, "core", SWAP)
-    y, zl, core = (lax.axis_index("y"), lax.axis_index("zl"), lax.axis_index("core"))
-    chips = [y * 2 + zl, y * 2 + 1 - zl]
-    chips += [(y + d) % 4 * 2 + z for z in (zl, 1 - zl) for d in (3, 1, 2)]
-    sources = jnp.stack([chip * 2 + c for c in (core, 1 - core) for chip in chips])
-
-    queries = project(
-        pieces, slots, ids, weights, inverse, b_query[None, :], cosine, sines, True
-    )
-
-    pos_all = weights[:, ROWS : ROWS + 2, :ROWS].astype(jnp.int32)
+    chips = [(y, 0), (y, 1)] + [((y + d) % 4, f) for f in (0, 1) for d in (3, 1, 2)]
+    sources = jnp.stack([(a * 2 + c) * 2 + f for c in (core, 1 - core) for a, f in chips])
+    pos_all = w_kv_all[:, :, :, ROWS : ROWS + 4].astype(jnp.int32).reshape(SOURCES, 2, ROWS)
     pos_all = pos_all[:, 0] * 128 + pos_all[:, 1]
     picked = sources[:, None] == jnp.arange(SOURCES)[None, :]
     pos_all = jnp.sum(jnp.where(picked[:, :, None], pos_all[None], 0), 1)
@@ -421,17 +423,40 @@
     bounds = jnp.stack([full, need])
     qpos = jnp.tile(by_block[:, None, :], (1, HEADS, 1)).reshape(BLOCKS, HEADS * BLOCK, 1)
 
-    swap = [
-        ((a * 2 + c) * 8 + b, (b * 2 + c) * 8 + a)
-        for a in range(8)
-        for c in range(2)
-        for b in range(8)
-    ]
-    moved = lax.ppermute(w_out, SEQ + TENSOR, swap)
-    moved, other_kv = lax.optimization_barrier((moved, other_kv))
-    w_out_all = lax.all_gather(moved, SEQ, axis=0, tiled=True).reshape(SOURCES, 512, 512)
-
-    mix_ids = jnp.stack([z * 4 + (x + d) % 4 for z in (zh, 1 - zh) for d in (0, 3, 1, 2)])
+    kv_bias = jnp.concatenate((b_key, b_value))[None, :]
+    start = project(pieces[:5], slots, ids, w_kv_all, (), False, "first")
+    inverse, kpos, bounds, qpos, start = lax.optimization_barrier(
+        (inverse, kpos, bounds, qpos, start)
+    )
+    finish = (inverse, kv_bias, cosine, sines)
+    kv = project(pieces[5:], slots, ids, w_kv_all, finish, False, "last", start)
+
+    def flipped(steps):
+        turn = dict(steps)
+        return [(a * 2 + b, turn[a] * 2 + 1 - b) for a in range(4) for b in range(2)]
+
+    found = [kv, lax.ppermute(kv, "zl", SWAP)]
+    found += [lax.ppermute(kv, "y", steps) for steps in (NEXT, PREV, ACROSS)]
+    found += [lax.ppermute(kv, ("y", "zl"), flipped(steps)) for steps in (NEXT, PREV, ACROSS)]
+    own_kv = jnp.stack(found)
+    other_kv = lax.ppermute(own_kv, "core", SWAP)
+
+    finish = (inverse, b_query[None, :], cosine, sines)
+    both_slots = slots + [(slot + 4, at, size) for slot, at, size in slots]
+    queries = project(pieces, both_slots, ids, w_q_all, finish, True)
+
+    def homes(flip):
+        return [
+            ((a * 2 + c) * 8 + b, ((b ^ flip) * 2 + c) * 8 + a)
+            for a in range(8)
+            for c in range(2)
+            for b in range(8)
+        ]
+
+    moved = lax.ppermute(w_out, SEQ + TENSOR, homes(0))
+    moved_flip = lax.ppermute(w_out, SEQ + TENSOR, homes(1))
+    w_out_all = over_seq(moved, moved_flip)
+
     base = tokens
     contexts = []
     for first, count in CALLS:
@@ -444,7 +469,7 @@
         found = near + far + [lax.ppermute(near[3], "zh", SWAP)]
         last = first + count == BLOCKS
         rows = slice(first * BLOCK, (first + count) * BLOCK)
-        base = mix(found, mix_ids.astype(jnp.int32), w_out_all, back[:, rows], base, last)
+        base = mix(found, ids, w_out_all, back[:, rows], base, last)
     context = jnp.dot(back, jnp.concatenate(contexts, 0), preferred_element_type=f32).astype(bf16)
     return (base, context)
 

time: 290 us -> 341 us (1.18)
  waiting for transfers between devices: 90.6 us -> 142 us
  local copies, waits for them, and re-layouts: 14.3 us -> 9.07 us
  Pallas kernels: 70.9 us -> 74.9 us
    ppermute x1 -> x8, waiting for transfers between devices: 0.01 us -> 73.5 us  [the longest x1 38.5 us: block(): moved_flip = lax.ppermute(w_out, SEQ + TENSOR, homes(1))]
    ppermute x2 -> x1, waiting for transfers between devices: 30.7 us -> 0.01 us  [ring(): high = lax.ppermute(high, 'x', PREV)]
    ppermute x2 -> x1, waiting for transfers between devices: 0.01 us -> 28.5 us  [ring(): low = lax.ppermute(low, 'x', NEXT)]
    ppermute x6, starting transfers between devices: 29.7 us -> 7.19 us  [block(): near = [own] + [lax.ppermute(own, 'x', s) for s in (NEXT, PREV, ACROSS)]]
    ppermute x1, waiting for transfers between devices: 35.1 us -> 16.2 us  [block(): other = lax.ppermute(sorted_tokens, 'zh', SWAP)]
    ppermute x1 -> x8, starting transfers between devices: 0.68 us -> 17.6 us  [the longest x1 5.18 us: block(): oleft = lax.ppermute(other, 'x', NEXT)]
    ppermute x1, starting transfers between devices: 3.99 us -> 20.2 us  [block(): other = lax.ppermute(sorted_tokens, 'zh', SWAP)]
    ppermute x2, starting transfers between devices: 10.4 us -> 3 us  [block(): across = lax.ppermute(own, 'zh', SWAP)]
  transfers between devices with their start and end apart: 34 -> 38, of which waited for: 9 -> 15; matrix products, arithmetic and copies ran while one was open for 9% -> 7% of each run, Pallas kernels for 18% -> 19%
where the time goes in v1:
time: 341 us
  waiting for transfers between devices  142 us (42%)
  starting transfers between devices  80.6 us (24%)
  Pallas kernels  74.9 us (22%)
  other arithmetic  16.1 us (5%)
  between operations  14.3 us (4%)
  local copies, waits for them, and re-layouts  9.07 us (3%)
  matrix products  3.92 us (1%)
    ppermute x1, waiting for transfers between devices, block(): moved_flip = lax.ppermute(w_out, SEQ + TENSOR, homes(1))  38.5 us
    pallas_call x2, Pallas kernels, attend(): pl.pallas_call(attend_body, grid_spec=pltpu.PrefetchScalarGridSpec(num_sc...  30.8 us
    ppermute x1, waiting for transfers between devices, ring(): low = lax.ppermute(low, 'x', NEXT)  28.5 us
    pallas_call x3, Pallas kernels, project(): pl.pallas_call(body, grid_spec=pltpu.PrefetchScalarGridSpec(num_scalar_pr...  23.7 us
    pallas_call x2, Pallas kernels, mix(): pl.pallas_call(body, grid_spec=pltpu.PrefetchScalarGridSpec(num_scalar_pr...  20.4 us
    ppermute x1, starting transfers between devices, block(): other = lax.ppermute(sorted_tokens, 'zh', SWAP)  20.2 us
    ppermute x1, waiting for transfers between devices, block(): other = lax.ppermute(sorted_tokens, 'zh', SWAP)  16.2 us
    ppermute x1, waiting for transfers between devices, block(): q_flip = lax.ppermute(w_q, 'zl', SWAP)  11.3 us
  transfers between devices with their start and end apart: 38, of which 15 were waited for; matrix products, arithmetic and copies ran while one was open for 7% of the time, Pallas kernels for 19%

profile of v1, /device:TPU:0, one launch (start us, length us, event | category | flops | bytes accessed | tf_op | source)
XLA Modules:
  0.0 340.6 jit_solution(1659050631055448728)
XLA Ops:
  13.2 6.5 %collective-permute-done.9 = bf16[528,256]{1,0:T(8,128)(2,1)S(1)} collective-permute-done((bf16[528,256]{1,0:T(8,128)(2,1)S(1)}, bf16[528,256]{1,0:T(8,128)(2,1)S(1)}, u32[]{:S(2)}, u32[]{:S(2)}) %collective-permute-start.9) | collective-permute-done | bytes 270368 | tf_op jit(solution)/shard_map/ppermute | solution.py:366
  22.6 11.3 %collective-permute-done.10 = bf16[512,512]{1,0:T(8,128)(2,1)S(1)} collective-permute-done((bf16[512,512]{1,0:T(8,128)(2,1)S(1)}, bf16[512,512]{1,0:T(8,128)(2,1)S(1)}, u32[]{:S(2)}, u32[]{:S(2)}) %collective-permute-start.10) | collective-permute-done | bytes 524320 | tf_op jit(solution)/shard_map/ppermute | solution.py:367
  35.9 4.1 %collective-permute-start.27 = (bf16[512,512]{1,0:T(8,128)(2,1)S(1)}, bf16[512,512]{1,0:T(8,128)(2,1)S(1)}, u32[]{:S(2)}, u32[]{:S(2)}) collective-permute-start(bf16[512,512]{1,0:T(8,128)(2,1)S(1)} %copy-done.25), channel_id=1, source_target_pairs={{0,16},{1,0},{2,48},{3,32},{4,80},{5,64},{6,112},{7,96},{8,24},{9,... | collective-permute-start | bytes 1572872 | tf_op jit(solution)/shard_map/ppermute | solution.py:457
  40.0 38.5 %collective-permute-done.27 = bf16[512,512]{1,0:T(8,128)(2,1)S(1)} collective-permute-done((bf16[512,512]{1,0:T(8,128)(2,1)S(1)}, bf16[512,512]{1,0:T(8,128)(2,1)S(1)}, u32[]{:S(2)}, u32[]{:S(2)}) %collective-permute-start.27) | collective-permute-done | bytes 524320 | tf_op jit(solution)/shard_map/ppermute | solution.py:457
  81.4 20.2 %collective-permute-start.2 = (bf16[512,1024]{1,0:T(8,128)(2,1)}, bf16[512,1024]{1,0:T(8,128)(2,1)S(1)}, u32[]{:S(2)}, u32[]{:S(2)}) collective-permute-start(bf16[512,1024]{1,0:T(8,128)(2,1)} %get-tuple-element.29.refs_1_), channel_id=1, source_target_pairs={{0,4},{4,0},{1,5},{5,1},{2,6},{6,2},{3,7},{7,3},{8,12},{12,8},{9,1... | collective-permute-start | bytes 3145736 | tf_op jit(solution)/shard_map/ppermute | solution.py:380
  101.6 4.8 %collective-permute-start = (bf16[512,1024]{1,0:T(8,128)(2,1)}, bf16[512,1024]{1,0:T(8,128)(2,1)S(1)}, u32[]{:S(2)}, u32[]{:S(2)}) collective-permute-start(bf16[512,1024]{1,0:T(8,128)(2,1)} %get-tuple-element.29.refs_1_), channel_id=1, source_target_pairs={{0,1},{1,2},{2,3},{3,0},{4,5},{5,6},{6,7},{7,4},{8,9},{9,10},{10,1... | collective-permute-start | bytes 3145736 | tf_op jit(solution)/shard_map/ppermute | solution.py:373
  108.7 16.2 %collective-permute-done.2.refs_6_.refs_1_ = bf16[512,1024]{1,0:T(8,128)(2,1)S(1)} collective-permute-done((bf16[512,1024]{1,0:T(8,128)(2,1)}, bf16[512,1024]{1,0:T(8,128)(2,1)S(1)}, u32[]{:S(2)}, u32[]{:S(2)}) %collective-permute-start.2) | collective-permute-done | bytes 1048608 | tf_op jit(solution)/shard_map/ppermute | solution.py:380
  125.8 5.2 %collective-permute-start.3 = (bf16[512,1024]{1,0:T(8,128)(2,1)S(1)}, bf16[512,1024]{1,0:T(8,128)(2,1)S(1)}, u32[]{:S(2)}, u32[]{:S(2)}) collective-permute-start(bf16[512,1024]{1,0:T(8,128)(2,1)S(1)} %collective-permute-done.2.refs_6_.refs_1_), channel_id=1, source_target_pairs={{0,1},{1,2},{2,3},{3,0},{4,5},{5,6},{6,7},{7,4},{8,9},{9,10},{10,1... | collective-permute-start | bytes 3145736 | tf_op jit(solution)/shard_map/ppermute | solution.py:382
  135.8 28.5 %collective-permute-done.5.refs_4_ = bf16[256,1024]{1,0:T(8,128)(2,1)} collective-permute-done((bf16[256,1024]{1,0:T(8,128)(2,1)S(1)}, bf16[256,1024]{1,0:T(8,128)(2,1)}, u32[]{:S(2)}, u32[]{:S(2)}) %collective-permute-start.5) | collective-permute-done | bytes 524320 | tf_op jit(solution)/shard_map/ppermute | solution.py:376
  164.3 3.1 collective-permute-start.7
  172.5 8.3 %collective-permute-done.7.refs_9_.refs_4_ = bf16[256,1024]{1,0:T(8,128)(2,1)S(1)} collective-permute-done((bf16[256,1024]{1,0:T(8,128)(2,1)}, bf16[256,1024]{1,0:T(8,128)(2,1)S(1)}, u32[]{:S(2)}, u32[]{:S(2)}) %collective-permute-start.7) | collective-permute-done | bytes 524320 | tf_op jit(solution)/shard_map/ppermute | solution.py:384
  181.0 8.8 %collective-permute-done.8.refs_10_.refs_5_ = bf16[256,1024]{1,0:T(8,128)(2,1)S(1)} collective-permute-done((bf16[256,1024]{1,0:T(8,128)(2,1)}, bf16[256,1024]{1,0:T(8,128)(2,1)S(1)}, u32[]{:S(2)}, u32[]{:S(2)}) %collective-permute-start.8) | collective-permute-done | bytes 524320 | tf_op jit(solution)/shard_map/ppermute | solution.py:385
  193.2 5.9 %shard_map.113.refs_8_ = f32[512,256]{1,0:T(8,128)} custom-call(s32[2,8]{1,0:T(2,128)} %pad_add_fusion.refs_0_, bf16[512,1024]{1,0:T(8,128)(2,1)} %get-tuple-element.29.refs_1_, bf16[512,1024]{1,0:T(8,128)(2,1)} %copy-done, bf16[512,1024]{1,0:T(8,128)(2,1)} %copy-done.1, bf16[256,1024]{1,0:T(8,128)(2,1)} %collective-permute-done.5.refs_4_, ...), custom_call_target="tpu_custom_call" | custom-call | flops 1073741824 | bytes 16777216 | tf_op jit(solution)/shard_map/pallas_call | solution.py:149
  199.4 6.6 %shard_map.115 = bf16[512,256]{1,0:T(8,128)(2,1)} custom-call(s32[2,8]{1,0:T(2,128)} %pad_add_fusion.refs_0_, bf16[512,1024]{1,0:T(8,128)(2,1)} %copy-done.2, bf16[512,1024]{1,0:T(8,128)(2,1)} %copy-done.4, bf16[512,1024]{1,0:T(8,128)(2,1)} %copy-done.3, bf16[256,1024]{1,0:T(8,128)(2,1)} %copy-done.5, bf16[256,1024]{1,0:T(8,128)(2,1)} %copy-done.6, ...), custom_call_target="tpu_custom_call" | custom-call | flops 1073741824 | bytes 16777216 | tf_op jit(solution)/shard_map/pallas_call | solution.py:149
  208.0 3.5 %collective-permute-start.12 = (bf16[512,256]{1,0:T(8,128)(2,1)}, bf16[512,256]{1,0:T(8,128)(2,1)S(1)}, u32[]{:S(2)}, u32[]{:S(2)}) collective-permute-start(bf16[512,256]{1,0:T(8,128)(2,1)} %shard_map.115), channel_id=1, source_target_pairs={{0,32},{32,64},{64,96},{96,0},{1,33},{33,65},{65,97},{97,1},{2,34}... | collective-permute-start | bytes 786440 | tf_op jit(solution)/shard_map/ppermute | solution.py:439
  212.4 2.6 collective-permute-start.13
  216.5 2.7 collective-permute-start.15
  220.7 2.3 collective-permute-done.12
  223.8 3.3 collective-permute-done.13
  228.5 7.8 %collective-permute-done.15 = bf16[512,256]{1,0:T(8,128)(2,1)S(1)} collective-permute-done((bf16[512,256]{1,0:T(8,128)(2,1)}, bf16[512,256]{1,0:T(8,128)(2,1)S(1)}, u32[]{:S(2)}, u32[]{:S(2)}) %collective-permute-start.15) | collective-permute-done | bytes 262176 | tf_op jit(solution)/shard_map/ppermute | solution.py:440
  241.5 11.2 %shard_map.114.q_ref = bf16[4,512,128]{2,1,0:T(8,128)(2,1)} custom-call(s32[2,8]{1,0:T(2,128)} %pad_add_fusion.refs_0_, bf16[512,1024]{1,0:T(8,128)(2,1)} %get-tuple-element.29.refs_1_, bf16[512,1024]{1,0:T(8,128)(2,1)} %copy-done, bf16[512,1024]{1,0:T(8,128)(2,1)} %copy-done.1, bf16[256,1024]{1,0:T(8,128)(2,1)} %collective-permute-done.5.refs_4_, ...), custom_call_target="tpu_custom_call" | custom-call | flops 4294967296 | bytes 16777216 | tf_op jit(solution)/shard_map/pallas_call | solution.py:149
  252.7 12.3 %shard_map.117.refs_1_ = bf16[256,512]{1,0:T(8,128)(2,1)} custom-call(s32[2,2]{1,0:T(2,128)} %get-tuple-element.24.bounds, bf16[4,512,128]{2,1,0:T(8,128)(2,1)} %shard_map.114.q_ref, s32[4,512,1]{2,1,0:T(8,128)} %copy.44.qpos_ref, bf16[8,512,256]{2,1,0:T(8,128)(2,1)} %copy-done.22, bf16[8,512,256]{2,1,0:T(8,128)(2,1)} %collective-permute-done.18.other_ref, ...), custom_call_target="tpu_custom_call" | custom-call | flops 4294967296 | bytes 6291456 | tf_op jit(solution)/shard_map/pallas_call | solution.py:243
  268.0 2.6 collective-permute-start.29
  270.6 18.5 %shard_map.116.refs_1_ = bf16[256,512]{1,0:T(8,128)(2,1)} custom-call(s32[2,2]{1,0:T(2,128)} %get-tuple-element.25.bounds, bf16[4,512,128]{2,1,0:T(8,128)(2,1)} %shard_map.114.q_ref, s32[4,512,1]{2,1,0:T(8,128)} %copy.44.qpos_ref, bf16[8,512,256]{2,1,0:T(8,128)(2,1)} %copy-done.22, bf16[8,512,256]{2,1,0:T(8,128)(2,1)} %collective-permute-done.18.other_ref, ...), custom_call_target="tpu_custom_call" | custom-call | flops 4294967296 | bytes 6291456 | tf_op jit(solution)/shard_map/pallas_call | solution.py:243
  290.5 2.3 collective-permute-start.21
  292.8 3.2 collective-permute-start.33
  298.7 2.8 collective-permute-done.21.refs_4_
  302.2 3.1 collective-permute-done.32.refs_6_
  305.3 2.5 collective-permute-start.23
  310.4 2.2 convolution_convert_fusion.1
  312.7 10.2 %mix_first.1.refs_12_ = f32[512,1024]{1,0:T(8,128)} custom-call(s32[2,8]{1,0:T(2,128)} %pad_add_fusion.refs_0_, bf16[256,512]{1,0:T(8,128)(2,1)} %shard_map.117.refs_1_, bf16[256,512]{1,0:T(8,128)(2,1)} %copy-done.14, bf16[256,512]{1,0:T(8,128)(2,1)} %copy-done.15, bf16[256,512]{1,0:T(8,128)(2,1)} %copy-done.13, bf16[256,512]{1,0:T(8,128)(2,1)} %copy-done.11, ...), custom_call_target="tpu_custom_call" | custom-call | flops 2147483648 | bytes 12582912 | tf_op jit(solution)/shard_map/mix_first/pallas_call | solution.py:318
  323.8 10.2 %mix_last.1 = bf16[512,1024]{1,0:T(8,128)(2,1)} custom-call(s32[2,8]{1,0:T(2,128)} %pad_add_fusion.refs_0_, bf16[256,512]{1,0:T(8,128)(2,1)} %shard_map.116.refs_1_, bf16[256,512]{1,0:T(8,128)(2,1)} %copy-done.16, bf16[256,512]{1,0:T(8,128)(2,1)} %copy-done.18, bf16[256,512]{1,0:T(8,128)(2,1)} %copy-done.12, bf16[256,512]{1,0:T(8,128)(2,1)} %copy-done.10, ...), custom_call_target="tpu_custom_call" | custom-call | flops 2147483648 | bytes 12582912 | tf_op jit(solution)/shard_map/mix_last/pallas_call | solution.py:318
  (178 shorter events, 54.9 us)
Async XLA Ops:
  7.2 183.7 %all-gather.4.cloned.1.call-start = ((), (), s32[]{:S(2)}) async-start(), calls=%async_computation | async-start | bytes 4866048 | tf_op jit(solution)/shard_map/all_gather | solution.py:363
  20.5 220.9 %all-gather.6.cloned.1.call-start = ((), (), s32[]{:S(2)}) async-start(), calls=%async_computation.1 | async-start | bytes 9437184 | tf_op jit(solution)/shard_map/all_gather | solution.py:363
  20.8 13.2 %collective-permute-start.10 = (bf16[512,512]{1,0:T(8,128)(2,1)S(1)}, bf16[512,512]{1,0:T(8,128)(2,1)S(1)}, u32[]{:S(2)}, u32[]{:S(2)}) collective-permute-start(bf16[512,512]{1,0:T(8,128)(2,1)S(1)} %multiply_convert_fusion), channel_id=1, source_target_pairs={{0,16},{16,0},{1,17},{17,1},{2,18},{18,2},{3,19},{19,3},{4,20},{20... | collective-permute-start | bytes 1572872 | tf_op jit(solution)/shard_map/ppermute | solution.py:367
  35.0 277.6 %all-gather.8.cloned.1.call-start = ((), (), s32[]{:S(2)}) async-start(), calls=%async_computation.2 | async-start | bytes 9437184 | tf_op jit(solution)/shard_map/all_gather | solution.py:363
  35.9 42.6 %collective-permute-start.27 = (bf16[512,512]{1,0:T(8,128)(2,1)S(1)}, bf16[512,512]{1,0:T(8,128)(2,1)S(1)}, u32[]{:S(2)}, u32[]{:S(2)}) collective-permute-start(bf16[512,512]{1,0:T(8,128)(2,1)S(1)} %copy-done.25), channel_id=1, source_target_pairs={{0,16},{1,0},{2,48},{3,32},{4,80},{5,64},{6,112},{7,96},{8,24},{9,... | collective-permute-start | bytes 1572872 | tf_op jit(solution)/shard_map/ppermute | solution.py:457
  81.4 43.6 %collective-permute-start.2 = (bf16[512,1024]{1,0:T(8,128)(2,1)}, bf16[512,1024]{1,0:T(8,128)(2,1)S(1)}, u32[]{:S(2)}, u32[]{:S(2)}) collective-permute-start(bf16[512,1024]{1,0:T(8,128)(2,1)} %get-tuple-element.29.refs_1_), channel_id=1, source_target_pairs={{0,4},{4,0},{1,5},{5,1},{2,6},{6,2},{3,7},{7,3},{8,12},{12,8},{9,1... | collective-permute-start | bytes 3145736 | tf_op jit(solution)/shard_map/ppermute | solution.py:380
  101.6 29.9 %collective-permute-start = (bf16[512,1024]{1,0:T(8,128)(2,1)}, bf16[512,1024]{1,0:T(8,128)(2,1)S(1)}, u32[]{:S(2)}, u32[]{:S(2)}) collective-permute-start(bf16[512,1024]{1,0:T(8,128)(2,1)} %get-tuple-element.29.refs_1_), channel_id=1, source_target_pairs={{0,1},{1,2},{2,3},{3,0},{4,5},{5,6},{6,7},{7,4},{8,9},{9,10},{10,1... | collective-permute-start | bytes 3145736 | tf_op jit(solution)/shard_map/ppermute | solution.py:373
  106.4 27.2 %collective-permute-start.1 = (bf16[512,1024]{1,0:T(8,128)(2,1)}, bf16[512,1024]{1,0:T(8,128)(2,1)S(1)}, u32[]{:S(2)}, u32[]{:S(2)}) collective-permute-start(bf16[512,1024]{1,0:T(8,128)(2,1)} %get-tuple-element.29.refs_1_), channel_id=1, source_target_pairs={{0,3},{1,0},{2,1},{3,2},{4,7},{5,4},{6,5},{7,6},{8,11},{9,8},{10,9... | collective-permute-start | bytes 3145736 | tf_op jit(solution)/shard_map/ppermute | solution.py:374
  124.9 45.4 %collective-permute-start.4 = (bf16[512,1024]{1,0:T(8,128)(2,1)S(1)}, bf16[512,1024]{1,0:T(8,128)(2,1)S(1)}, u32[]{:S(2)}, u32[]{:S(2)}) collective-permute-start(bf16[512,1024]{1,0:T(8,128)(2,1)S(1)} %collective-permute-done.2.refs_6_.refs_1_), channel_id=1, source_target_pairs={{0,3},{1,0},{2,1},{3,2},{4,7},{5,4},{6,5},{7,6},{8,11},{9,8},{10,9... | collective-permute-start | bytes 3145736 | tf_op jit(solution)/shard_map/ppermute | solution.py:383
  125.8 44.9 %collective-permute-start.3 = (bf16[512,1024]{1,0:T(8,128)(2,1)S(1)}, bf16[512,1024]{1,0:T(8,128)(2,1)S(1)}, u32[]{:S(2)}, u32[]{:S(2)}) collective-permute-start(bf16[512,1024]{1,0:T(8,128)(2,1)S(1)} %collective-permute-done.2.refs_6_.refs_1_), channel_id=1, source_target_pairs={{0,1},{1,2},{2,3},{3,0},{4,5},{5,6},{6,7},{7,4},{8,9},{9,10},{10,1... | collective-permute-start | bytes 3145736 | tf_op jit(solution)/shard_map/ppermute | solution.py:382
  131.5 32.8 %collective-permute-start.5 = (bf16[256,1024]{1,0:T(8,128)(2,1)S(1)}, bf16[256,1024]{1,0:T(8,128)(2,1)}, u32[]{:S(2)}, u32[]{:S(2)}) collective-permute-start(bf16[256,1024]{1,0:T(8,128)(2,1)S(1)} %slice.44), channel_id=1, source_target_pairs={{0,1},{1,2},{2,3},{3,0},{4,5},{5,6},{6,7},{7,4},{8,9},{9,10},{10,1... | collective-permute-start | bytes 1572872 | tf_op jit(solution)/shard_map/ppermute | solution.py:376
  133.6 33.8 %collective-permute-start.6 = (bf16[256,1024]{1,0:T(8,128)(2,1)S(1)}, bf16[256,1024]{1,0:T(8,128)(2,1)}, u32[]{:S(2)}, u32[]{:S(2)}) collective-permute-start(bf16[256,1024]{1,0:T(8,128)(2,1)S(1)} %slice.45), channel_id=1, source_target_pairs={{0,3},{1,0},{2,1},{3,2},{4,7},{5,4},{6,5},{7,6},{8,11},{9,8},{10,9... | collective-permute-start | bytes 1572872 | tf_op jit(solution)/shard_map/ppermute | solution.py:377
  164.3 16.5 %collective-permute-start.7 = (bf16[256,1024]{1,0:T(8,128)(2,1)}, bf16[256,1024]{1,0:T(8,128)(2,1)S(1)}, u32[]{:S(2)}, u32[]{:S(2)}) collective-permute-start(bf16[256,1024]{1,0:T(8,128)(2,1)} %collective-permute-done.5.refs_4_), channel_id=1, source_target_pairs={{0,4},{4,0},{1,5},{5,1},{2,6},{6,2},{3,7},{7,3},{8,12},{12,8},{9,1... | collective-permute-start | bytes 1572872 | tf_op jit(solution)/shard_map/ppermute | solution.py:384
  167.4 22.4 %collective-permute-start.8 = (bf16[256,1024]{1,0:T(8,128)(2,1)}, bf16[256,1024]{1,0:T(8,128)(2,1)S(1)}, u32[]{:S(2)}, u32[]{:S(2)}) collective-permute-start(bf16[256,1024]{1,0:T(8,128)(2,1)} %collective-permute-done.6.refs_5_), channel_id=1, source_target_pairs={{0,4},{4,0},{1,5},{5,1},{2,6},{6,2},{3,7},{7,3},{8,12},{12,8},{9,1... | collective-permute-start | bytes 1572872 | tf_op jit(solution)/shard_map/ppermute | solution.py:385
  206.0 13.2 %collective-permute-start.11 = (bf16[512,256]{1,0:T(8,128)(2,1)}, bf16[512,256]{1,0:T(8,128)(2,1)S(1)}, u32[]{:S(2)}, u32[]{:S(2)}) collective-permute-start(bf16[512,256]{1,0:T(8,128)(2,1)} %shard_map.115), channel_id=1, source_target_pairs={{0,16},{16,0},{1,17},{17,1},{2,18},{18,2},{3,19},{19,3},{4,20},{20... | collective-permute-start | bytes 786440 | tf_op jit(solution)/shard_map/ppermute | solution.py:438
  208.0 15.1 %collective-permute-start.12 = (bf16[512,256]{1,0:T(8,128)(2,1)}, bf16[512,256]{1,0:T(8,128)(2,1)S(1)}, u32[]{:S(2)}, u32[]{:S(2)}) collective-permute-start(bf16[512,256]{1,0:T(8,128)(2,1)} %shard_map.115), channel_id=1, source_target_pairs={{0,32},{32,64},{64,96},{96,0},{1,33},{33,65},{65,97},{97,1},{2,34}... | collective-permute-start | bytes 786440 | tf_op jit(solution)/shard_map/ppermute | solution.py:439
  212.4 14.7 %collective-permute-start.13 = (bf16[512,256]{1,0:T(8,128)(2,1)}, bf16[512,256]{1,0:T(8,128)(2,1)S(1)}, u32[]{:S(2)}, u32[]{:S(2)}) collective-permute-start(bf16[512,256]{1,0:T(8,128)(2,1)} %shard_map.115), channel_id=1, source_target_pairs={{0,96},{32,0},{64,32},{96,64},{1,97},{33,1},{65,33},{97,65},{2,98}... | collective-permute-start | bytes 786440 | tf_op jit(solution)/shard_map/ppermute | solution.py:439
  215.0 13.5 %collective-permute-start.14 = (bf16[512,256]{1,0:T(8,128)(2,1)}, bf16[512,256]{1,0:T(8,128)(2,1)S(1)}, u32[]{:S(2)}, u32[]{:S(2)}) collective-permute-start(bf16[512,256]{1,0:T(8,128)(2,1)} %shard_map.115), channel_id=1, source_target_pairs={{0,64},{32,96},{64,0},{96,32},{1,65},{33,97},{65,1},{97,33},{2,66}... | collective-permute-start | bytes 786440 | tf_op jit(solution)/shard_map/ppermute | solution.py:439
  216.5 19.7 %collective-permute-start.15 = (bf16[512,256]{1,0:T(8,128)(2,1)}, bf16[512,256]{1,0:T(8,128)(2,1)S(1)}, u32[]{:S(2)}, u32[]{:S(2)}) collective-permute-start(bf16[512,256]{1,0:T(8,128)(2,1)} %shard_map.115), channel_id=1, source_target_pairs={{0,48},{16,32},{32,80},{48,64},{64,112},{80,96},{96,16},{112,0},{1... | collective-permute-start | bytes 786440 | tf_op jit(solution)/shard_map/ppermute | solution.py:440
  219.3 17.8 %collective-permute-start.16 = (bf16[512,256]{1,0:T(8,128)(2,1)}, bf16[512,256]{1,0:T(8,128)(2,1)S(1)}, u32[]{:S(2)}, u32[]{:S(2)}) collective-permute-start(bf16[512,256]{1,0:T(8,128)(2,1)} %shard_map.115), channel_id=1, source_target_pairs={{0,112},{16,96},{32,16},{48,0},{64,48},{80,32},{96,80},{112,64},{1... | collective-permute-start | bytes 786440 | tf_op jit(solution)/shard_map/ppermute | solution.py:440
  223.0 16.1 %collective-permute-start.17 = (bf16[512,256]{1,0:T(8,128)(2,1)}, bf16[512,256]{1,0:T(8,128)(2,1)S(1)}, u32[]{:S(2)}, u32[]{:S(2)}) collective-permute-start(bf16[512,256]{1,0:T(8,128)(2,1)} %shard_map.115), channel_id=1, source_target_pairs={{0,80},{16,64},{32,112},{48,96},{64,16},{80,0},{96,48},{112,32},{1... | collective-permute-start | bytes 786440 | tf_op jit(solution)/shard_map/ppermute | solution.py:440
  239.1 13.6 %collective-permute-start.18 = (bf16[8,512,256]{2,1,0:T(8,128)(2,1)S(1)}, bf16[8,512,256]{2,1,0:T(8,128)(2,1)}, u32[]{:S(2)}, u32[]{:S(2)}) collective-permute-start(bf16[8,512,256]{2,1,0:T(8,128)(2,1)S(1)} %bitcast_dynamic-update-slice_fusion.own_ref), channel_id=1, source_target_pairs={{0,8},{8,0},{1,9},{9,1},{2,10},{10,2},{3,11},{11,3},{4,12},{12,4},... | collective-permute-start | bytes 6291464 | tf_op jit(solution)/shard_map/ppermute | solution.py:442
  265.0 25.5 %collective-permute-start.31 = (bf16[256,512]{1,0:T(8,128)(2,1)}, bf16[256,512]{1,0:T(8,128)(2,1)S(1)}, u32[]{:S(2)}, u32[]{:S(2)}) collective-permute-start(bf16[256,512]{1,0:T(8,128)(2,1)} %shard_map.117.refs_1_), channel_id=1, source_target_pairs={{0,4},{4,0},{1,5},{5,1},{2,6},{6,2},{3,7},{7,3},{8,12},{12,8},{9,1... | collective-permute-start | bytes 786440 | tf_op jit(solution)/shard_map/ppermute | solution.py:466
  266.6 26.2 %collective-permute-start.30 = (bf16[256,512]{1,0:T(8,128)(2,1)}, bf16[256,512]{1,0:T(8,128)(2,1)S(1)}, u32[]{:S(2)}, u32[]{:S(2)}) collective-permute-start(bf16[256,512]{1,0:T(8,128)(2,1)} %shard_map.117.refs_1_), channel_id=1, source_target_pairs={{0,2},{1,3},{2,0},{3,1},{4,6},{5,7},{6,4},{7,5},{8,10},{9,11},{10,... | collective-permute-start | bytes 786440 | tf_op jit(solution)/shard_map/ppermute | solution.py:467
  267.3 25.5 %collective-permute-start.28 = (bf16[256,512]{1,0:T(8,128)(2,1)}, bf16[256,512]{1,0:T(8,128)(2,1)S(1)}, u32[]{:S(2)}, u32[]{:S(2)}) collective-permute-start(bf16[256,512]{1,0:T(8,128)(2,1)} %shard_map.117.refs_1_), channel_id=1, source_target_pairs={{0,1},{1,2},{2,3},{3,0},{4,5},{5,6},{6,7},{7,4},{8,9},{9,10},{10,1... | collective-permute-start | bytes 786440 | tf_op jit(solution)/shard_map/ppermute | solution.py:467
  268.0 28.1 %collective-permute-start.29 = (bf16[256,512]{1,0:T(8,128)(2,1)}, bf16[256,512]{1,0:T(8,128)(2,1)S(1)}, u32[]{:S(2)}, u32[]{:S(2)}) collective-permute-start(bf16[256,512]{1,0:T(8,128)(2,1)} %shard_map.117.refs_1_), channel_id=1, source_target_pairs={{0,3},{1,0},{2,1},{3,2},{4,7},{5,4},{6,5},{7,6},{8,11},{9,8},{10,9... | collective-permute-start | bytes 786440 | tf_op jit(solution)/shard_map/ppermute | solution.py:467
  292.8 15.0 %collective-permute-start.33 = (bf16[256,512]{1,0:T(8,128)(2,1)S(1)}, bf16[256,512]{1,0:T(8,128)(2,1)S(1)}, u32[]{:S(2)}, u32[]{:S(2)}) collective-permute-start(bf16[256,512]{1,0:T(8,128)(2,1)S(1)} %collective-permute-done.31.refs_5_), channel_id=1, source_target_pairs={{0,3},{1,0},{2,1},{3,2},{4,7},{5,4},{6,5},{7,6},{8,11},{9,8},{10,9... | collective-permute-start | bytes 786440 | tf_op jit(solution)/shard_map/ppermute | solution.py:468
  298.5 24.4 %collective-permute-start.19 = (bf16[256,512]{1,0:T(8,128)(2,1)}, bf16[256,512]{1,0:T(8,128)(2,1)S(1)}, u32[]{:S(2)}, u32[]{:S(2)}) collective-permute-start(bf16[256,512]{1,0:T(8,128)(2,1)} %shard_map.116.refs_1_), channel_id=1, source_target_pairs={{0,1},{1,2},{2,3},{3,0},{4,5},{5,6},{6,7},{7,4},{8,9},{9,10},{10,1... | collective-permute-start | bytes 786440 | tf_op jit(solution)/shard_map/ppermute | solution.py:467
  301.5 21.5 %collective-permute-start.20 = (bf16[256,512]{1,0:T(8,128)(2,1)}, bf16[256,512]{1,0:T(8,128)(2,1)S(1)}, u32[]{:S(2)}, u32[]{:S(2)}) collective-permute-start(bf16[256,512]{1,0:T(8,128)(2,1)} %shard_map.116.refs_1_), channel_id=1, source_target_pairs={{0,3},{1,0},{2,1},{3,2},{4,7},{5,4},{6,5},{7,6},{8,11},{9,8},{10,9... | collective-permute-start | bytes 786440 | tf_op jit(solution)/shard_map/ppermute | solution.py:467
  305.3 17.7 %collective-permute-start.23 = (bf16[256,512]{1,0:T(8,128)(2,1)S(1)}, bf16[256,512]{1,0:T(8,128)(2,1)S(1)}, u32[]{:S(2)}, u32[]{:S(2)}) collective-permute-start(bf16[256,512]{1,0:T(8,128)(2,1)S(1)} %collective-permute-done.22.refs_5_), channel_id=1, source_target_pairs={{0,1},{1,2},{2,3},{3,0},{4,5},{5,6},{6,7},{7,4},{8,9},{9,10},{10,1... | collective-permute-start | bytes 786440 | tf_op jit(solution)/shard_map/ppermute | solution.py:468
  307.8 15.2 %collective-permute-start.24 = (bf16[256,512]{1,0:T(8,128)(2,1)S(1)}, bf16[256,512]{1,0:T(8,128)(2,1)}, u32[]{:S(2)}, u32[]{:S(2)}) collective-permute-start(bf16[256,512]{1,0:T(8,128)(2,1)S(1)} %collective-permute-done.22.refs_5_), channel_id=1, source_target_pairs={{0,3},{1,0},{2,1},{3,2},{4,7},{5,4},{6,5},{7,6},{8,11},{9,8},{10,9... | collective-permute-start | bytes 786440 | tf_op jit(solution)/shard_map/ppermute | solution.py:468
  308.6 14.4 %collective-permute-start.25 = (bf16[256,512]{1,0:T(8,128)(2,1)S(1)}, bf16[256,512]{1,0:T(8,128)(2,1)}, u32[]{:S(2)}, u32[]{:S(2)}) collective-permute-start(bf16[256,512]{1,0:T(8,128)(2,1)S(1)} %collective-permute-done.21.refs_4_), channel_id=1, source_target_pairs={{0,4},{4,0},{1,5},{5,1},{2,6},{6,2},{3,7},{7,3},{8,12},{12,8},{9,1... | collective-permute-start | bytes 786440 | tf_op jit(solution)/shard_map/ppermute | solution.py:469
  (32 other events, 477.2 us)
Sparse Core Ops, SparseCore 0:
  20.6 77.2 all-gather.3
  99.7 52.0 all-gather.5
  153.5 49.8 all-gather.7

commit v2 on v1

v2 whole, which is shorter than its diff:
```python
import math

import jax
import jax.numpy as jnp
from jax import lax
from jax.experimental import pallas as pl
from jax.experimental.pallas import tpu as pltpu
from jax.sharding import Mesh, PartitionSpec as P


HD = 128
NORM_EPS = 1e-06
ROPE_BASE = 1000000.0
NEG_FILL = -1e30
SEQ = ("y", "zl", "core")
TENSOR = ("zh", "x")
ROWS = 512
FEAT = 1024
MODEL = 8192
SOURCES = 16
GROUPS = 8
HEADS = 4
POS_ROWS = 16
KSTEP = 64
NSTEPS = ROWS // KSTEP
KEYS = SOURCES * KSTEP
BLOCK = 128
BLOCKS = ROWS // BLOCK
CALLS = ((0, 2), (2, 2))
PER_DOT = 1
QSCALE = HD**-0.5 * math.log2(math.e)


IN_ORDER = ("arbitrary",)
FIRST, LAST = (1, 2)
NEXT = [(i, (i + 1) % 4) for i in range(4)]
PREV = [(i, (i - 1) % 4) for i in range(4)]
ACROSS = [(i, (i + 2) % 4) for i in range(4)]
SWAP = [(0, 1), (1, 0)]


def whole(*shape):
    return pl.BlockSpec(shape, lambda k, ids: (0,) * len(shape))


def dots(ids, pieces, slots, w_ref, w_to, size, buffer, w_buffer, acc, sems, before=None):
    groups = buffer.shape[1] // size
    made = []
    for i, (slot, start, count) in enumerate(slots):
        to = buffer.at[pl.ds(start, count), pl.ds(slot * size, size)]
        made.append((slot, pltpu.make_async_copy(pieces[i], to, sems.at[i])))
    for g in range(groups):
        for c in range(2):
            source = w_ref.at[ids[0, g], c, ids[1, g], pl.ds(0, ROWS)]
            sem = sems.at[len(slots) + g * 2 + c]
            made.append((g, pltpu.make_async_copy(source, w_to(w_buffer, g, c), sem)))
    made.sort(key=lambda pair: pair[0])
    for _, copy in made:
        copy.start()
    for k in range(groups // PER_DOT):
        for slot, copy in made:
            if slot // PER_DOT == k:
                copy.wait()
        deep = slice(k * PER_DOT * size, (k + 1) * PER_DOT * size)
        part = jnp.dot(buffer[:, deep], w_buffer[deep, :], preferred_element_type=jnp.float32)
        if k == 0:
            acc[...] = part if before is None else part + before[...]
        else:
            acc[...] += part


def rows_to(w_buffer, g, c):
    return w_buffer.at[pl.ds((g * 2 + c) * ROWS, ROWS)]


def columns_to(w_buffer, g, c):
    return w_buffer.at[pl.ds(g * ROWS, ROWS), pl.ds(c * ROWS, ROWS)]


def project_body(slots, queries, partial, ids, *refs):
    pieces = refs[: len(slots)]
    w_ref = refs[len(slots)]
    refs = refs[len(slots) + 1 :]
    before = None
    if partial == FIRST:
        acc, buffer, w_buffer, sems = refs
    else:
        if partial == LAST:
            before, refs = (refs[0], refs[1:])
        inverse_ref, bias_ref, cos_ref, sin_ref, out_ref, buffer, w_buffer, acc, sems = refs
    dots(ids, pieces, slots, w_ref, rows_to, FEAT, buffer, w_buffer, acc, sems, before)
    if partial == FIRST:
        return
    inverse = inverse_ref[...]
    cosine = cos_ref[...]
    sines = sin_ref[...]

    def head(i):
        return acc[:, i * HD : (i + 1) * HD] * inverse + bias_ref[:, i * HD : (i + 1) * HD]

    def turned(u):
        return u * cosine + pltpu.roll(u, HD // 2, 1) * sines

    if queries:
        for i in range(HEADS):
            q = (turned(head(i)) * QSCALE).astype(jnp.bfloat16)
            for b in range(BLOCKS):
                out_ref[b, i * BLOCK : (i + 1) * BLOCK] = q[b * BLOCK : (b + 1) * BLOCK]
    else:
        out_ref[:, :HD] = turned(head(0)).astype(jnp.bfloat16)
        out_ref[:, HD:] = head(1).astype(jnp.bfloat16)


SCALARS = pl.BlockSpec(memory_space=pltpu.SMEM)
ANYWHERE = pl.BlockSpec(memory_space=pl.ANY)
NEAR = pl.BlockSpec(memory_space=pltpu.VMEM)


def project(pieces, slots, ids, weights, finish, queries, partial=None, before=None):
    width = HEADS * HD if queries else 2 * HD
    groups = GROUPS if partial is None else GROUPS // 2
    ids = ids[:, GROUPS - groups :] if partial == LAST else ids[:, :groups]
    dtype = jnp.bfloat16
    out_shape = (BLOCKS, HEADS * BLOCK, HD) if queries else (ROWS, 2 * HD)
    extra = finish if before is None else (before,) + finish
    scratch = [
        pltpu.VMEM((ROWS, groups * FEAT), jnp.bfloat16),
        pltpu.VMEM((groups * FEAT, width), jnp.bfloat16),
    ]
    if partial == FIRST:
        out_shape, dtype = ((ROWS, width), jnp.float32)
    else:
        scratch += [pltpu.VMEM((ROWS, width), jnp.float32)]
    scratch += [pltpu.SemaphoreType.DMA((len(pieces) + 2 * groups,))]

    def body(*refs):
        project_body(slots, queries, partial, *refs)

    return pl.pallas_call(
        body,
        in_specs=[SCALARS] + [ANYWHERE] * (len(pieces) + 1) + [NEAR] * len(extra),
        out_specs=NEAR,
        scratch_shapes=scratch,
        out_shape=jax.ShapeDtypeStruct(out_shape, dtype),
        cost_estimate=pl.CostEstimate(
            flops=2 * ROWS * groups * FEAT * width, transcendentals=0, bytes_accessed=16 << 20
        ),
        name="pq" if queries else ("pk0" if partial == FIRST else "pk1"),
    )(ids, *pieces, weights, *extra)


def attend_body(first, bounds, q_ref, qpos_ref, kpos_ref, *refs):
    pairs = refs[: SOURCES // 2]
    out_ref, kv_ref, top, acc, sems = refs[SOURCES // 2 :]
    block_at = pl.program_id(0)
    full = bounds[0, block_at]
    need = bounds[1, block_at]

    def fetch(i):
        return pltpu.make_async_copy(pairs[i], kv_ref.at[pl.ds(2 * i, 2)], sems.at[i])

    @pl.when(block_at == 0)
    def _():
        for i in range(len(pairs)):
            fetch(i).start()

    top[...] = jnp.full_like(top, NEG_FILL)
    acc[...] = jnp.zeros_like(acc)

    @pl.when(block_at == 0)
    def _():
        for i in range(len(pairs)):
            fetch(i).wait()

    ones = jnp.ones((KEYS, HD), jnp.bfloat16)
    parts = top.shape[0]
    rows = top.shape[1]

    def one_step(j, masked):
        at = pl.multiple_of(j * KSTEP, KSTEP)
        block = kv_ref[:, pl.ds(at, KSTEP), :].reshape(KEYS, 2 * HD)
        keys = block[:, :HD]
        values = jnp.concatenate([block[:, HD:], ones], axis=1)

        def scores_of(h):
            return lax.dot_general(
                q_ref[0, h * rows : (h + 1) * rows],
                keys,
                (((1,), (1,)), ((), ())),
                preferred_element_type=jnp.float32,
            )

        following = scores_of(0)
        for h in range(parts):
            scores = following
            following = scores_of(h + 1) if h + 1 < parts else None
            if masked:
                allowed = kpos_ref[j] <= qpos_ref[0, h * rows : (h + 1) * rows]
                scores = jnp.where(allowed, scores, NEG_FILL)
            old = top[h]
            new = jnp.maximum(old, jnp.max(scores, axis=1, keepdims=True))
            weights = jnp.exp2(scores - jnp.concatenate([new] * (KEYS // HD), axis=1))
            rescale = jnp.exp2(old - new)
            top[h] = new
            acc[h] = acc[h] * jnp.concatenate([rescale, rescale], axis=1) + jnp.dot(
                weights.astype(jnp.bfloat16), values, preferred_element_type=jnp.float32
            )

    def unmasked(j, carry):
        one_step(j, False)
        return carry

    def masked(j, carry):
        one_step(j, True)
        return carry

    if first == 0:
        lax.fori_loop(0, need, masked, 0)
    else:
        lax.fori_loop(0, full, unmasked, 0)
        lax.fori_loop(full, need, masked, 0)
    for h in range(HEADS):
        part, at = (h * BLOCK // rows, h * BLOCK % rows)
        done = acc[part, at : at + BLOCK, :HD] / acc[part, at : at + BLOCK, HD:]
        out_ref[:, h * HD : (h + 1) * HD] = done.astype(jnp.bfloat16)


def attend(bounds, queries, qpos, pairs, kpos, first, count):
    part = 2 * BLOCK

    def body(*refs):
        attend_body(first, *refs)

    return pl.pallas_call(
        body,
        grid_spec=pltpu.PrefetchScalarGridSpec(
            num_scalar_prefetch=1,
            grid=(count,),
            in_specs=[
                pl.BlockSpec((1, HEADS * BLOCK, HD), lambda c, b: (c + first, 0, 0)),
                pl.BlockSpec((1, HEADS * BLOCK, 1), lambda c, b: (c + first, 0, 0)),
                whole(NSTEPS, 1, KEYS),
            ]
            + [pl.BlockSpec(memory_space=pl.ANY)] * len(pairs),
            out_specs=pl.BlockSpec((BLOCK, HEADS * HD), lambda c, b: (c, 0)),
            scratch_shapes=[
                pltpu.VMEM((SOURCES, ROWS, 2 * HD), jnp.bfloat16),
                pltpu.VMEM((HEADS * BLOCK // part, part, HD), jnp.float32),
                pltpu.VMEM((HEADS * BLOCK // part, part, 2 * HD), jnp.float32),
                pltpu.SemaphoreType.DMA((len(pairs),)),
            ],
        ),
        out_shape=jax.ShapeDtypeStruct((BLOCK * count, HEADS * HD), jnp.bfloat16),
        compiler_params=pltpu.CompilerParams(dimension_semantics=IN_ORDER),
        cost_estimate=pl.CostEstimate(
            flops=4 * HEADS * BLOCK * count * SOURCES * ROWS * HD,
            transcendentals=HEADS * BLOCK * count * SOURCES * ROWS,
            bytes_accessed=6 << 20,
        ),
    )(bounds, queries, qpos, kpos, *pairs)


def mix_body(slots, ids, *refs):
    pieces = refs[: len(slots)]
    w_ref, back_ref, base_ref, out_ref, buffer, w_buffer, acc, sems = refs[len(slots) :]
    dots(ids, pieces, slots, w_ref, columns_to, ROWS, buffer, w_buffer, acc, sems)
    back = back_ref[...]
    high = acc[...].astype(jnp.bfloat16)
    low = (acc[...] - high.astype(jnp.float32)).astype(jnp.bfloat16)
    mixed = jnp.dot(back, high, preferred_element_type=jnp.float32) + jnp.dot(
        back, low, preferred_element_type=jnp.float32
    )
    out_ref[...] = (base_ref[...].astype(jnp.float32) + mixed).astype(out_ref.dtype)


def mix(pieces, ids, w_out, back, base, last):
    rows = pieces[0].shape[0]
    slots = [(i, 0, rows) for i in range(GROUPS)]

    def body(*refs):
        mix_body(slots, *refs)

    return pl.pallas_call(
        body,
        in_specs=[SCALARS] + [ANYWHERE] * (len(pieces) + 1) + [NEAR] * 2,
        out_specs=NEAR,
        scratch_shapes=[
            pltpu.VMEM((rows, GROUPS * ROWS), jnp.bfloat16),
            pltpu.VMEM((GROUPS * ROWS, FEAT), jnp.bfloat16),
            pltpu.VMEM((rows, FEAT), jnp.float32),
            pltpu.SemaphoreType.DMA((len(pieces) + 2 * GROUPS,)),
        ],
        out_shape=jax.ShapeDtypeStruct((ROWS, FEAT), jnp.bfloat16 if last else jnp.float32),
        cost_estimate=pl.CostEstimate(
            flops=2 * rows * HEADS * HD * GROUPS * FEAT, transcendentals=0, bytes_accessed=12 << 20
        ),
        name="m1" if last else "m0",
    )(ids, *pieces, w_out, back, base)


def block(tokens, positions, norm_gain, w_query, w_key, w_value, b_query, b_key, b_value, w_out):
    bf16, f32 = (jnp.bfloat16, jnp.float32)
    seq_at = lax.axis_index(SEQ)
    zh, x = (lax.axis_index("zh"), lax.axis_index("x"))

    spread = [
        (
            ((yy * 2 + zz) * 2 + hh) * 4 + xx,
            ((((yy % 2) * 2 + zz + xx) % 4 * 2 + hh) * 2 + yy // 2) * 4 + xx,
        )
        for yy in range(4)
        for zz in range(2)
        for hh in range(2)
        for xx in range(4)
    ]
    moved = lax.ppermute(w_out, ("y", "zl", "zh", "x"), spread)

    rank = jnp.sum((positions[None, :] < positions[:, None]).astype(jnp.int32), 1)
    chosen = rank[None, :] == jnp.arange(ROWS, dtype=jnp.int32)[:, None]
    order = chosen.astype(bf16)
    back = (rank[:, None] == jnp.arange(ROWS, dtype=jnp.int32)[None, :]).astype(bf16)
    sorted_pos = jnp.sum(jnp.where(chosen, positions[None, :], 0), 1)
    sorted_tokens = jnp.dot(order, tokens, preferred_element_type=f32).astype(bf16)

    gain = lax.dynamic_slice(norm_gain, (seq_at * ROWS,), (ROWS,))[:, None]
    w_kv = (jnp.concatenate((w_key, w_value), 1).astype(f32) * gain).astype(bf16)
    w_q = (w_query.astype(f32) * gain).astype(bf16)
    pos_rows = jnp.stack([sorted_pos >> 7, sorted_pos & 127]).astype(bf16)
    pos_rows = jnp.pad(pos_rows.reshape(4, 2 * HD), ((0, POS_ROWS - 4), (0, 0)))
    w_kv = jnp.concatenate([w_kv, pos_rows], 0)

    def over_seq(own, flip):
        both = jnp.concatenate([own, flip], 0)
        whole_seq = lax.all_gather(both, ("y", "core"), axis=0, tiled=True)
        return whole_seq.reshape((4, 2, 2) + own.shape)

    kv_flip = lax.ppermute(w_kv, "zl", SWAP)
    q_flip = lax.ppermute(w_q, "zl", SWAP)
    w_kv_all = over_seq(w_kv, kv_flip)
    w_q_all = over_seq(w_q, q_flip)

    def ring(own):
        half = own.shape[0] // 2
        left = lax.ppermute(own, "x", NEXT)
        right = lax.ppermute(own, "x", PREV)
        low, high = (left[:half], right[half:])
        low = lax.ppermute(low, "x", NEXT)
        high = lax.ppermute(high, "x", PREV)
        return left, right, low, high

    other = lax.ppermute(sorted_tokens, "zh", SWAP)
    left, right, low, high = ring(sorted_tokens)
    oleft, oright, olow, ohigh = ring(other)

    def square(piece):
        wide = piece.astype(f32)
        return jnp.sum(wide * wide, 1, keepdims=True)

    total = sum(square(p) for p in (sorted_tokens, left, right, other, oleft, oright))
    total_low, total_high = (square(low), square(high))
    total += jnp.concatenate([total_low, total_high], 0)
    total += jnp.concatenate([square(olow), square(ohigh)], 0)
    inverse = lax.rsqrt(total * (1.0 / MODEL) + NORM_EPS)
    y, zl, core = (lax.axis_index("y"), lax.axis_index("zl"), lax.axis_index("core"))
    groups = jnp.stack([z * 4 + (x + d) % 4 for z in (zh, 1 - zh) for d in (0, 3, 1, 2)])
    ids = jnp.stack([groups // 2, (groups % 2) ^ zl]).astype(jnp.int32)
    half = ROWS // 2
    pieces = [sorted_tokens, left, right, low, high, other, oleft, oright, olow, ohigh]
    slots = [(0, 0, ROWS), (1, 0, ROWS), (2, 0, ROWS), (3, 0, half), (3, half, half)]

    half_dim = HD // 2
    inv_freq = ROPE_BASE ** (-jnp.arange(half_dim, dtype=f32) * 2.0 / HD)
    angles = sorted_pos.astype(f32)[:, None] * inv_freq[None, :]
    cosine = jnp.cos(angles)
    sines = jnp.sin(angles)
    cosine = jnp.concatenate([cosine, cosine], 1)
    sines = jnp.concatenate([-sines, sines], 1)

    chips = [((y + d) % 4, f) for d in (0, 3, 1, 2) for f in (0, 1)]
    sources = jnp.stack([(a * 2 + c) * 2 + f for c in (core, 1 - core) for a, f in chips])
    pos_all = w_kv_all[:, :, :, ROWS : ROWS + 4].astype(jnp.int32).reshape(SOURCES, 2, ROWS)
    pos_all = pos_all[:, 0] * 128 + pos_all[:, 1]
    picked = sources[:, None] == jnp.arange(SOURCES)[None, :]
    pos_all = jnp.sum(jnp.where(picked[:, :, None], pos_all[None], 0), 1)
    kpos = pos_all.reshape(SOURCES, NSTEPS, KSTEP).transpose(1, 0, 2)
    first_pos = jnp.min(kpos, (1, 2))
    last_pos = jnp.max(kpos, (1, 2))
    kpos = kpos.reshape(NSTEPS, 1, KEYS)
    by_block = sorted_pos.reshape(BLOCKS, BLOCK)
    full = jnp.sum((last_pos[None, :] <= by_block[:, :1]).astype(jnp.int32), 1)
    need = jnp.sum((first_pos[None, :] <= by_block[:, -1:]).astype(jnp.int32), 1)
    bounds = jnp.stack([full, need])
    qpos = jnp.tile(by_block[:, None, :], (1, HEADS, 1)).reshape(BLOCKS, HEADS * BLOCK, 1)

    kv_bias = jnp.concatenate((b_key, b_value))[None, :]
    start = project(pieces[:5], slots, ids, w_kv_all, (), False, FIRST)
    inverse, kpos, bounds, qpos, start = lax.optimization_barrier(
        (inverse, kpos, bounds, qpos, start)
    )
    finish = (inverse, kv_bias, cosine, sines)
    kv = project(pieces[5:], slots, ids, w_kv_all, finish, False, LAST, start)

    pair = jnp.stack([kv, lax.ppermute(kv, "zl", SWAP)])
    own_kv = [pair] + [lax.ppermute(pair, "y", steps) for steps in (NEXT, PREV, ACROSS)]
    all_kv = own_kv + [lax.ppermute(a, "core", SWAP) for a in own_kv]

    finish = (inverse, b_query[None, :], cosine, sines)
    both_slots = slots + [(slot + 4, at, size) for slot, at, size in slots]
    queries = project(pieces, both_slots, ids, w_q_all, finish, True)

    mirrored = [
        ((yy * 4 + xx), (yy * 4 + (yy - xx) % 4)) for yy in range(4) for xx in range(4)
    ]
    moved = lax.ppermute(moved, ("y", "x"), mirrored)
    flip = lax.ppermute(moved, "zl", SWAP)
    moved, flip, _ = lax.optimization_barrier((moved, flip, all_kv[1:4]))
    w_out_all = over_seq(moved, flip)
    mix_ids = jnp.stack([(groups + x) % 4, (groups // 4) ^ zl]).astype(jnp.int32)

    base = tokens
    contexts, parts = ([], [])
    for first, count in CALLS:
        at = slice(first, first + count)
        parts.append(attend(bounds[:, at], queries, qpos, all_kv, kpos, first, count))
        if first + count == BLOCKS // 2 or first + count == BLOCKS:
            own = parts[0] if len(parts) == 1 else jnp.concatenate(parts, 0)
            contexts.append(own)
            parts = []
            last = first + count == BLOCKS
            half = BLOCKS // 2 if last else 0
            across = lax.ppermute(own, "zh", SWAP)
            near = [own] + [lax.ppermute(own, "x", s) for s in (NEXT, PREV, ACROSS)]
            far = [across] + [lax.ppermute(across, "x", s) for s in (NEXT, PREV)]
            found = near + far + [lax.ppermute(near[3], "zh", SWAP)]
            rows = slice(half * BLOCK, (first + count) * BLOCK)
            base = mix(found, mix_ids, w_out_all, back[:, rows], base, last)
    context = jnp.dot(back, jnp.concatenate(contexts, 0), preferred_element_type=f32).astype(bf16)
    return (base, context)


def solution(mesh):
    fine = Mesh(mesh.devices.reshape(4, 2, 2, 2, 4), SEQ + TENSOR)
    in_specs = (
        P(SEQ, TENSOR),
        P(SEQ),
        P(),
        P(SEQ, TENSOR),
        P(SEQ, TENSOR),
        P(SEQ, TENSOR),
        P(TENSOR),
        P(TENSOR),
        P(TENSOR),
        P(TENSOR, SEQ),
    )
    out_specs = (P(SEQ, TENSOR), P(SEQ, TENSOR))
    return jax.shard_map(block, mesh=fine, in_specs=in_specs, out_specs=out_specs, check_vma=False)
```

time: 341 us -> 281 us (0.82)
  waiting for transfers between devices: 142 us -> 104 us
  starting transfers between devices: 80.6 us -> 64.3 us
  Pallas kernels: 74.9 us -> 67.5 us
    ppermute x14 -> x11, waiting for transfers between devices: 73.2 us -> 21.4 us  [the longest x3 14.4 us: block(): lax.ppermute(pair, 'y', steps)]
    ppermute x1 -> x2, waiting for transfers between devices: 0.01 us -> 31 us  [ring(): high = lax.ppermute(high, 'x', PREV)]
    ppermute x1 -> x2, waiting for transfers between devices: 28.5 us -> 6.24 us  [ring(): low = lax.ppermute(low, 'x', NEXT)]
    ppermute x1, starting transfers between devices: 20.2 us -> 3.42 us  [block(): other = lax.ppermute(sorted_tokens, 'zh', SWAP)]
    ppermute x1, waiting for transfers between devices: 16.2 us -> 24.6 us  [block(): other = lax.ppermute(sorted_tokens, 'zh', SWAP)]
    ppermute x14 -> x11, starting transfers between devices: 28.1 us -> 20 us  [the longest x3 6.13 us: block(): lax.ppermute(pair, 'y', steps)]
    pallas_call x7, Pallas kernels: 74.9 us -> 67.5 us  [the longest x2 30.9 us: attend(): pl.pallas_call(body, grid_spec=pltpu.PrefetchScalarGridSpec(num_scalar_pr...]
    ppermute x1 -> x2, starting transfers between devices: 1.33 us -> 6.38 us  [ring(): high = lax.ppermute(high, 'x', PREV)]
  transfers between devices with their start and end apart: 38 -> 39, of which waited for: 15 -> 12; matrix products, arithmetic and copies ran while one was open for 7% -> 9% of each run, Pallas kernels for 19% -> 21%
where the time goes in v2:
time: 281 us; the launch traced here: 280 us
  waiting for transfers between devices  104 us (37%)
  Pallas kernels  67.5 us (24%)
  starting transfers between devices  64.3 us (23%)
  other arithmetic  17.4 us (6%)
  between operations  14.5 us (5%)
  local copies, waits for them, and re-layouts  8.09 us (3%)
  matrix products  3.92 us (1%)
    ppermute x2, waiting for transfers between devices, ring(): high = lax.ppermute(high, 'x', PREV)  31 us
    pallas_call x2, Pallas kernels, attend(): pl.pallas_call(body, grid_spec=pltpu.PrefetchScalarGridSpec(num_scalar_pr...  30.9 us
    ppermute x1, waiting for transfers between devices, block(): other = lax.ppermute(sorted_tokens, 'zh', SWAP)  24.6 us
    pallas_call x3, Pallas kernels, project(): pl.pallas_call(body, in_specs=[SCALARS] + [ANYWHERE] * (len(pieces) + 1)...  20.9 us
    pallas_call x2, Pallas kernels, mix(): pl.pallas_call(body, in_specs=[SCALARS] + [ANYWHERE] * (len(pieces) + 1)...  15.7 us
    ppermute x3, waiting for transfers between devices, block(): lax.ppermute(pair, 'y', steps)  14.4 us
    ppermute x1, waiting for transfers between devices, block(): q_flip = lax.ppermute(w_q, 'zl', SWAP)  11.3 us
    ppermute x6, starting transfers between devices, block(): near = [own] + [lax.ppermute(own, 'x', s) for s in (NEXT, PREV, ACROSS)]  9.89 us
  transfers between devices with their start and end apart: 39, of which 12 were waited for; matrix products, arithmetic and copies ran while one was open for 9% of the time, Pallas kernels for 21%

profile of v2, /device:TPU:0, one launch (start us, length us, event | category | flops | bytes accessed | tf_op | source)
XLA Modules:
  0.0 279.7 jit_solution(13408753037213744811)
XLA Ops:
  11.1 2.1 collective-permute-start.9
  13.2 6.5 %collective-permute-done.9 = bf16[528,256]{1,0:T(8,128)(2,1)S(1)} collective-permute-done((bf16[528,256]{1,0:T(8,128)(2,1)S(1)}, bf16[528,256]{1,0:T(8,128)(2,1)S(1)}, u32[]{:S(2)}, u32[]{:S(2)}) %collective-permute-start.9) | collective-permute-done | bytes 270368 | tf_op jit(solution)/shard_map/ppermute | solution.py:337
  22.6 11.3 %collective-permute-done.10 = bf16[512,512]{1,0:T(8,128)(2,1)S(1)} collective-permute-done((bf16[512,512]{1,0:T(8,128)(2,1)S(1)}, bf16[512,512]{1,0:T(8,128)(2,1)S(1)}, u32[]{:S(2)}, u32[]{:S(2)}) %collective-permute-start.10) | collective-permute-done | bytes 524320 | tf_op jit(solution)/shard_map/ppermute | solution.py:338
  40.0 3.4 %collective-permute-start.2 = (bf16[512,1024]{1,0:T(8,128)(2,1)}, bf16[512,1024]{1,0:T(8,128)(2,1)}, u32[]{:S(2)}, u32[]{:S(2)}) collective-permute-start(bf16[512,1024]{1,0:T(8,128)(2,1)} %get-tuple-element.37.refs_1_), channel_id=1, source_target_pairs={{0,4},{4,0},{1,5},{5,1},{2,6},{6,2},{3,7},{7,3},{8,12},{12,8},{9,1... | collective-permute-start | bytes 3145736 | tf_op jit(solution)/shard_map/ppermute | solution.py:351
  43.4 5.4 %collective-permute-start.26 = (bf16[512,512]{1,0:T(8,128)(2,1)}, bf16[512,512]{1,0:T(8,128)(2,1)}, u32[]{:S(2)}, u32[]{:S(2)}) collective-permute-start(bf16[512,512]{1,0:T(8,128)(2,1)} %param.19), channel_id=1, source_target_pairs={{0,0},{1,33},{2,66},{3,99},{4,16},{5,49},{6,82},{7,115},{16,32},{1... | collective-permute-start | bytes 1572872 | tf_op jit(solution)/shard_map/ppermute | solution.py:316
  51.4 24.6 %collective-permute-done.2.refs_6_.refs_1_ = bf16[512,1024]{1,0:T(8,128)(2,1)} collective-permute-done((bf16[512,1024]{1,0:T(8,128)(2,1)}, bf16[512,1024]{1,0:T(8,128)(2,1)}, u32[]{:S(2)}, u32[]{:S(2)}) %collective-permute-start.2) | collective-permute-done | bytes 1048608 | tf_op jit(solution)/shard_map/ppermute | solution.py:351
  79.2 5.3 %collective-permute-start.27 = (bf16[512,512]{1,0:T(8,128)(2,1)}, bf16[512,512]{1,0:T(8,128)(2,1)}, u32[]{:S(2)}, u32[]{:S(2)}) collective-permute-start(bf16[512,512]{1,0:T(8,128)(2,1)} %collective-permute-done.26), channel_id=1, source_target_pairs={{0,0},{1,3},{2,2},{3,1},{32,33},{33,32},{34,35},{35,34},{64,66},{6... | collective-permute-start | bytes 1572872 | tf_op jit(solution)/shard_map/ppermute | solution.py:414
  84.8 3.3 %collective-permute-start.6 = (bf16[256,1024]{1,0:T(8,128)(2,1)S(1)}, bf16[256,1024]{1,0:T(8,128)(2,1)S(1)}, u32[]{:S(2)}, u32[]{:S(2)}) collective-permute-start(bf16[256,1024]{1,0:T(8,128)(2,1)S(1)} %slice.61), channel_id=1, source_target_pairs={{0,3},{1,0},{2,1},{3,2},{4,7},{5,4},{6,5},{7,6},{8,11},{9,8},{10,9... | collective-permute-start | bytes 1572872 | tf_op jit(solution)/shard_map/ppermute | solution.py:348
  90.1 30.6 %collective-permute-done.6.refs_5_ = bf16[256,1024]{1,0:T(8,128)(2,1)S(1)} collective-permute-done((bf16[256,1024]{1,0:T(8,128)(2,1)S(1)}, bf16[256,1024]{1,0:T(8,128)(2,1)S(1)}, u32[]{:S(2)}, u32[]{:S(2)}) %collective-permute-start.6) | collective-permute-done | bytes 524320 | tf_op jit(solution)/shard_map/ppermute | solution.py:348
  122.3 3.1 %collective-permute-start.8 = (bf16[256,1024]{1,0:T(8,128)(2,1)}, bf16[256,1024]{1,0:T(8,128)(2,1)S(1)}, u32[]{:S(2)}, u32[]{:S(2)}) collective-permute-start(bf16[256,1024]{1,0:T(8,128)(2,1)} %slice.63), channel_id=1, source_target_pairs={{0,3},{1,0},{2,1},{3,2},{4,7},{5,4},{6,5},{7,6},{8,11},{9,8},{10,9... | collective-permute-start | bytes 1572872 | tf_op jit(solution)/shard_map/ppermute | solution.py:348
  126.2 6.2 %collective-permute-done.7.refs_9_.refs_4_ = bf16[256,1024]{1,0:T(8,128)(2,1)S(1)} collective-permute-done((bf16[256,1024]{1,0:T(8,128)(2,1)S(1)}, bf16[256,1024]{1,0:T(8,128)(2,1)S(1)}, u32[]{:S(2)}, u32[]{:S(2)}) %collective-permute-start.7) | collective-permute-done | bytes 524320 | tf_op jit(solution)/shard_map/ppermute | solution.py:347
  135.8 5.5 %pk0.1.refs_7_ = f32[512,256]{1,0:T(8,128)} custom-call(s32[2,4]{1,0:T(2,128)} %get-tuple-element.31.refs_0_, bf16[512,1024]{1,0:T(8,128)(2,1)} %get-tuple-element.37.refs_1_, bf16[512,1024]{1,0:T(8,128)(2,1)} %copy-done, bf16[512,1024]{1,0:T(8,128)(2,1)} %copy-done.1, bf16[256,1024]{1,0:T(8,128)(2,1)} %copy-done.4, bf16[256,1024]{1,0:T(8,128)(2,1)} %copy-done.5, ...), custom_call_target="tpu_custom_call" | custom-call | flops 1073741824 | bytes 16777216 | tf_op jit(solution)/shard_map/pk0/pallas_call | solution.py:139
  142.2 6.1 %pk1.1 = bf16[512,256]{1,0:T(8,128)(2,1)} custom-call(s32[2,4]{1,0:T(2,128)} %get-tuple-element.30.refs_0_, bf16[512,1024]{1,0:T(8,128)(2,1)} %collective-permute-done.2.refs_6_.refs_1_, bf16[512,1024]{1,0:T(8,128)(2,1)} %copy-done.3, bf16[512,1024]{1,0:T(8,128)(2,1)} %copy-done.2, bf16[256,1024]{1,0:T(8,128)(2,1)} %copy-done.6, ...), custom_call_target="tpu_custom_call" | custom-call | flops 1073741824 | bytes 16777216 | tf_op jit(solution)/shard_map/pk1/pallas_call | solution.py:139
  148.4 2.0 collective-permute-start.28
  150.4 7.0 %collective-permute-done.11 = bf16[512,256]{1,0:T(8,128)(2,1)S(1)} collective-permute-done((bf16[512,256]{1,0:T(8,128)(2,1)}, bf16[512,256]{1,0:T(8,128)(2,1)S(1)}, u32[]{:S(2)}, u32[]{:S(2)}) %collective-permute-start.11) | collective-permute-done | bytes 262176 | tf_op jit(solution)/shard_map/ppermute | solution.py:403
  160.0 3.2 %collective-permute-start.13 = (bf16[2,512,256]{2,1,0:T(8,128)(2,1)S(1)}, bf16[2,512,256]{2,1,0:T(8,128)(2,1)S(1)}, u32[]{:S(2)}, u32[]{:S(2)}) collective-permute-start(bf16[2,512,256]{2,1,0:T(8,128)(2,1)S(1)} %pad_maximum_fusion.3.refs_4_), channel_id=1, source_target_pairs={{0,96},{32,0},{64,32},{96,64},{1,97},{33,1},{65,33},{97,65},{2,98}... | collective-permute-start | bytes 1572872 | tf_op jit(solution)/shard_map/ppermute | solution.py:404
  164.6 8.8 %collective-permute-done.12.refs_5_ = bf16[2,512,256]{2,1,0:T(8,128)(2,1)S(1)} collective-permute-done((bf16[2,512,256]{2,1,0:T(8,128)(2,1)S(1)}, bf16[2,512,256]{2,1,0:T(8,128)(2,1)S(1)}, u32[]{:S(2)}, u32[]{:S(2)}) %collective-permute-start.12) | collective-permute-done | bytes 524320 | tf_op jit(solution)/shard_map/ppermute | solution.py:404
  173.4 3.8 %collective-permute-done.13.refs_6_ = bf16[2,512,256]{2,1,0:T(8,128)(2,1)S(1)} collective-permute-done((bf16[2,512,256]{2,1,0:T(8,128)(2,1)S(1)}, bf16[2,512,256]{2,1,0:T(8,128)(2,1)S(1)}, u32[]{:S(2)}, u32[]{:S(2)}) %collective-permute-start.13) | collective-permute-done | bytes 524320 | tf_op jit(solution)/shard_map/ppermute | solution.py:404
  179.0 2.3 pad_maximum_fusion.1
  184.6 9.2 %pq.1.refs_1_ = bf16[4,512,128]{2,1,0:T(8,128)(2,1)} custom-call(s32[2,8]{1,0:T(2,128)} %copy-done.24, bf16[512,1024]{1,0:T(8,128)(2,1)} %get-tuple-element.37.refs_1_, bf16[512,1024]{1,0:T(8,128)(2,1)} %copy-done, bf16[512,1024]{1,0:T(8,128)(2,1)} %copy-done.1, bf16[256,1024]{1,0:T(8,128)(2,1)} %copy-done.4, bf16[256,1024]{1,0:T(8,128)(2,1)} %copy-done.5, ...), custom_call_target="tpu_custom_call" | custom-call | flops 4294967296 | bytes 16777216 | tf_op jit(solution)/shard_map/pq/pallas_call | solution.py:139
  193.9 12.3 %shard_map.114.refs_1_ = bf16[256,512]{1,0:T(8,128)(2,1)} custom-call(s32[2,2]{1,0:T(2,128)} %get-tuple-element.28.refs_0_, bf16[4,512,128]{2,1,0:T(8,128)(2,1)} %pq.1.refs_1_, s32[4,512,1]{2,1,0:T(8,128)} %copy.44.refs_2_, s32[8,1,1024]{2,1,0:T(1,128)} %reshape.1309.refs_3_, bf16[2,512,256]{2,1,0:T(8,128)(2,1)} %copy-done.10, ...), custom_call_target="tpu_custom_call" | custom-call | flops 4294967296 | bytes 6291456 | tf_op jit(solution)/shard_map/pallas_call | solution.py:234
  206.2 3.0 %collective-permute-start.32 = (bf16[256,512]{1,0:T(8,128)(2,1)}, bf16[256,512]{1,0:T(8,128)(2,1)S(1)}, u32[]{:S(2)}, u32[]{:S(2)}) collective-permute-start(bf16[256,512]{1,0:T(8,128)(2,1)} %shard_map.114.refs_1_), channel_id=1, source_target_pairs={{0,4},{4,0},{1,5},{5,1},{2,6},{6,2},{3,7},{7,3},{8,12},{12,8},{9,1... | collective-permute-start | bytes 786440 | tf_op jit(solution)/shard_map/ppermute | solution.py:431
  209.1 2.0 collective-permute-start.31
  211.2 2.1 collective-permute-start.29
  214.4 18.7 %shard_map.113.refs_1_ = bf16[256,512]{1,0:T(8,128)(2,1)} custom-call(s32[2,2]{1,0:T(2,128)} %get-tuple-element.29.refs_0_, bf16[4,512,128]{2,1,0:T(8,128)(2,1)} %pq.1.refs_1_, s32[4,512,1]{2,1,0:T(8,128)} %copy.44.refs_2_, s32[8,1,1024]{2,1,0:T(1,128)} %reshape.1309.refs_3_, bf16[2,512,256]{2,1,0:T(8,128)(2,1)} %copy-done.10, ...), custom_call_target="tpu_custom_call" | custom-call | flops 4294967296 | bytes 6291456 | tf_op jit(solution)/shard_map/pallas_call | solution.py:234
  235.3 3.2 %collective-permute-start.34 = (bf16[256,512]{1,0:T(8,128)(2,1)S(1)}, bf16[256,512]{1,0:T(8,128)(2,1)S(1)}, u32[]{:S(2)}, u32[]{:S(2)}) collective-permute-start(bf16[256,512]{1,0:T(8,128)(2,1)S(1)} %collective-permute-done.32.refs_5_), channel_id=1, source_target_pairs={{0,3},{1,0},{2,1},{3,2},{4,7},{5,4},{6,5},{7,6},{8,11},{9,8},{10,9... | collective-permute-start | bytes 786440 | tf_op jit(solution)/shard_map/ppermute | solution.py:433
  238.5 2.2 collective-permute-start.35
  248.2 2.0 collective-permute-start.23
  251.5 2.8 collective-permute-start.25
  254.2 2.2 convolution_convert_fusion.1
  256.5 7.8 %m0.1.refs_11_ = f32[512,1024]{1,0:T(8,128)} custom-call(s32[2,8]{1,0:T(2,128)} %pad_add_fusion.refs_0_, bf16[256,512]{1,0:T(8,128)(2,1)} %shard_map.114.refs_1_, bf16[256,512]{1,0:T(8,128)(2,1)} %copy-done.15, bf16[256,512]{1,0:T(8,128)(2,1)} %copy-done.16, bf16[256,512]{1,0:T(8,128)(2,1)} %copy-done.13, bf16[256,512]{1,0:T(8,128)(2,1)} %copy-done.12, ...), custom_call_target="tpu_custom_call" | custom-call | flops 2147483648 | bytes 12582912 | tf_op jit(solution)/shard_map/m0/pallas_call | solution.py:283
  265.3 7.8 %m1.1 = bf16[512,1024]{1,0:T(8,128)(2,1)} custom-call(s32[2,8]{1,0:T(2,128)} %pad_add_fusion.refs_0_, bf16[256,512]{1,0:T(8,128)(2,1)} %shard_map.113.refs_1_, bf16[256,512]{1,0:T(8,128)(2,1)} %copy-done.19, bf16[256,512]{1,0:T(8,128)(2,1)} %copy-done.21, bf16[256,512]{1,0:T(8,128)(2,1)} %copy-done.17, bf16[256,512]{1,0:T(8,128)(2,1)} %copy-done.14, ...), custom_call_target="tpu_custom_call" | custom-call | flops 2147483648 | bytes 12582912 | tf_op jit(solution)/shard_map/m1/pallas_call | solution.py:283
  (185 shorter events, 49.2 us)
Async XLA Ops:
  7.2 126.9 %all-gather.4.cloned.1.call-start = ((), (), s32[]{:S(2)}) async-start(), calls=%async_computation | async-start | bytes 4866048 | tf_op jit(solution)/shard_map/all_gather | solution.py:334
  20.5 164.1 %all-gather.6.cloned.1.call-start = ((), (), s32[]{:S(2)}) async-start(), calls=%async_computation.1 | async-start | bytes 9437184 | tf_op jit(solution)/shard_map/all_gather | solution.py:334
  20.8 13.2 %collective-permute-start.10 = (bf16[512,512]{1,0:T(8,128)(2,1)S(1)}, bf16[512,512]{1,0:T(8,128)(2,1)S(1)}, u32[]{:S(2)}, u32[]{:S(2)}) collective-permute-start(bf16[512,512]{1,0:T(8,128)(2,1)S(1)} %multiply_convert_fusion), channel_id=1, source_target_pairs={{0,16},{16,0},{1,17},{17,1},{2,18},{18,2},{3,19},{19,3},{4,20},{20... | collective-permute-start | bytes 1572872 | tf_op jit(solution)/shard_map/ppermute | solution.py:338
  35.0 221.5 %all-gather.8.cloned.1.call-start = ((), (), s32[]{:S(2)}) async-start(), calls=%async_computation.2 | async-start | bytes 9437184 | tf_op jit(solution)/shard_map/all_gather | solution.py:334
  36.8 47.8 %collective-permute-start = (bf16[512,1024]{1,0:T(8,128)(2,1)}, bf16[512,1024]{1,0:T(8,128)(2,1)S(1)}, u32[]{:S(2)}, u32[]{:S(2)}) collective-permute-start(bf16[512,1024]{1,0:T(8,128)(2,1)} %get-tuple-element.37.refs_1_), channel_id=1, source_target_pairs={{0,1},{1,2},{2,3},{3,0},{4,5},{5,6},{6,7},{7,4},{8,9},{9,10},{10,1... | collective-permute-start | bytes 3145736 | tf_op jit(solution)/shard_map/ppermute | solution.py:344
  38.1 46.5 %collective-permute-start.1 = (bf16[512,1024]{1,0:T(8,128)(2,1)}, bf16[512,1024]{1,0:T(8,128)(2,1)S(1)}, u32[]{:S(2)}, u32[]{:S(2)}) collective-permute-start(bf16[512,1024]{1,0:T(8,128)(2,1)} %get-tuple-element.37.refs_1_), channel_id=1, source_target_pairs={{0,3},{1,0},{2,1},{3,2},{4,7},{5,4},{6,5},{7,6},{8,11},{9,8},{10,9... | collective-permute-start | bytes 3145736 | tf_op jit(solution)/shard_map/ppermute | solution.py:345
  40.0 36.0 %collective-permute-start.2 = (bf16[512,1024]{1,0:T(8,128)(2,1)}, bf16[512,1024]{1,0:T(8,128)(2,1)}, u32[]{:S(2)}, u32[]{:S(2)}) collective-permute-start(bf16[512,1024]{1,0:T(8,128)(2,1)} %get-tuple-element.37.refs_1_), channel_id=1, source_target_pairs={{0,4},{4,0},{1,5},{5,1},{2,6},{6,2},{3,7},{7,3},{8,12},{12,8},{9,1... | collective-permute-start | bytes 3145736 | tf_op jit(solution)/shard_map/ppermute | solution.py:351
  43.4 35.8 %collective-permute-start.26 = (bf16[512,512]{1,0:T(8,128)(2,1)}, bf16[512,512]{1,0:T(8,128)(2,1)}, u32[]{:S(2)}, u32[]{:S(2)}) collective-permute-start(bf16[512,512]{1,0:T(8,128)(2,1)} %param.19), channel_id=1, source_target_pairs={{0,0},{1,33},{2,66},{3,99},{4,16},{5,49},{6,82},{7,115},{16,32},{1... | collective-permute-start | bytes 1572872 | tf_op jit(solution)/shard_map/ppermute | solution.py:316
  76.0 45.3 %collective-permute-start.4 = (bf16[512,1024]{1,0:T(8,128)(2,1)}, bf16[512,1024]{1,0:T(8,128)(2,1)S(1)}, u32[]{:S(2)}, u32[]{:S(2)}) collective-permute-start(bf16[512,1024]{1,0:T(8,128)(2,1)} %collective-permute-done.2.refs_6_.refs_1_), channel_id=1, source_target_pairs={{0,3},{1,0},{2,1},{3,2},{4,7},{5,4},{6,5},{7,6},{8,11},{9,8},{10,9... | collective-permute-start | bytes 3145736 | tf_op jit(solution)/shard_map/ppermute | solution.py:345
  76.6 44.5 %collective-permute-start.3 = (bf16[512,1024]{1,0:T(8,128)(2,1)}, bf16[512,1024]{1,0:T(8,128)(2,1)S(1)}, u32[]{:S(2)}, u32[]{:S(2)}) collective-permute-start(bf16[512,1024]{1,0:T(8,128)(2,1)} %collective-permute-done.2.refs_6_.refs_1_), channel_id=1, source_target_pairs={{0,1},{1,2},{2,3},{3,0},{4,5},{5,6},{6,7},{7,4},{8,9},{9,10},{10,1... | collective-permute-start | bytes 3145736 | tf_op jit(solution)/shard_map/ppermute | solution.py:344
  79.2 69.2 %collective-permute-start.27 = (bf16[512,512]{1,0:T(8,128)(2,1)}, bf16[512,512]{1,0:T(8,128)(2,1)}, u32[]{:S(2)}, u32[]{:S(2)}) collective-permute-start(bf16[512,512]{1,0:T(8,128)(2,1)} %collective-permute-done.26), channel_id=1, source_target_pairs={{0,0},{1,3},{2,2},{3,1},{32,33},{33,32},{34,35},{35,34},{64,66},{6... | collective-permute-start | bytes 1572872 | tf_op jit(solution)/shard_map/ppermute | solution.py:414
  84.6 36.3 %collective-permute-start.5 = (bf16[256,1024]{1,0:T(8,128)(2,1)S(1)}, bf16[256,1024]{1,0:T(8,128)(2,1)S(1)}, u32[]{:S(2)}, u32[]{:S(2)}) collective-permute-start(bf16[256,1024]{1,0:T(8,128)(2,1)S(1)} %slice.60), channel_id=1, source_target_pairs={{0,1},{1,2},{2,3},{3,0},{4,5},{5,6},{6,7},{7,4},{8,9},{9,10},{10,1... | collective-permute-start | bytes 1572872 | tf_op jit(solution)/shard_map/ppermute | solution.py:347
  84.8 36.0 %collective-permute-start.6 = (bf16[256,1024]{1,0:T(8,128)(2,1)S(1)}, bf16[256,1024]{1,0:T(8,128)(2,1)S(1)}, u32[]{:S(2)}, u32[]{:S(2)}) collective-permute-start(bf16[256,1024]{1,0:T(8,128)(2,1)S(1)} %slice.61), channel_id=1, source_target_pairs={{0,3},{1,0},{2,1},{3,2},{4,7},{5,4},{6,5},{7,6},{8,11},{9,8},{10,9... | collective-permute-start | bytes 1572872 | tf_op jit(solution)/shard_map/ppermute | solution.py:348
  121.2 11.2 %collective-permute-start.7 = (bf16[256,1024]{1,0:T(8,128)(2,1)S(1)}, bf16[256,1024]{1,0:T(8,128)(2,1)S(1)}, u32[]{:S(2)}, u32[]{:S(2)}) collective-permute-start(bf16[256,1024]{1,0:T(8,128)(2,1)S(1)} %slice.62), channel_id=1, source_target_pairs={{0,1},{1,2},{2,3},{3,0},{4,5},{5,6},{6,7},{7,4},{8,9},{9,10},{10,1... | collective-permute-start | bytes 1572872 | tf_op jit(solution)/shard_map/ppermute | solution.py:347
  148.4 16.2 %collective-permute-start.28 = (bf16[512,512]{1,0:T(8,128)(2,1)}, bf16[512,512]{1,0:T(8,128)(2,1)S(1)}, u32[]{:S(2)}, u32[]{:S(2)}) collective-permute-start(bf16[512,512]{1,0:T(8,128)(2,1)} %collective-permute-done.27), channel_id=1, source_target_pairs={{0,16},{16,0},{1,17},{17,1},{2,18},{18,2},{3,19},{19,3},{4,20},{20... | collective-permute-start | bytes 1572872 | tf_op jit(solution)/shard_map/ppermute | solution.py:415
  158.4 14.9 %collective-permute-start.12 = (bf16[2,512,256]{2,1,0:T(8,128)(2,1)S(1)}, bf16[2,512,256]{2,1,0:T(8,128)(2,1)S(1)}, u32[]{:S(2)}, u32[]{:S(2)}) collective-permute-start(bf16[2,512,256]{2,1,0:T(8,128)(2,1)S(1)} %pad_maximum_fusion.3.refs_4_), channel_id=1, source_target_pairs={{0,32},{32,64},{64,96},{96,0},{1,33},{33,65},{65,97},{97,1},{2,34}... | collective-permute-start | bytes 1572872 | tf_op jit(solution)/shard_map/ppermute | solution.py:404
  160.0 17.2 %collective-permute-start.13 = (bf16[2,512,256]{2,1,0:T(8,128)(2,1)S(1)}, bf16[2,512,256]{2,1,0:T(8,128)(2,1)S(1)}, u32[]{:S(2)}, u32[]{:S(2)}) collective-permute-start(bf16[2,512,256]{2,1,0:T(8,128)(2,1)S(1)} %pad_maximum_fusion.3.refs_4_), channel_id=1, source_target_pairs={{0,96},{32,0},{64,32},{96,64},{1,97},{33,1},{65,33},{97,65},{2,98}... | collective-permute-start | bytes 1572872 | tf_op jit(solution)/shard_map/ppermute | solution.py:404
  163.2 15.8 %collective-permute-start.14 = (bf16[2,512,256]{2,1,0:T(8,128)(2,1)S(1)}, bf16[2,512,256]{2,1,0:T(8,128)(2,1)S(1)}, u32[]{:S(2)}, u32[]{:S(2)}) collective-permute-start(bf16[2,512,256]{2,1,0:T(8,128)(2,1)S(1)} %pad_maximum_fusion.3.refs_4_), channel_id=1, source_target_pairs={{0,64},{32,96},{64,0},{96,32},{1,65},{33,97},{65,1},{97,33},{2,66}... | collective-permute-start | bytes 1572872 | tf_op jit(solution)/shard_map/ppermute | solution.py:404
  182.9 10.9 %collective-permute-start.16 = (bf16[2,512,256]{2,1,0:T(8,128)(2,1)S(1)}, bf16[2,512,256]{2,1,0:T(8,128)(2,1)}, u32[]{:S(2)}, u32[]{:S(2)}) collective-permute-start(bf16[2,512,256]{2,1,0:T(8,128)(2,1)S(1)} %collective-permute-done.12.refs_5_), channel_id=1, source_target_pairs={{0,8},{8,0},{1,9},{9,1},{2,10},{10,2},{3,11},{11,3},{4,12},{12,4},... | collective-permute-start | bytes 1572872 | tf_op jit(solution)/shard_map/ppermute | solution.py:405
  206.2 27.6 %collective-permute-start.32 = (bf16[256,512]{1,0:T(8,128)(2,1)}, bf16[256,512]{1,0:T(8,128)(2,1)S(1)}, u32[]{:S(2)}, u32[]{:S(2)}) collective-permute-start(bf16[256,512]{1,0:T(8,128)(2,1)} %shard_map.114.refs_1_), channel_id=1, source_target_pairs={{0,4},{4,0},{1,5},{5,1},{2,6},{6,2},{3,7},{7,3},{8,12},{12,8},{9,1... | collective-permute-start | bytes 786440 | tf_op jit(solution)/shard_map/ppermute | solution.py:431
  209.1 26.1 %collective-permute-start.31 = (bf16[256,512]{1,0:T(8,128)(2,1)}, bf16[256,512]{1,0:T(8,128)(2,1)S(1)}, u32[]{:S(2)}, u32[]{:S(2)}) collective-permute-start(bf16[256,512]{1,0:T(8,128)(2,1)} %shard_map.114.refs_1_), channel_id=1, source_target_pairs={{0,2},{1,3},{2,0},{3,1},{4,6},{5,7},{6,4},{7,5},{8,10},{9,11},{10,... | collective-permute-start | bytes 786440 | tf_op jit(solution)/shard_map/ppermute | solution.py:432
  211.2 24.1 %collective-permute-start.29 = (bf16[256,512]{1,0:T(8,128)(2,1)}, bf16[256,512]{1,0:T(8,128)(2,1)S(1)}, u32[]{:S(2)}, u32[]{:S(2)}) collective-permute-start(bf16[256,512]{1,0:T(8,128)(2,1)} %shard_map.114.refs_1_), channel_id=1, source_target_pairs={{0,1},{1,2},{2,3},{3,0},{4,5},{5,6},{6,7},{7,4},{8,9},{9,10},{10,1... | collective-permute-start | bytes 786440 | tf_op jit(solution)/shard_map/ppermute | solution.py:432
  213.2 25.2 %collective-permute-start.30 = (bf16[256,512]{1,0:T(8,128)(2,1)}, bf16[256,512]{1,0:T(8,128)(2,1)S(1)}, u32[]{:S(2)}, u32[]{:S(2)}) collective-permute-start(bf16[256,512]{1,0:T(8,128)(2,1)} %shard_map.114.refs_1_), channel_id=1, source_target_pairs={{0,3},{1,0},{2,1},{3,2},{4,7},{5,4},{6,5},{7,6},{8,11},{9,8},{10,9... | collective-permute-start | bytes 786440 | tf_op jit(solution)/shard_map/ppermute | solution.py:432
  233.8 11.1 %collective-permute-start.21 = (bf16[256,512]{1,0:T(8,128)(2,1)}, bf16[256,512]{1,0:T(8,128)(2,1)S(1)}, u32[]{:S(2)}, u32[]{:S(2)}) collective-permute-start(bf16[256,512]{1,0:T(8,128)(2,1)} %shard_map.113.refs_1_), channel_id=1, source_target_pairs={{0,2},{1,3},{2,0},{3,1},{4,6},{5,7},{6,4},{7,5},{8,10},{9,11},{10,... | collective-permute-start | bytes 786440 | tf_op jit(solution)/shard_map/ppermute | solution.py:432
  235.2 13.0 %collective-permute-start.33 = (bf16[256,512]{1,0:T(8,128)(2,1)S(1)}, bf16[256,512]{1,0:T(8,128)(2,1)S(1)}, u32[]{:S(2)}, u32[]{:S(2)}) collective-permute-start(bf16[256,512]{1,0:T(8,128)(2,1)S(1)} %collective-permute-done.32.refs_5_), channel_id=1, source_target_pairs={{0,1},{1,2},{2,3},{3,0},{4,5},{5,6},{6,7},{7,4},{8,9},{9,10},{10,1... | collective-permute-start | bytes 786440 | tf_op jit(solution)/shard_map/ppermute | solution.py:433
  235.3 15.0 %collective-permute-start.34 = (bf16[256,512]{1,0:T(8,128)(2,1)S(1)}, bf16[256,512]{1,0:T(8,128)(2,1)S(1)}, u32[]{:S(2)}, u32[]{:S(2)}) collective-permute-start(bf16[256,512]{1,0:T(8,128)(2,1)S(1)} %collective-permute-done.32.refs_5_), channel_id=1, source_target_pairs={{0,3},{1,0},{2,1},{3,2},{4,7},{5,4},{6,5},{7,6},{8,11},{9,8},{10,9... | collective-permute-start | bytes 786440 | tf_op jit(solution)/shard_map/ppermute | solution.py:433
  238.5 13.0 %collective-permute-start.35 = (bf16[256,512]{1,0:T(8,128)(2,1)S(1)}, bf16[256,512]{1,0:T(8,128)(2,1)S(1)}, u32[]{:S(2)}, u32[]{:S(2)}) collective-permute-start(bf16[256,512]{1,0:T(8,128)(2,1)S(1)} %collective-permute-done.31.refs_4_), channel_id=1, source_target_pairs={{0,4},{4,0},{1,5},{5,1},{2,6},{6,2},{3,7},{7,3},{8,12},{12,8},{9,1... | collective-permute-start | bytes 786440 | tf_op jit(solution)/shard_map/ppermute | solution.py:434
  243.5 20.9 %collective-permute-start.19 = (bf16[256,512]{1,0:T(8,128)(2,1)}, bf16[256,512]{1,0:T(8,128)(2,1)S(1)}, u32[]{:S(2)}, u32[]{:S(2)}) collective-permute-start(bf16[256,512]{1,0:T(8,128)(2,1)} %shard_map.113.refs_1_), channel_id=1, source_target_pairs={{0,1},{1,2},{2,3},{3,0},{4,5},{5,6},{6,7},{7,4},{8,9},{9,10},{10,1... | collective-permute-start | bytes 786440 | tf_op jit(solution)/shard_map/ppermute | solution.py:432
  244.9 19.5 %collective-permute-start.20 = (bf16[256,512]{1,0:T(8,128)(2,1)}, bf16[256,512]{1,0:T(8,128)(2,1)S(1)}, u32[]{:S(2)}, u32[]{:S(2)}) collective-permute-start(bf16[256,512]{1,0:T(8,128)(2,1)} %shard_map.113.refs_1_), channel_id=1, source_target_pairs={{0,3},{1,0},{2,1},{3,2},{4,7},{5,4},{6,5},{7,6},{8,11},{9,8},{10,9... | collective-permute-start | bytes 786440 | tf_op jit(solution)/shard_map/ppermute | solution.py:432
  248.2 16.2 %collective-permute-start.23 = (bf16[256,512]{1,0:T(8,128)(2,1)S(1)}, bf16[256,512]{1,0:T(8,128)(2,1)S(1)}, u32[]{:S(2)}, u32[]{:S(2)}) collective-permute-start(bf16[256,512]{1,0:T(8,128)(2,1)S(1)} %collective-permute-done.22.refs_5_), channel_id=1, source_target_pairs={{0,1},{1,2},{2,3},{3,0},{4,5},{5,6},{6,7},{7,4},{8,9},{9,10},{10,1... | collective-permute-start | bytes 786440 | tf_op jit(solution)/shard_map/ppermute | solution.py:433
  250.2 14.2 %collective-permute-start.24 = (bf16[256,512]{1,0:T(8,128)(2,1)S(1)}, bf16[256,512]{1,0:T(8,128)(2,1)}, u32[]{:S(2)}, u32[]{:S(2)}) collective-permute-start(bf16[256,512]{1,0:T(8,128)(2,1)S(1)} %collective-permute-done.22.refs_5_), channel_id=1, source_target_pairs={{0,3},{1,0},{2,1},{3,2},{4,7},{5,4},{6,5},{7,6},{8,11},{9,8},{10,9... | collective-permute-start | bytes 786440 | tf_op jit(solution)/shard_map/ppermute | solution.py:433
  251.5 13.0 %collective-permute-start.25 = (bf16[256,512]{1,0:T(8,128)(2,1)S(1)}, bf16[256,512]{1,0:T(8,128)(2,1)}, u32[]{:S(2)}, u32[]{:S(2)}) collective-permute-start(bf16[256,512]{1,0:T(8,128)(2,1)S(1)} %collective-permute-done.21.refs_4_), channel_id=1, source_target_pairs={{0,4},{4,0},{1,5},{5,1},{2,6},{6,2},{3,7},{7,3},{8,12},{12,8},{9,1... | collective-permute-start | bytes 786440 | tf_op jit(solution)/shard_map/ppermute | solution.py:434
  (37 other events, 501.7 us)
Sparse Core Ops, SparseCore 0:
  20.7 40.6 all-gather.3
  63.1 52.7 all-gather.5
  181.4 49.8 all-gather.7

commit v3 on v2

--- a/solution.py
+++ b/solution.py
@@ -43,7 +43,18 @@
     return pl.BlockSpec(shape, lambda k, ids: (0,) * len(shape))
 
 
-def dots(ids, pieces, slots, w_ref, w_to, size, buffer, w_buffer, acc, sems, before=None):
+def add_squares(rows, square, started):
+    wide = rows.astype(jnp.float32)
+    wide = wide * wide
+    total = wide[:, :HD]
+    for i in range(1, rows.shape[1] // HD):
+        total = total + wide[:, i * HD : (i + 1) * HD]
+    square[...] = square[...] + total if started else total
+
+
+def dots(
+    ids, pieces, slots, w_ref, w_to, size, buffer, w_buffer, acc, sems, before=None, square=None
+):
     groups = buffer.shape[1] // size
     made = []
     for i, (slot, start, count) in enumerate(slots):
@@ -67,6 +78,8 @@
             acc[...] = part if before is None else part + before[...]
         else:
             acc[...] += part
+        if square is not None:
+            add_squares(buffer[:, deep], square, k > 0)
 
 
 def rows_to(w_buffer, g, c):
@@ -81,17 +94,22 @@
     pieces = refs[: len(slots)]
     w_ref = refs[len(slots)]
     refs = refs[len(slots) + 1 :]
-    before = None
+    before, square = (None, None)
     if partial == FIRST:
-        acc, buffer, w_buffer, sems = refs
+        acc, square, buffer, w_buffer, sems = refs
+    elif partial == LAST:
+        before, early_ref, *refs = refs
+        bias_ref, cos_ref, sin_ref, out_ref, square, buffer, w_buffer, acc, sems = refs
     else:
-        if partial == LAST:
-            before, refs = (refs[0], refs[1:])
-        inverse_ref, bias_ref, cos_ref, sin_ref, out_ref, buffer, w_buffer, acc, sems = refs
-    dots(ids, pieces, slots, w_ref, rows_to, FEAT, buffer, w_buffer, acc, sems, before)
+        square_ref, bias_ref, cos_ref, sin_ref, out_ref, buffer, w_buffer, acc, sems = refs
+    dots(ids, pieces, slots, w_ref, rows_to, FEAT, buffer, w_buffer, acc, sems, before, square)
     if partial == FIRST:
         return
-    inverse = inverse_ref[...]
+    if partial == LAST:
+        square[...] += early_ref[...]
+        square_ref = square
+    mean = jnp.sum(square_ref[...], axis=1, keepdims=True) * (1.0 / MODEL)
+    inverse = lax.rsqrt(mean + NORM_EPS)
     cosine = cos_ref[...]
     sines = sin_ref[...]
 
@@ -122,7 +140,7 @@
     ids = ids[:, GROUPS - groups :] if partial == LAST else ids[:, :groups]
     dtype = jnp.bfloat16
     out_shape = (BLOCKS, HEADS * BLOCK, HD) if queries else (ROWS, 2 * HD)
-    extra = finish if before is None else (before,) + finish
+    extra = finish if before is None else before + finish
     scratch = [
         pltpu.VMEM((ROWS, groups * FEAT), jnp.bfloat16),
         pltpu.VMEM((groups * FEAT, width), jnp.bfloat16),
@@ -132,6 +150,7 @@
     else:
         scratch += [pltpu.VMEM((ROWS, width), jnp.float32)]
     scratch += [pltpu.SemaphoreType.DMA((len(pieces) + 2 * groups,))]
+    out = [jax.ShapeDtypeStruct(out_shape, dtype), jax.ShapeDtypeStruct((ROWS, HD), jnp.float32)]
 
     def body(*refs):
         project_body(slots, queries, partial, *refs)
@@ -139,9 +158,9 @@
     return pl.pallas_call(
         body,
         in_specs=[SCALARS] + [ANYWHERE] * (len(pieces) + 1) + [NEAR] * len(extra),
-        out_specs=NEAR,
+        out_specs=NEAR if queries else [NEAR, NEAR],
         scratch_shapes=scratch,
-        out_shape=jax.ShapeDtypeStruct(out_shape, dtype),
+        out_shape=out[0] if queries else out,
         cost_estimate=pl.CostEstimate(
             flops=2 * ROWS * groups * FEAT * width, transcendentals=0, bytes_accessed=16 << 20
         ),
@@ -195,7 +214,8 @@
             scores = following
             following = scores_of(h + 1) if h + 1 < parts else None
             if masked:
-                allowed = kpos_ref[j] <= qpos_ref[0, h * rows : (h + 1) * rows]
+                row_pos = qpos_ref[0, h * rows : (h + 1) * rows]
+                allowed = kpos_ref[j] <= jnp.concatenate([row_pos] * (KEYS // HD), axis=1)
                 scores = jnp.where(allowed, scores, NEG_FILL)
             old = top[h]
             new = jnp.maximum(old, jnp.max(scores, axis=1, keepdims=True))
@@ -238,7 +258,7 @@
             grid=(count,),
             in_specs=[
                 pl.BlockSpec((1, HEADS * BLOCK, HD), lambda c, b: (c + first, 0, 0)),
-                pl.BlockSpec((1, HEADS * BLOCK, 1), lambda c, b: (c + first, 0, 0)),
+                pl.BlockSpec((1, HEADS * BLOCK, HD), lambda c, b: (c + first, 0, 0)),
                 whole(NSTEPS, 1, KEYS),
             ]
             + [pl.BlockSpec(memory_space=pl.ANY)] * len(pairs),
@@ -262,40 +282,43 @@
 
 def mix_body(slots, ids, *refs):
     pieces = refs[: len(slots)]
-    w_ref, back_ref, base_ref, out_ref, buffer, w_buffer, acc, sems = refs[len(slots) :]
+    refs = refs[len(slots) :]
+    w_ref, back_ref, tokens_ref, out_ref, context_ref, buffer, w_buffer, acc, sems = refs
     dots(ids, pieces, slots, w_ref, columns_to, ROWS, buffer, w_buffer, acc, sems)
     back = back_ref[...]
+    context = jnp.dot(back, buffer[:, :ROWS], preferred_element_type=jnp.float32)
+    context_ref[...] = context.astype(jnp.bfloat16)
     high = acc[...].astype(jnp.bfloat16)
     low = (acc[...] - high.astype(jnp.float32)).astype(jnp.bfloat16)
     mixed = jnp.dot(back, high, preferred_element_type=jnp.float32) + jnp.dot(
         back, low, preferred_element_type=jnp.float32
     )
-    out_ref[...] = (base_ref[...].astype(jnp.float32) + mixed).astype(out_ref.dtype)
-
-
-def mix(pieces, ids, w_out, back, base, last):
-    rows = pieces[0].shape[0]
-    slots = [(i, 0, rows) for i in range(GROUPS)]
-
+    out_ref[...] = (tokens_ref[...].astype(jnp.float32) + mixed).astype(jnp.bfloat16)
+
+
+def mix(pieces, slots, ids, w_out, back, tokens):
     def body(*refs):
         mix_body(slots, *refs)
 
     return pl.pallas_call(
         body,
         in_specs=[SCALARS] + [ANYWHERE] * (len(pieces) + 1) + [NEAR] * 2,
-        out_specs=NEAR,
+        out_specs=[NEAR, NEAR],
         scratch_shapes=[
-            pltpu.VMEM((rows, GROUPS * ROWS), jnp.bfloat16),
+            pltpu.VMEM((ROWS, GROUPS * ROWS), jnp.bfloat16),
             pltpu.VMEM((GROUPS * ROWS, FEAT), jnp.bfloat16),
-            pltpu.VMEM((rows, FEAT), jnp.float32),
+            pltpu.VMEM((ROWS, FEAT), jnp.float32),
             pltpu.SemaphoreType.DMA((len(pieces) + 2 * GROUPS,)),
         ],
-        out_shape=jax.ShapeDtypeStruct((ROWS, FEAT), jnp.bfloat16 if last else jnp.float32),
+        out_shape=[
+            jax.ShapeDtypeStruct((ROWS, FEAT), jnp.bfloat16),
+            jax.ShapeDtypeStruct((ROWS, HEADS * HD), jnp.bfloat16),
+        ],
         cost_estimate=pl.CostEstimate(
-            flops=2 * rows * HEADS * HD * GROUPS * FEAT, transcendentals=0, bytes_accessed=12 << 20
+            flops=2 * ROWS * HEADS * HD * GROUPS * FEAT, transcendentals=0, bytes_accessed=16 << 20
         ),
-        name="m1" if last else "m0",
-    )(ids, *pieces, w_out, back, base)
+        name="m",
+    )(ids, *pieces, w_out, back, tokens)
 
 
 def block(tokens, positions, norm_gain, w_query, w_key, w_value, b_query, b_key, b_value, w_out):
@@ -352,15 +375,6 @@
     left, right, low, high = ring(sorted_tokens)
     oleft, oright, olow, ohigh = ring(other)
 
-    def square(piece):
-        wide = piece.astype(f32)
-        return jnp.sum(wide * wide, 1, keepdims=True)
-
-    total = sum(square(p) for p in (sorted_tokens, left, right, other, oleft, oright))
-    total_low, total_high = (square(low), square(high))
-    total += jnp.concatenate([total_low, total_high], 0)
-    total += jnp.concatenate([square(olow), square(ohigh)], 0)
-    inverse = lax.rsqrt(total * (1.0 / MODEL) + NORM_EPS)
     y, zl, core = (lax.axis_index("y"), lax.axis_index("zl"), lax.axis_index("core"))
     groups = jnp.stack([z * 4 + (x + d) % 4 for z in (zh, 1 - zh) for d in (0, 3, 1, 2)])
     ids = jnp.stack([groups // 2, (groups % 2) ^ zl]).astype(jnp.int32)
@@ -390,21 +404,20 @@
     full = jnp.sum((last_pos[None, :] <= by_block[:, :1]).astype(jnp.int32), 1)
     need = jnp.sum((first_pos[None, :] <= by_block[:, -1:]).astype(jnp.int32), 1)
     bounds = jnp.stack([full, need])
-    qpos = jnp.tile(by_block[:, None, :], (1, HEADS, 1)).reshape(BLOCKS, HEADS * BLOCK, 1)
+    qpos = jnp.broadcast_to(by_block[:, None, :, None], (BLOCKS, HEADS, BLOCK, HD))
+    qpos = qpos.reshape(BLOCKS, HEADS * BLOCK, HD)
 
     kv_bias = jnp.concatenate((b_key, b_value))[None, :]
-    start = project(pieces[:5], slots, ids, w_kv_all, (), False, FIRST)
-    inverse, kpos, bounds, qpos, start = lax.optimization_barrier(
-        (inverse, kpos, bounds, qpos, start)
-    )
-    finish = (inverse, kv_bias, cosine, sines)
-    kv = project(pieces[5:], slots, ids, w_kv_all, finish, False, LAST, start)
+    kpos, bounds, qpos, ids = lax.optimization_barrier((kpos, bounds, qpos, ids))
+    early = tuple(project(pieces[:5], slots, ids, w_kv_all, (), False, FIRST))
+    finish = (kv_bias, cosine, sines)
+    kv, square = project(pieces[5:], slots, ids, w_kv_all, finish, False, LAST, early)
 
     pair = jnp.stack([kv, lax.ppermute(kv, "zl", SWAP)])
     own_kv = [pair] + [lax.ppermute(pair, "y", steps) for steps in (NEXT, PREV, ACROSS)]
     all_kv = own_kv + [lax.ppermute(a, "core", SWAP) for a in own_kv]
 
-    finish = (inverse, b_query[None, :], cosine, sines)
+    finish = (square, b_query[None, :], cosine, sines)
     both_slots = slots + [(slot + 4, at, size) for slot, at, size in slots]
     queries = project(pieces, both_slots, ids, w_q_all, finish, True)
 
@@ -417,25 +430,16 @@
     w_out_all = over_seq(moved, flip)
     mix_ids = jnp.stack([(groups + x) % 4, (groups // 4) ^ zl]).astype(jnp.int32)
 
-    base = tokens
-    contexts, parts = ([], [])
+    found, mix_slots = ([], [])
     for first, count in CALLS:
         at = slice(first, first + count)
-        parts.append(attend(bounds[:, at], queries, qpos, all_kv, kpos, first, count))
-        if first + count == BLOCKS // 2 or first + count == BLOCKS:
-            own = parts[0] if len(parts) == 1 else jnp.concatenate(parts, 0)
-            contexts.append(own)
-            parts = []
-            last = first + count == BLOCKS
-            half = BLOCKS // 2 if last else 0
-            across = lax.ppermute(own, "zh", SWAP)
-            near = [own] + [lax.ppermute(own, "x", s) for s in (NEXT, PREV, ACROSS)]
-            far = [across] + [lax.ppermute(across, "x", s) for s in (NEXT, PREV)]
-            found = near + far + [lax.ppermute(near[3], "zh", SWAP)]
-            rows = slice(half * BLOCK, (first + count) * BLOCK)
-            base = mix(found, mix_ids, w_out_all, back[:, rows], base, last)
-    context = jnp.dot(back, jnp.concatenate(contexts, 0), preferred_element_type=f32).astype(bf16)
-    return (base, context)
+        own = attend(bounds[:, at], queries, qpos, all_kv, kpos, first, count)
+        across = lax.ppermute(own, "zh", SWAP)
+        near = [own] + [lax.ppermute(own, "x", s) for s in (NEXT, PREV, ACROSS)]
+        far = [across] + [lax.ppermute(across, "x", s) for s in (NEXT, PREV)]
+        found += near + far + [lax.ppermute(near[3], "zh", SWAP)]
+        mix_slots += [(i, first * BLOCK, count * BLOCK) for i in range(GROUPS)]
+    return tuple(mix(found, mix_slots, mix_ids, w_out_all, back, tokens))
 
 
 def solution(mesh):

time: 281 us -> 271 us (0.964)
  starting transfers between devices: 64.3 us -> 60.6 us
  other arithmetic: 17.4 us -> 14.1 us
    ppermute x2, waiting for transfers between devices: 31 us -> 1.92 us  [ring(): high = lax.ppermute(high, 'x', PREV)]
    ppermute x2, waiting for transfers between devices: 0.01 us -> 10.7 us  [ring(): left = lax.ppermute(own, 'x', NEXT)]
    ppermute x6, waiting for transfers between devices: 0.02 us -> 10.6 us  [block(): near = [own] + [lax.ppermute(own, 'x', s) for s in (NEXT, PREV, ACROSS)]]
    ppermute x2, waiting for transfers between devices: 0.01 us -> 9.83 us  [ring(): right = lax.ppermute(own, 'x', PREV)]
    ppermute x2, waiting for transfers between devices: 6.24 us -> 0.01 us  [ring(): low = lax.ppermute(low, 'x', NEXT)]
    ppermute x2, waiting for transfers between devices: 0.01 us -> 5.75 us  [block(): found += near + far + [lax.ppermute(near[3], 'zh', SWAP)]]
    pallas_call x2 -> x1, Pallas kernels: 15.7 us -> 10.3 us  [mix(): pl.pallas_call(body, in_specs=[SCALARS] + [ANYWHERE] * (len(pieces) + 1)...]
    slice x4, local copies, waits for them, and re-layouts: 1.14 us -> 4.59 us  [ring(): low, high = (left[:half], right[half:])]
  transfers between devices with their start and end apart: 39 -> 39, of which waited for: 12 -> 15; matrix products, arithmetic and copies ran while one was open for 9% -> 8% of each run, Pallas kernels for 21% -> 20%
where the time goes in v3:
time: 271 us; the launch traced here: 270 us
  waiting for transfers between devices  103 us (38%)
  Pallas kernels  65.2 us (24%)
  starting transfers between devices  60.6 us (22%)
  between operations  14.4 us (5%)
  other arithmetic  14.1 us (5%)
  local copies, waits for them, and re-layouts  10.5 us (4%)
    pallas_call x2, Pallas kernels, attend(): pl.pallas_call(body, grid_spec=pltpu.PrefetchScalarGridSpec(num_scalar_pr...  31.4 us
    ppermute x1, waiting for transfers between devices, block(): other = lax.ppermute(sorted_tokens, 'zh', SWAP)  24.3 us
    pallas_call x3, Pallas kernels, project(): pl.pallas_call(body, in_specs=[SCALARS] + [ANYWHERE] * (len(pieces) + 1)...  23.5 us
    ppermute x3, waiting for transfers between devices, block(): lax.ppermute(pair, 'y', steps)  14.6 us
    ppermute x1, waiting for transfers between devices, block(): q_flip = lax.ppermute(w_q, 'zl', SWAP)  11.3 us
    ppermute x2, waiting for transfers between devices, ring(): left = lax.ppermute(own, 'x', NEXT)  10.7 us
    ppermute x6, waiting for transfers between devices, block(): near = [own] + [lax.ppermute(own, 'x', s) for s in (NEXT, PREV, ACROSS)]  10.6 us
    pallas_call x1, Pallas kernels, mix(): pl.pallas_call(body, in_specs=[SCALARS] + [ANYWHERE] * (len(pieces) + 1)...  10.3 us
  transfers between devices with their start and end apart: 39, of which 15 were waited for; matrix products, arithmetic and copies ran while one was open for 8% of the time, Pallas kernels for 20%

profile of v3, /device:TPU:0, one launch (start us, length us, event | category | flops | bytes accessed | tf_op | source)
XLA Modules:
  0.0 270.0 jit_solution(15279914569679766134)
XLA Ops:
  11.1 2.1 collective-permute-start
  13.2 6.5 %collective-permute-done = bf16[528,256]{1,0:T(8,128)(2,1)S(1)} collective-permute-done((bf16[528,256]{1,0:T(8,128)(2,1)S(1)}, bf16[528,256]{1,0:T(8,128)(2,1)S(1)}, u32[]{:S(2)}, u32[]{:S(2)}) %collective-permute-start) | collective-permute-done | bytes 270368 | tf_op jit(solution)/shard_map/ppermute | solution.py:360
  22.6 11.3 %collective-permute-done.10 = bf16[512,512]{1,0:T(8,128)(2,1)S(1)} collective-permute-done((bf16[512,512]{1,0:T(8,128)(2,1)S(1)}, bf16[512,512]{1,0:T(8,128)(2,1)S(1)}, u32[]{:S(2)}, u32[]{:S(2)}) %collective-permute-start.10) | collective-permute-done | bytes 524320 | tf_op jit(solution)/shard_map/ppermute | solution.py:361
  36.8 3.4 %collective-permute-start.5 = (bf16[512,1024]{1,0:T(8,128)(2,1)}, bf16[512,1024]{1,0:T(8,128)(2,1)}, u32[]{:S(2)}, u32[]{:S(2)}) collective-permute-start(bf16[512,1024]{1,0:T(8,128)(2,1)} %convolution_convert_fusion.refs_1_), channel_id=1, source_target_pairs={{0,4},{4,0},{1,5},{5,1},{2,6},{6,2},{3,7},{7,3},{8,12},{12,8},{9,1... | collective-permute-start | bytes 3145736 | tf_op jit(solution)/shard_map/ppermute | solution.py:374
  43.5 5.4 %collective-permute-start.33 = (bf16[512,512]{1,0:T(8,128)(2,1)}, bf16[512,512]{1,0:T(8,128)(2,1)}, u32[]{:S(2)}, u32[]{:S(2)}) collective-permute-start(bf16[512,512]{1,0:T(8,128)(2,1)} %param.19), channel_id=1, source_target_pairs={{0,0},{1,33},{2,66},{3,99},{4,16},{5,49},{6,82},{7,115},{16,32},{1... | collective-permute-start | bytes 1572872 | tf_op jit(solution)/shard_map/ppermute | solution.py:339
  49.0 24.3 %collective-permute-done.5.refs_1_.refs_6_ = bf16[512,1024]{1,0:T(8,128)(2,1)} collective-permute-done((bf16[512,1024]{1,0:T(8,128)(2,1)}, bf16[512,1024]{1,0:T(8,128)(2,1)}, u32[]{:S(2)}, u32[]{:S(2)}) %collective-permute-start.5) | collective-permute-done | bytes 1048608 | tf_op jit(solution)/shard_map/ppermute | solution.py:374
  73.9 2.6 collective-permute-start.7
  79.7 5.4 %collective-permute-start.34 = (bf16[512,512]{1,0:T(8,128)(2,1)}, bf16[512,512]{1,0:T(8,128)(2,1)}, u32[]{:S(2)}, u32[]{:S(2)}) collective-permute-start(bf16[512,512]{1,0:T(8,128)(2,1)} %collective-permute-done.33), channel_id=1, source_target_pairs={{0,0},{1,3},{2,2},{3,1},{32,33},{33,32},{34,35},{35,34},{64,66},{6... | collective-permute-start | bytes 1572872 | tf_op jit(solution)/shard_map/ppermute | solution.py:427
  86.9 3.2 %collective-permute-start.4 = (bf16[256,1024]{1,0:T(8,128)(2,1)}, bf16[256,1024]{1,0:T(8,128)(2,1)}, u32[]{:S(2)}, u32[]{:S(2)}) collective-permute-start(bf16[256,1024]{1,0:T(8,128)(2,1)} %slice.56), channel_id=1, source_target_pairs={{0,3},{1,0},{2,1},{3,2},{4,7},{5,4},{6,5},{7,6},{8,11},{9,8},{10,9... | collective-permute-start | bytes 1572872 | tf_op jit(solution)/shard_map/ppermute | solution.py:371
  90.1 10.7 %collective-permute-done.6.refs_2_.refs_7_ = bf16[512,1024]{1,0:T(8,128)(2,1)S(1)} collective-permute-done((bf16[512,1024]{1,0:T(8,128)(2,1)}, bf16[512,1024]{1,0:T(8,128)(2,1)S(1)}, u32[]{:S(2)}, u32[]{:S(2)}) %collective-permute-start.6) | collective-permute-done | bytes 1048608 | tf_op jit(solution)/shard_map/ppermute | solution.py:367
  101.7 9.8 %collective-permute-done.7.refs_3_.refs_8_ = bf16[512,1024]{1,0:T(8,128)(2,1)} collective-permute-done((bf16[512,1024]{1,0:T(8,128)(2,1)}, bf16[512,1024]{1,0:T(8,128)(2,1)}, u32[]{:S(2)}, u32[]{:S(2)}) %collective-permute-start.7) | collective-permute-done | bytes 1048608 | tf_op jit(solution)/shard_map/ppermute | solution.py:368
  111.5 1.9 slice.58
  113.4 3.8 %collective-permute-start.9 = (bf16[256,1024]{1,0:T(8,128)(2,1)}, bf16[256,1024]{1,0:T(8,128)(2,1)}, u32[]{:S(2)}, u32[]{:S(2)}) collective-permute-start(bf16[256,1024]{1,0:T(8,128)(2,1)} %slice.58), channel_id=1, source_target_pairs={{0,3},{1,0},{2,1},{3,2},{4,7},{5,4},{6,5},{7,6},{8,11},{9,8},{10,9... | collective-permute-start | bytes 1572872 | tf_op jit(solution)/shard_map/ppermute | solution.py:371
  123.1 7.1 %pk0.1 = (f32[512,256]{1,0:T(8,128)}, f32[512,128]{1,0:T(8,128)}) custom-call(s32[2,4]{1,0:T(2,128)} %get-tuple-element.34.refs_0_, bf16[512,1024]{1,0:T(8,128)(2,1)} %convolution_convert_fusion.refs_1_, bf16[512,1024]{1,0:T(8,128)(2,1)} %copy-done, bf16[512,1024]{1,0:T(8,128)(2,1)} %copy-done.1, bf16[256,1024]{1,0:T(8,128)(2,1)} %collective-permute-done.3.refs_4_, ...), custom_call_target="tpu_custom_call" | custom-call | flops 1073741824 | bytes 16777216 | tf_op jit(solution)/shard_map/pk0/pallas_call | solution.py:158
  130.9 7.5 %pk1.1 = (bf16[512,256]{1,0:T(8,128)(2,1)}, f32[512,128]{1,0:T(8,128)}) custom-call(s32[2,4]{1,0:T(2,128)} %get-tuple-element.35.refs_0_, bf16[512,1024]{1,0:T(8,128)(2,1)} %collective-permute-done.5.refs_1_.refs_6_, bf16[512,1024]{1,0:T(8,128)(2,1)} %copy-done.2, bf16[512,1024]{1,0:T(8,128)(2,1)} %collective-permute-done.7.refs_3_.refs_8_, ...), custom_call_target="tpu_custom_call" | custom-call | flops 1073741824 | bytes 16777216 | tf_op jit(solution)/shard_map/pk1/pallas_call | solution.py:158
  140.5 7.4 %collective-permute-done.11 = bf16[512,256]{1,0:T(8,128)(2,1)S(1)} collective-permute-done((bf16[512,256]{1,0:T(8,128)(2,1)}, bf16[512,256]{1,0:T(8,128)(2,1)S(1)}, u32[]{:S(2)}, u32[]{:S(2)}) %collective-permute-start.11) | collective-permute-done | bytes 262176 | tf_op jit(solution)/shard_map/ppermute | solution.py:416
  152.2 2.2 collective-permute-start.14
  154.8 9.0 %collective-permute-done.12.refs_5_ = bf16[2,512,256]{2,1,0:T(8,128)(2,1)S(1)} collective-permute-done((bf16[2,512,256]{2,1,0:T(8,128)(2,1)S(1)}, bf16[2,512,256]{2,1,0:T(8,128)(2,1)S(1)}, u32[]{:S(2)}, u32[]{:S(2)}) %collective-permute-start.12) | collective-permute-done | bytes 524320 | tf_op jit(solution)/shard_map/ppermute | solution.py:417
  163.8 3.8 %collective-permute-done.13.refs_6_ = bf16[2,512,256]{2,1,0:T(8,128)(2,1)S(1)} collective-permute-done((bf16[2,512,256]{2,1,0:T(8,128)(2,1)S(1)}, bf16[2,512,256]{2,1,0:T(8,128)(2,1)S(1)}, u32[]{:S(2)}, u32[]{:S(2)}) %collective-permute-start.13) | collective-permute-done | bytes 524320 | tf_op jit(solution)/shard_map/ppermute | solution.py:417
  169.4 2.3 pad_maximum_fusion.1
  173.5 8.9 %pq.1.refs_1_ = bf16[4,512,128]{2,1,0:T(8,128)(2,1)} custom-call(s32[2,8]{1,0:T(2,128)} %copy-done.5, bf16[512,1024]{1,0:T(8,128)(2,1)} %convolution_convert_fusion.refs_1_, bf16[512,1024]{1,0:T(8,128)(2,1)} %copy-done, bf16[512,1024]{1,0:T(8,128)(2,1)} %copy-done.1, bf16[256,1024]{1,0:T(8,128)(2,1)} %collective-permute-done.3.refs_4_, ...), custom_call_target="tpu_custom_call" | custom-call | flops 4294967296 | bytes 16777216 | tf_op jit(solution)/shard_map/pq/pallas_call | solution.py:158
  183.5 12.7 %shard_map.113.refs_1_ = bf16[256,512]{1,0:T(8,128)(2,1)} custom-call(s32[2,2]{1,0:T(2,128)} %get-tuple-element.33.refs_0_, bf16[4,512,128]{2,1,0:T(8,128)(2,1)} %pq.1.refs_1_, s32[4,512,128]{2,1,0:T(8,128)} %broadcast_in_dim.67.refs_2_, s32[8,1,1024]{2,1,0:T(1,128)} %reshape.1174.refs_3_, bf16[2,512,256]{2,1,0:T(8,128)(2,1)} %copy-done.4, ...), custom_call_target="tpu_custom_call" | custom-call | flops 4294967296 | bytes 6291456 | tf_op jit(solution)/shard_map/pallas_call | solution.py:254
  197.0 2.4 collective-permute-start.20
  200.3 2.7 collective-permute-start.22
  203.0 18.8 %shard_map.114.refs_9_ = bf16[256,512]{1,0:T(8,128)(2,1)} custom-call(s32[2,2]{1,0:T(2,128)} %get-tuple-element.32.refs_0_, bf16[4,512,128]{2,1,0:T(8,128)(2,1)} %pq.1.refs_1_, s32[4,512,128]{2,1,0:T(8,128)} %broadcast_in_dim.67.refs_2_, s32[8,1,1024]{2,1,0:T(1,128)} %reshape.1174.refs_3_, bf16[2,512,256]{2,1,0:T(8,128)(2,1)} %copy-done.4, ...), custom_call_target="tpu_custom_call" | custom-call | flops 4294967296 | bytes 6291456 | tf_op jit(solution)/shard_map/pallas_call | solution.py:254
  227.5 10.6 %collective-permute-done.26.refs_10_ = bf16[256,512]{1,0:T(8,128)(2,1)S(1)} collective-permute-done((bf16[256,512]{1,0:T(8,128)(2,1)}, bf16[256,512]{1,0:T(8,128)(2,1)S(1)}, u32[]{:S(2)}, u32[]{:S(2)}) %collective-permute-start.26) | collective-permute-done | bytes 262176 | tf_op jit(solution)/shard_map/ppermute | solution.py:438
  238.1 2.0 collective-permute-start.30
  240.1 2.0 collective-permute-start.31
  242.2 2.7 collective-permute-start.25
  247.2 2.9 %collective-permute-done.25.refs_8_ = bf16[256,512]{1,0:T(8,128)(2,1)S(1)} collective-permute-done((bf16[256,512]{1,0:T(8,128)(2,1)S(1)}, bf16[256,512]{1,0:T(8,128)(2,1)S(1)}, u32[]{:S(2)}, u32[]{:S(2)}) %collective-permute-start.25) | collective-permute-done | bytes 262176 | tf_op jit(solution)/shard_map/ppermute | solution.py:440
  250.1 2.9 %collective-permute-done.32.refs_16_ = bf16[256,512]{1,0:T(8,128)(2,1)} collective-permute-done((bf16[256,512]{1,0:T(8,128)(2,1)S(1)}, bf16[256,512]{1,0:T(8,128)(2,1)}, u32[]{:S(2)}, u32[]{:S(2)}) %collective-permute-start.32) | collective-permute-done | bytes 262176 | tf_op jit(solution)/shard_map/ppermute | solution.py:440
  253.1 10.3 %m.1 = (bf16[512,1024]{1,0:T(8,128)(2,1)}, bf16[512,512]{1,0:T(8,128)(2,1)}) custom-call(s32[2,8]{1,0:T(2,128)} %pad_add_fusion.refs_0_, bf16[256,512]{1,0:T(8,128)(2,1)} %shard_map.113.refs_1_, bf16[256,512]{1,0:T(8,128)(2,1)} %copy-done.14, bf16[256,512]{1,0:T(8,128)(2,1)} %copy-done.15, bf16[256,512]{1,0:T(8,128)(2,1)} %copy-done.16, ...), custom_call_target="tpu_custom_call" | custom-call | flops 4294967296 | bytes 16777216 | tf_op jit(solution)/shard_map/m/pallas_call | solution.py:303
  (162 shorter events, 47.0 us)
Async XLA Ops:
  7.2 110.1 %all-gather.4.cloned.1.call-start = ((), (), s32[]{:S(2)}) async-start(), calls=%async_computation | async-start | bytes 4866048 | tf_op jit(solution)/shard_map/all_gather | solution.py:357
  20.6 153.0 %all-gather.6.cloned.1.call-start = ((), (), s32[]{:S(2)}) async-start(), calls=%async_computation.1 | async-start | bytes 9437184 | tf_op jit(solution)/shard_map/all_gather | solution.py:357
  20.8 13.2 %collective-permute-start.10 = (bf16[512,512]{1,0:T(8,128)(2,1)S(1)}, bf16[512,512]{1,0:T(8,128)(2,1)S(1)}, u32[]{:S(2)}, u32[]{:S(2)}) collective-permute-start(bf16[512,512]{1,0:T(8,128)(2,1)S(1)} %multiply_convert_fusion), channel_id=1, source_target_pairs={{0,16},{16,0},{1,17},{17,1},{2,18},{18,2},{3,19},{19,3},{4,20},{20... | collective-permute-start | bytes 1572872 | tf_op jit(solution)/shard_map/ppermute | solution.py:361
  35.1 218.0 %all-gather.8.cloned.1.call-start = ((), (), s32[]{:S(2)}) async-start(), calls=%async_computation.2 | async-start | bytes 9437184 | tf_op jit(solution)/shard_map/all_gather | solution.py:357
  36.8 36.5 %collective-permute-start.5 = (bf16[512,1024]{1,0:T(8,128)(2,1)}, bf16[512,1024]{1,0:T(8,128)(2,1)}, u32[]{:S(2)}, u32[]{:S(2)}) collective-permute-start(bf16[512,1024]{1,0:T(8,128)(2,1)} %convolution_convert_fusion.refs_1_), channel_id=1, source_target_pairs={{0,4},{4,0},{1,5},{5,1},{2,6},{6,2},{3,7},{7,3},{8,12},{12,8},{9,1... | collective-permute-start | bytes 3145736 | tf_op jit(solution)/shard_map/ppermute | solution.py:374
  40.2 44.8 %collective-permute-start.1 = (bf16[512,1024]{1,0:T(8,128)(2,1)}, bf16[512,1024]{1,0:T(8,128)(2,1)S(1)}, u32[]{:S(2)}, u32[]{:S(2)}) collective-permute-start(bf16[512,1024]{1,0:T(8,128)(2,1)} %convolution_convert_fusion.refs_1_), channel_id=1, source_target_pairs={{0,1},{1,2},{2,3},{3,0},{4,5},{5,6},{6,7},{7,4},{8,9},{9,10},{10,1... | collective-permute-start | bytes 3145736 | tf_op jit(solution)/shard_map/ppermute | solution.py:367
  41.7 44.2 %collective-permute-start.2 = (bf16[512,1024]{1,0:T(8,128)(2,1)}, bf16[512,1024]{1,0:T(8,128)(2,1)S(1)}, u32[]{:S(2)}, u32[]{:S(2)}) collective-permute-start(bf16[512,1024]{1,0:T(8,128)(2,1)} %convolution_convert_fusion.refs_1_), channel_id=1, source_target_pairs={{0,3},{1,0},{2,1},{3,2},{4,7},{5,4},{6,5},{7,6},{8,11},{9,8},{10,9... | collective-permute-start | bytes 3145736 | tf_op jit(solution)/shard_map/ppermute | solution.py:368
  43.5 36.2 %collective-permute-start.33 = (bf16[512,512]{1,0:T(8,128)(2,1)}, bf16[512,512]{1,0:T(8,128)(2,1)}, u32[]{:S(2)}, u32[]{:S(2)}) collective-permute-start(bf16[512,512]{1,0:T(8,128)(2,1)} %param.19), channel_id=1, source_target_pairs={{0,0},{1,33},{2,66},{3,99},{4,16},{5,49},{6,82},{7,115},{16,32},{1... | collective-permute-start | bytes 1572872 | tf_op jit(solution)/shard_map/ppermute | solution.py:339
  73.3 27.5 %collective-permute-start.6 = (bf16[512,1024]{1,0:T(8,128)(2,1)}, bf16[512,1024]{1,0:T(8,128)(2,1)S(1)}, u32[]{:S(2)}, u32[]{:S(2)}) collective-permute-start(bf16[512,1024]{1,0:T(8,128)(2,1)} %collective-permute-done.5.refs_1_.refs_6_), channel_id=1, source_target_pairs={{0,1},{1,2},{2,3},{3,0},{4,5},{5,6},{6,7},{7,4},{8,9},{9,10},{10,1... | collective-permute-start | bytes 3145736 | tf_op jit(solution)/shard_map/ppermute | solution.py:367
  73.9 37.6 %collective-permute-start.7 = (bf16[512,1024]{1,0:T(8,128)(2,1)}, bf16[512,1024]{1,0:T(8,128)(2,1)}, u32[]{:S(2)}, u32[]{:S(2)}) collective-permute-start(bf16[512,1024]{1,0:T(8,128)(2,1)} %collective-permute-done.5.refs_1_.refs_6_), channel_id=1, source_target_pairs={{0,3},{1,0},{2,1},{3,2},{4,7},{5,4},{6,5},{7,6},{8,11},{9,8},{10,9... | collective-permute-start | bytes 3145736 | tf_op jit(solution)/shard_map/ppermute | solution.py:368
  79.7 60.0 %collective-permute-start.34 = (bf16[512,512]{1,0:T(8,128)(2,1)}, bf16[512,512]{1,0:T(8,128)(2,1)}, u32[]{:S(2)}, u32[]{:S(2)}) collective-permute-start(bf16[512,512]{1,0:T(8,128)(2,1)} %collective-permute-done.33), channel_id=1, source_target_pairs={{0,0},{1,3},{2,2},{3,1},{32,33},{33,32},{34,35},{35,34},{64,66},{6... | collective-permute-start | bytes 1572872 | tf_op jit(solution)/shard_map/ppermute | solution.py:427
  85.9 35.9 %collective-permute-start.3 = (bf16[256,1024]{1,0:T(8,128)(2,1)}, bf16[256,1024]{1,0:T(8,128)(2,1)}, u32[]{:S(2)}, u32[]{:S(2)}) collective-permute-start(bf16[256,1024]{1,0:T(8,128)(2,1)} %slice.55), channel_id=1, source_target_pairs={{0,1},{1,2},{2,3},{3,0},{4,5},{5,6},{6,7},{7,4},{8,9},{9,10},{10,1... | collective-permute-start | bytes 1572872 | tf_op jit(solution)/shard_map/ppermute | solution.py:370
  86.9 36.2 %collective-permute-start.4 = (bf16[256,1024]{1,0:T(8,128)(2,1)}, bf16[256,1024]{1,0:T(8,128)(2,1)}, u32[]{:S(2)}, u32[]{:S(2)}) collective-permute-start(bf16[256,1024]{1,0:T(8,128)(2,1)} %slice.56), channel_id=1, source_target_pairs={{0,3},{1,0},{2,1},{3,2},{4,7},{5,4},{6,5},{7,6},{8,11},{9,8},{10,9... | collective-permute-start | bytes 1572872 | tf_op jit(solution)/shard_map/ppermute | solution.py:371
  101.7 28.5 %collective-permute-start.8 = (bf16[256,1024]{1,0:T(8,128)(2,1)}, bf16[256,1024]{1,0:T(8,128)(2,1)}, u32[]{:S(2)}, u32[]{:S(2)}) collective-permute-start(bf16[256,1024]{1,0:T(8,128)(2,1)} %slice.57), channel_id=1, source_target_pairs={{0,1},{1,2},{2,3},{3,0},{4,5},{5,6},{6,7},{7,4},{8,9},{9,10},{10,1... | collective-permute-start | bytes 1572872 | tf_op jit(solution)/shard_map/ppermute | solution.py:370
  113.4 17.5 %collective-permute-start.9 = (bf16[256,1024]{1,0:T(8,128)(2,1)}, bf16[256,1024]{1,0:T(8,128)(2,1)}, u32[]{:S(2)}, u32[]{:S(2)}) collective-permute-start(bf16[256,1024]{1,0:T(8,128)(2,1)} %slice.58), channel_id=1, source_target_pairs={{0,3},{1,0},{2,1},{3,2},{4,7},{5,4},{6,5},{7,6},{8,11},{9,8},{10,9... | collective-permute-start | bytes 1572872 | tf_op jit(solution)/shard_map/ppermute | solution.py:371
  139.7 15.1 %collective-permute-start.35 = (bf16[512,512]{1,0:T(8,128)(2,1)}, bf16[512,512]{1,0:T(8,128)(2,1)S(1)}, u32[]{:S(2)}, u32[]{:S(2)}) collective-permute-start(bf16[512,512]{1,0:T(8,128)(2,1)} %collective-permute-done.34), channel_id=1, source_target_pairs={{0,16},{16,0},{1,17},{17,1},{2,18},{18,2},{3,19},{19,3},{4,20},{20... | collective-permute-start | bytes 1572872 | tf_op jit(solution)/shard_map/ppermute | solution.py:428
  148.9 15.0 %collective-permute-start.12 = (bf16[2,512,256]{2,1,0:T(8,128)(2,1)S(1)}, bf16[2,512,256]{2,1,0:T(8,128)(2,1)S(1)}, u32[]{:S(2)}, u32[]{:S(2)}) collective-permute-start(bf16[2,512,256]{2,1,0:T(8,128)(2,1)S(1)} %pad_maximum_fusion.3.refs_4_), channel_id=1, source_target_pairs={{0,32},{32,64},{64,96},{96,0},{1,33},{33,65},{65,97},{97,1},{2,34}... | collective-permute-start | bytes 1572872 | tf_op jit(solution)/shard_map/ppermute | solution.py:417
  150.7 16.9 %collective-permute-start.13 = (bf16[2,512,256]{2,1,0:T(8,128)(2,1)S(1)}, bf16[2,512,256]{2,1,0:T(8,128)(2,1)S(1)}, u32[]{:S(2)}, u32[]{:S(2)}) collective-permute-start(bf16[2,512,256]{2,1,0:T(8,128)(2,1)S(1)} %pad_maximum_fusion.3.refs_4_), channel_id=1, source_target_pairs={{0,96},{32,0},{64,32},{96,64},{1,97},{33,1},{65,33},{97,65},{2,98}... | collective-permute-start | bytes 1572872 | tf_op jit(solution)/shard_map/ppermute | solution.py:417
  152.2 17.3 %collective-permute-start.14 = (bf16[2,512,256]{2,1,0:T(8,128)(2,1)S(1)}, bf16[2,512,256]{2,1,0:T(8,128)(2,1)S(1)}, u32[]{:S(2)}, u32[]{:S(2)}) collective-permute-start(bf16[2,512,256]{2,1,0:T(8,128)(2,1)S(1)} %pad_maximum_fusion.3.refs_4_), channel_id=1, source_target_pairs={{0,64},{32,96},{64,0},{96,32},{1,65},{33,97},{65,1},{97,33},{2,66}... | collective-permute-start | bytes 1572872 | tf_op jit(solution)/shard_map/ppermute | solution.py:417
  171.7 10.8 %collective-permute-start.15 = (bf16[2,512,256]{2,1,0:T(8,128)(2,1)S(1)}, bf16[2,512,256]{2,1,0:T(8,128)(2,1)S(1)}, u32[]{:S(2)}, u32[]{:S(2)}) collective-permute-start(bf16[2,512,256]{2,1,0:T(8,128)(2,1)S(1)} %pad_maximum_fusion.3.refs_4_), channel_id=1, source_target_pairs={{0,8},{8,0},{1,9},{9,1},{2,10},{10,2},{3,11},{11,3},{4,12},{12,4},... | collective-permute-start | bytes 1572872 | tf_op jit(solution)/shard_map/ppermute | solution.py:418
  171.8 10.7 %collective-permute-start.16 = (bf16[2,512,256]{2,1,0:T(8,128)(2,1)S(1)}, bf16[2,512,256]{2,1,0:T(8,128)(2,1)S(1)}, u32[]{:S(2)}, u32[]{:S(2)}) collective-permute-start(bf16[2,512,256]{2,1,0:T(8,128)(2,1)S(1)} %collective-permute-done.12.refs_5_), channel_id=1, source_target_pairs={{0,8},{8,0},{1,9},{9,1},{2,10},{10,2},{3,11},{11,3},{4,12},{12,4},... | collective-permute-start | bytes 1572872 | tf_op jit(solution)/shard_map/ppermute | solution.py:418
  172.3 10.2 %collective-permute-start.17 = (bf16[2,512,256]{2,1,0:T(8,128)(2,1)S(1)}, bf16[2,512,256]{2,1,0:T(8,128)(2,1)}, u32[]{:S(2)}, u32[]{:S(2)}) collective-permute-start(bf16[2,512,256]{2,1,0:T(8,128)(2,1)S(1)} %collective-permute-done.13.refs_6_), channel_id=1, source_target_pairs={{0,8},{8,0},{1,9},{9,1},{2,10},{10,2},{3,11},{11,3},{4,12},{12,4},... | collective-permute-start | bytes 1572872 | tf_op jit(solution)/shard_map/ppermute | solution.py:418
  196.2 27.1 %collective-permute-start.19 = (bf16[256,512]{1,0:T(8,128)(2,1)}, bf16[256,512]{1,0:T(8,128)(2,1)S(1)}, u32[]{:S(2)}, u32[]{:S(2)}) collective-permute-start(bf16[256,512]{1,0:T(8,128)(2,1)} %shard_map.113.refs_1_), channel_id=1, source_target_pairs={{0,1},{1,2},{2,3},{3,0},{4,5},{5,6},{6,7},{7,4},{8,9},{9,10},{10,1... | collective-permute-start | bytes 786440 | tf_op jit(solution)/shard_map/ppermute | solution.py:438
  197.0 27.2 %collective-permute-start.20 = (bf16[256,512]{1,0:T(8,128)(2,1)}, bf16[256,512]{1,0:T(8,128)(2,1)S(1)}, u32[]{:S(2)}, u32[]{:S(2)}) collective-permute-start(bf16[256,512]{1,0:T(8,128)(2,1)} %shard_map.113.refs_1_), channel_id=1, source_target_pairs={{0,3},{1,0},{2,1},{3,2},{4,7},{5,4},{6,5},{7,6},{8,11},{9,8},{10,9... | collective-permute-start | bytes 786440 | tf_op jit(solution)/shard_map/ppermute | solution.py:438
  199.5 26.6 %collective-permute-start.21 = (bf16[256,512]{1,0:T(8,128)(2,1)}, bf16[256,512]{1,0:T(8,128)(2,1)S(1)}, u32[]{:S(2)}, u32[]{:S(2)}) collective-permute-start(bf16[256,512]{1,0:T(8,128)(2,1)} %shard_map.113.refs_1_), channel_id=1, source_target_pairs={{0,2},{1,3},{2,0},{3,1},{4,6},{5,7},{6,4},{7,5},{8,10},{9,11},{10,... | collective-permute-start | bytes 786440 | tf_op jit(solution)/shard_map/ppermute | solution.py:438
  200.3 27.2 %collective-permute-start.22 = (bf16[256,512]{1,0:T(8,128)(2,1)}, bf16[256,512]{1,0:T(8,128)(2,1)S(1)}, u32[]{:S(2)}, u32[]{:S(2)}) collective-permute-start(bf16[256,512]{1,0:T(8,128)(2,1)} %shard_map.113.refs_1_), channel_id=1, source_target_pairs={{0,4},{4,0},{1,5},{5,1},{2,6},{6,2},{3,7},{7,3},{8,12},{12,8},{9,1... | collective-permute-start | bytes 786440 | tf_op jit(solution)/shard_map/ppermute | solution.py:437
  221.8 16.3 %collective-permute-start.26 = (bf16[256,512]{1,0:T(8,128)(2,1)}, bf16[256,512]{1,0:T(8,128)(2,1)S(1)}, u32[]{:S(2)}, u32[]{:S(2)}) collective-permute-start(bf16[256,512]{1,0:T(8,128)(2,1)} %shard_map.114.refs_9_), channel_id=1, source_target_pairs={{0,1},{1,2},{2,3},{3,0},{4,5},{5,6},{6,7},{7,4},{8,9},{9,10},{10,1... | collective-permute-start | bytes 786440 | tf_op jit(solution)/shard_map/ppermute | solution.py:438
  223.3 14.8 %collective-permute-start.29 = (bf16[256,512]{1,0:T(8,128)(2,1)}, bf16[256,512]{1,0:T(8,128)(2,1)S(1)}, u32[]{:S(2)}, u32[]{:S(2)}) collective-permute-start(bf16[256,512]{1,0:T(8,128)(2,1)} %shard_map.114.refs_9_), channel_id=1, source_target_pairs={{0,4},{4,0},{1,5},{5,1},{2,6},{6,2},{3,7},{7,3},{8,12},{12,8},{9,1... | collective-permute-start | bytes 786440 | tf_op jit(solution)/shard_map/ppermute | solution.py:437
  224.3 15.9 %collective-permute-start.27 = (bf16[256,512]{1,0:T(8,128)(2,1)}, bf16[256,512]{1,0:T(8,128)(2,1)S(1)}, u32[]{:S(2)}, u32[]{:S(2)}) collective-permute-start(bf16[256,512]{1,0:T(8,128)(2,1)} %shard_map.114.refs_9_), channel_id=1, source_target_pairs={{0,3},{1,0},{2,1},{3,2},{4,7},{5,4},{6,5},{7,6},{8,11},{9,8},{10,9... | collective-permute-start | bytes 786440 | tf_op jit(solution)/shard_map/ppermute | solution.py:438
  226.1 16.1 %collective-permute-start.28 = (bf16[256,512]{1,0:T(8,128)(2,1)}, bf16[256,512]{1,0:T(8,128)(2,1)S(1)}, u32[]{:S(2)}, u32[]{:S(2)}) collective-permute-start(bf16[256,512]{1,0:T(8,128)(2,1)} %shard_map.114.refs_9_), channel_id=1, source_target_pairs={{0,2},{1,3},{2,0},{3,1},{4,6},{5,7},{6,4},{7,5},{8,10},{9,11},{10,... | collective-permute-start | bytes 786440 | tf_op jit(solution)/shard_map/ppermute | solution.py:438
  227.5 17.4 %collective-permute-start.23 = (bf16[256,512]{1,0:T(8,128)(2,1)S(1)}, bf16[256,512]{1,0:T(8,128)(2,1)S(1)}, u32[]{:S(2)}, u32[]{:S(2)}) collective-permute-start(bf16[256,512]{1,0:T(8,128)(2,1)S(1)} %collective-permute-done.22.refs_5_), channel_id=1, source_target_pairs={{0,1},{1,2},{2,3},{3,0},{4,5},{5,6},{6,7},{7,4},{8,9},{9,10},{10,1... | collective-permute-start | bytes 786440 | tf_op jit(solution)/shard_map/ppermute | solution.py:439
  238.1 12.0 %collective-permute-start.30 = (bf16[256,512]{1,0:T(8,128)(2,1)S(1)}, bf16[256,512]{1,0:T(8,128)(2,1)S(1)}, u32[]{:S(2)}, u32[]{:S(2)}) collective-permute-start(bf16[256,512]{1,0:T(8,128)(2,1)S(1)} %collective-permute-done.29.refs_13_), channel_id=1, source_target_pairs={{0,1},{1,2},{2,3},{3,0},{4,5},{5,6},{6,7},{7,4},{8,9},{9,10},{10,1... | collective-permute-start | bytes 786440 | tf_op jit(solution)/shard_map/ppermute | solution.py:439
  (34 other events, 584.0 us)
Sparse Core Ops, SparseCore 0:
  20.7 40.6 all-gather.3
  63.0 52.7 all-gather.5
  171.9 49.3 all-gather.7
